TPU v7x, 32 devices: a whole 2x2x4 slice. The times are simulated.
32 devices in a mesh: dp: 4 (over z), space: 8 (over y, x, core).
Axes of the slice: x: 2, y: 2, z: 4, core: 2. Of those that a mesh axis runs over, the one named last changes fastest.
Arguments:
- lateral3: bfloat16 [16, 32, 128, 256], P('dp', 'space'), may hold values from -1200 to 1200
- lateral4: bfloat16 [16, 16, 64, 256], P('dp', 'space'), may hold values from -1200 to 1200
- lateral5: bfloat16 [16, 8, 32, 256], P('dp', 'space'), may hold values from -1200 to 1200
- conv_weight3: bfloat16 [3, 3, 256, 256], P(None, None, None, ('dp', 'space')), may hold values from -0.125 to 0.125
- conv_weight4: bfloat16 [3, 3, 256, 256], P(None, None, None, ('dp', 'space')), may hold values from -0.125 to 0.125
- conv_weight5: bfloat16 [3, 3, 256, 256], P(None, None, None, ('dp', 'space')), may hold values from -0.125 to 0.125
- norm_gain3: float32 [256], replicated, may hold values from 0.1 to 1.9
- norm_shift3: float32 [256], replicated, may hold values from -3 to 3
- norm_gain4: float32 [256], replicated, may hold values from 0.1 to 1.9
- norm_shift4: float32 [256], replicated, may hold values from -3 to 3
- norm_gain5: float32 [256], replicated, may hold values from 0.1 to 1.9
- norm_shift5: float32 [256], replicated, may hold values from -3 to 3
Outputs:
- pyramid3: float32 [16, 32, 128, 256], P('dp', 'space')
- pyramid4: float32 [16, 16, 64, 256], P('dp', 'space')
- pyramid5: float32 [16, 8, 32, 256], P('dp', 'space')
All inputs are finite; a program needn't handle non-finite values.
Results may differ from a plain program's by a relative error of at most 0.007.
Values may be sent and summed in bfloat16 or wider, within the bound.
No kernel may reach another device: no remote copies, remote signals or barrier semaphores. Data moves between devices by JAX's collectives and lax.ppermute only.
A program may use at most 64 MiB of HBM per device.

v0:
```python
import jax
import jax.numpy as jnp
from jax import lax
from jax.sharding import PartitionSpec as P

C = 256
G = 32


epsilon = 1e-05


def extended(array, sides, width):
    for axis, dim in sides:
        devices, length = (lax.axis_size(axis), array.shape[dim])
        up = [(i, (i + 1) % devices) for i in range(devices - 1)]
        down = [(j, i) for i, j in up]
        last = lax.slice_in_dim(array, length - width, length, axis=dim)
        first = lax.slice_in_dim(array, 0, width, axis=dim)
        before = lax.ppermute(last, axis, up)
        after = lax.ppermute(first, axis, down)
        array = jnp.concatenate([before, array, after], axis=dim)
    return array


def enlarge(values):
    return jnp.repeat(jnp.repeat(values, 2, axis=1), 2, axis=2)


def convolve(padded, kernel, margin):
    return lax.conv_general_dilated(
        padded,
        kernel,
        (1, 1),
        (margin, (1, 1)),
        dimension_numbers=("NHWC", "HWIO", "NHWC"),
        preferred_element_type=jnp.float32,
    )


def rowwise(padded, kernel_piece):
    return convolve(padded, kernel_piece, (0, 0))


def grouped(values, groups):
    return values.reshape(
        values.shape[0], values.shape[1], values.shape[2], groups, values.shape[3] // groups
    )


def group_totals(values, groups):
    return jnp.sum(grouped(values, groups), axis=(1, 2, 4))


def square_terms(values, center, groups):
    deviation = grouped(values, groups) - center[:, None, None, :, None]
    return jnp.sum(deviation * deviation, axis=(1, 2, 4))


def normalize(values, center, spread, gain_vector, shift_vector, groups):
    deviation = grouped(values, groups) - center[:, None, None, :, None]
    scaled = deviation * lax.rsqrt(spread + epsilon)[:, None, None, :, None]
    return scaled.reshape(values.shape) * gain_vector + shift_vector


def norm_levels(levels):
    strip_count = lax.axis_size("space")
    volumes = [
        record[0].shape[1] * strip_count * record[0].shape[2] * (record[0].shape[3] // G)
        for record in levels
    ]
    statistics = []
    for record, volume in zip(levels, volumes):
        center = lax.psum(group_totals(record[0], G), "space") / volume
        spread = lax.psum(square_terms(record[0], center, G), "space") / volume
        statistics.append((center, spread))
    return [
        normalize(record[0], stats_pair[0], stats_pair[1], record[1], record[2], G)
        for record, stats_pair in zip(levels, statistics)
    ]


def local(
    lateral3,
    lateral4,
    lateral5,
    conv_weight3,
    conv_weight4,
    conv_weight5,
    norm_gain3,
    norm_shift3,
    norm_gain4,
    norm_shift4,
    norm_gain5,
    norm_shift5,
):
    merged4 = (lateral4.astype(jnp.float32) + enlarge(lateral5).astype(jnp.float32)).astype(
        jnp.bfloat16
    )
    padded4 = extended(merged4, (("space", 1),), 1)
    merged3 = (lateral3.astype(jnp.float32) + enlarge(merged4).astype(jnp.float32)).astype(
        jnp.bfloat16
    )
    padded3 = extended(merged3, (("space", 1),), 1)
    filtered3 = rowwise(padded3, lax.all_gather(conv_weight3, ("dp", "space"), axis=3, tiled=True))
    filtered4 = rowwise(padded4, lax.all_gather(conv_weight4, ("dp", "space"), axis=3, tiled=True))
    levels = [(filtered3, norm_gain3, norm_shift3), (filtered4, norm_gain4, norm_shift4)]
    gathered5 = lax.all_gather(lateral5, "space", axis=1, tiled=True)
    kernel_full = lax.all_gather(conv_weight5, ("dp", "space"), axis=3, tiled=True)
    channel_share = kernel_full.shape[3] // lax.axis_size("space")
    first_channel = lax.axis_index("space") * channel_share
    kernel_mine = lax.dynamic_slice_in_dim(kernel_full, first_channel, channel_share, 3)
    filtered5 = convolve(gathered5, kernel_mine, (1, 1))
    local_groups = G // lax.axis_size("space")
    volume5 = filtered5.shape[1] * filtered5.shape[2] * (C // G)
    center5 = group_totals(filtered5, local_groups) / volume5
    spread5 = square_terms(filtered5, center5, local_groups) / volume5
    gain_mine = lax.dynamic_slice_in_dim(norm_gain5, first_channel, channel_share, 0)
    shift_mine = lax.dynamic_slice_in_dim(norm_shift5, first_channel, channel_share, 0)
    normed5 = normalize(filtered5, center5, spread5, gain_mine, shift_mine, local_groups)
    pyramid5 = lax.all_to_all(normed5, "space", split_axis=1, concat_axis=3, tiled=True)
    results = norm_levels(levels)
    pyramid3 = results[0]
    pyramid4 = results[1]
    return (pyramid3, pyramid4, pyramid5)


def solution(mesh):
    placed = (
        P("dp", "space", None, None),
        P("dp", "space", None, None),
        P("dp", "space", None, None),
        P(None, None, None, ("dp", "space")),
        P(None, None, None, ("dp", "space")),
        P(None, None, None, ("dp", "space")),
        P(),
        P(),
        P(),
        P(),
        P(),
        P(),
    )
    return jax.shard_map(
        local,
        mesh=mesh,
        in_specs=placed,
        out_specs=(
            P("dp", "space", None, None),
            P("dp", "space", None, None),
            P("dp", "space", None, None),
        ),
        check_vma=False,
    )
```

profile of v0, /device:TPU:0, one launch (start us, length us, event | category | flops | bytes accessed | tf_op | source)
XLA Modules:
  0.0 201.7 jit_solution(8424565491353374304)
XLA Ops:
  7.2 0.7 all-gather.4.cloned.1.call-update
  7.9 0.7 all-gather.6.cloned.1.call-update
  8.7 0.9 bitcast_convert_fusion
  9.6 0.2 convert_element_type.38
  9.8 1.0 add_convert_fusion.1
  10.9 0.7 broadcast_in_dim.11
  11.7 2.4 %convert_element_type.42 = f32[4,4,128,256]{3,2,1,0:T(8,128)} reshape(f32[4,4,64,2,256]{4,3,2,1,0:T(2,128)S(1)} %broadcast_in_dim.11) | data formatting | bytes 4194304 | tf_op jit(solution)/shard_map/convert_element_type | solution.py:101
  14.1 2.2 %add_convert_fusion = bf16[4,4,128,256]{3,2,1,0:T(8,128)(2,1)S(1)} fusion(f32[4,4,128,256]{3,2,1,0:T(8,128)} %convert_element_type.42, bf16[4,4,128,256]{3,2,1,0:T(8,128)(2,1)} %param.12), kind=kLoop, calls=%fused_computation.9 | loop fusion | flops 1572864 | bytes 4194304 | tf_op jit(solution)/shard_map/convert_element_type | solution.py:101
  16.3 2.4 %collective-permute-start = (bf16[4,1,128,256]{3,2,1,0:T(8,128)(2,1)S(1)}, bf16[4,1,128,256]{3,2,1,0:T(8,128)(2,1)S(1)}, u32[]{:S(2)}, u32[]{:S(2)}) collective-permute-start(bf16[4,1,128,256]{3,2,1,0:T(8,128)(2,1)S(1)} %get-tuple-element.16), channel_id=1, source_target_pairs={{0,1},{1,2},{2,3},{3,4},{4,5},{5,6},{6,7},{8,9},{9,10},{10,11},{11... | collective-permute-start | bytes 786440 | tf_op jit(solution)/shard_map/ppermute | solution.py:20
  18.8 1.3 collective-permute-start.1
  20.1 5.1 %collective-permute-start.2 = (bf16[4,1,64,256]{3,2,1,0:T(8,128)(2,1)S(1)}, bf16[4,1,64,256]{3,2,1,0:T(8,128)(2,1)S(1)}, u32[]{:S(2)}, u32[]{:S(2)}) collective-permute-start(bf16[4,1,64,256]{3,2,1,0:T(8,128)(2,1)S(1)} %get-tuple-element.18), channel_id=1, source_target_pairs={{0,1},{1,2},{2,3},{3,4},{4,5},{5,6},{6,7},{8,9},{9,10},{10,11},{11... | collective-permute-start | bytes 393224 | tf_op jit(solution)/shard_map/ppermute | solution.py:20
  25.2 1.3 collective-permute-start.3
  26.6 14.5 %all_gather.14 = bf16[4,8,32,256]{3,2,0,1:T(8,128)(2,1)S(1)} all-gather(bf16[4,1,32,256]{3,2,0,1:T(8,128)(2,1)S(1)} %bitcast.90), channel_id=1, replica_groups=mesh['dp'=4,'space'=8] {'space'}, dimensions={1}, use_global_device_ids=true | all-gather | bytes 589824 | tf_op jit(solution)/shard_map/all_gather | solution.py:108
  41.1 0.3 copy.145
  41.5 1.1 fusion.12
  42.7 0.4 copy.98
  43.2 0.2 pad.2.clone
  43.4 0.3 fusion.16
  43.8 0.2 maximum_bitcast_fusion
  44.0 1.2 copy.97
  45.2 0.6 pad.clone
  45.9 1.8 fusion.3
  47.7 19.4 %all-gather.4.cloned.1.call-done = bf16[3,3,256,256]{2,3,1,0:T(8,128)(2,1)} async-done(((bf16[3,3,256,8]{2,3,1,0:T(8,128)(2,1)}), bf16[3,3,256,256]{2,3,1,0:T(8,128)(2,1)}) %all-gather.4.cloned.1.call-update) | async-done | bytes 1179664 | tf_op jit(solution)/shard_map/all_gather | solution.py:105
  67.1 4.7 %fusion.8 = f32[4,32,17,256]{3,1,2,0:T(8,128)S(1)} fusion(bf16[3,3,256,256]{2,3,1,0:T(8,128)(2,1)} %all-gather.4.cloned.1.call-done, bf16[6,4,8,19,256]{4,1,3,2,0:T(4,128)(2,1)} %fusion.3, pred[32,17]{0,1:T(8,128)(4,1)S(1)} %copy-done.10), kind=kOutput, calls=%fused_computation.17 | convolution fusion | flops 2567471104 | bytes 5276192 | tf_op jit(solution)/shard_map/conv_general_dilated | solution.py:31
  71.7 1.4 copy.72
  73.2 0.2 slice_reduce_fusion.1
  73.4 0.7 reduce_sum.70
  74.2 47.8 %all-gather.6.cloned.1.call-done = bf16[3,3,256,256]{2,3,1,0:T(8,128)(2,1)} async-done(((bf16[3,3,256,8]{2,3,1,0:T(8,128)(2,1)}), bf16[3,3,256,256]{2,3,1,0:T(8,128)(2,1)}) %all-gather.6.cloned.1.call-update) | async-done | bytes 1179664 | tf_op jit(solution)/shard_map/all_gather | solution.py:106
  121.9 2.2 %convolution_select_fusion.1 = f32[2,32,9,256]{3,1,2,0:T(8,128)S(1)} fusion(bf16[3,3,256,256]{2,3,1,0:T(8,128)(2,1)} %all-gather.6.cloned.1.call-done, bf16[4,4,8,11,256]{4,1,3,2,0:T(4,128)(2,1)S(1)} %fusion.16, pred[32,9]{0,1:T(8,128)(4,1)S(1)} %copy-done.11), kind=kOutput, calls=%fused_computation.21 | convolution fusion | flops 679624704 | bytes 2490656 | tf_op jit(solution)/shard_map/conv_general_dilated | solution.py:31
  124.1 0.5 copy.79
  124.8 0.9 reduce_sum.74
  125.8 14.4 %all-reduce.1 = (f32[4,32]{1,0:T(4,128)S(1)}, f32[4,32]{1,0:T(4,128)S(1)}) all-reduce(f32[4,32]{1,0:T(4,128)S(1)} %reduce_sum.74, f32[4,32]{1,0:T(4,128)S(1)} %reduce_sum.83), channel_id=1, replica_groups=mesh['dp'=4,'space'=8] {'space'}, use_global_device_ids=true, to_apply=%region_2.0 | all-reduce | flops 256 | bytes 2048 | tf_op jit(solution)/shard_map/psum | solution.py:74
  140.4 0.3 broadcast.77
  140.7 0.6 fusion.15
  141.3 0.8 copy-done
  142.1 1.4 copy.74
  143.5 0.2 slice_reduce_fusion
  144.4 0.5 copy.81
  145.2 11.8 %all-reduce = (f32[4,32]{1,0:T(4,128)S(1)}, f32[4,32]{1,0:T(4,128)S(1)}) all-reduce(f32[4,32]{1,0:T(4,128)S(1)} %reduce_sum.77, f32[4,32]{1,0:T(4,128)S(1)} %reduce_sum.89), channel_id=1, replica_groups=mesh['dp'=4,'space'=8] {'space'}, use_global_device_ids=true, to_apply=%region_5.0 | all-reduce | flops 256 | bytes 2048 | tf_op jit(solution)/shard_map/psum | solution.py:75
  157.2 0.2 broadcast.84
  157.5 1.3 copy.83
  159.0 0.3 broadcast.78
  159.3 1.3 copy-done.1
  160.6 0.9 fusion.2
  161.5 1.4 copy.76
  163.0 0.4 slice_bitcast_fusion
  163.3 13.5 %all-gather.8.cloned.1.call-done = bf16[3,3,256,256]{2,3,1,0:T(8,128)(2,1)} async-done(((bf16[3,3,256,8]{2,3,1,0:T(8,128)(2,1)}), bf16[3,3,256,256]{2,3,1,0:T(8,128)(2,1)}) %all-gather.8.cloned.1.call-update) | async-done | bytes 1179664 | tf_op jit(solution)/shard_map/all_gather | solution.py:109
  176.9 2.9 %convolution_select_fusion = f32[8,32,5,32]{3,1,2,0:T(8,128)S(1)} fusion(bf16[8,4,8,7,256]{4,0,3,2,1:T(8,128)(2,1)} %fusion.12, pred[32,5]{0,1:T(8,128)(4,1)S(1)} %copy-done.12, bf16[3,3,256,256]{2,3,1,0:T(8,128)(2,1)} %all-gather.8.cloned.1.call-done, s32[]{:T(128)S(6)} %select_n.2), kind=kOutput, calls=%fused_computation.20 | convolution fusion | flops 173056000 | bytes 1228964 | tf_op jit(solution)/shard_map/conv_general_dilated | solution.py:31
  179.8 0.4 copy.87
  180.6 0.2 fusion.23
  180.8 0.4 copy.89
  181.6 0.3 fusion.20
  181.9 0.4 copy.91
  182.5 0.9 reshape.117
  183.4 3.4 %all-to-all-start = ((f32[8,1,4096]{2,1,0:T(1,128)}), f32[8,1,4096]{2,1,0:T(1,128)S(1)}, u32[]{:S(2)}, u32[]{:S(2)}) async-start(f32[8,1,4096]{2,1,0:T(1,128)} %reshape.117), calls=%async_computation | async-start | bytes 262144 | tf_op jit(solution)/shard_map/all_to_all | solution.py:121
  186.8 0.2 slice_bitcast_fusion.2
  187.0 0.8 copy.95
  187.8 1.7 copy.94
  189.5 2.8 %all-to-all-done = f32[8,1,4096]{2,1,0:T(1,128)S(1)} async-done(((f32[8,1,4096]{2,1,0:T(1,128)}), f32[8,1,4096]{2,1,0:T(1,128)S(1)}, u32[]{:S(2)}, u32[]{:S(2)}) %all-to-all-start) | async-done | bytes 131104 | tf_op jit(solution)/shard_map/all_to_all | solution.py:121
  192.3 0.5 broadcast.126
  192.8 1.0 reduce.18
  193.8 0.2 reshape.118
  194.0 0.3 copy.93
  194.3 0.8 all_to_all.16
  (82 shorter events, 3.8 us)
Async XLA Ops:
  7.2 59.9 %all-gather.4.cloned.1.call-start = ((), (), s32[]{:S(2)}) async-start(), calls=%async_computation.1 | async-start | bytes 1216512 | tf_op jit(solution)/shard_map/all_gather | solution.py:105
  7.9 114.0 %all-gather.6.cloned.1.call-start = ((), (), s32[]{:S(2)}) async-start(), calls=%async_computation.2 | async-start | bytes 1216512 | tf_op jit(solution)/shard_map/all_gather | solution.py:106
  8.6 168.2 %all-gather.8.cloned.1.call-start = ((), (), s32[]{:S(2)}) async-start(), calls=%async_computation.3 | async-start | bytes 1216512 | tf_op jit(solution)/shard_map/all_gather | solution.py:109
  14.1 12.4 %copy-start.3 = (bf16[4,1,32,256]{3,2,1,0:T(8,128)(2,1)S(1)}, bf16[4,1,32,256]{3,2,1,0:T(8,128)(2,1)}, u32[]{:S(2)}) copy-start(bf16[4,1,32,256]{3,2,1,0:T(8,128)(2,1)} %param.14) | copy-start | bytes 196612
  16.3 27.4 %collective-permute-start = (bf16[4,1,128,256]{3,2,1,0:T(8,128)(2,1)S(1)}, bf16[4,1,128,256]{3,2,1,0:T(8,128)(2,1)S(1)}, u32[]{:S(2)}, u32[]{:S(2)}) collective-permute-start(bf16[4,1,128,256]{3,2,1,0:T(8,128)(2,1)S(1)} %get-tuple-element.16), channel_id=1, source_target_pairs={{0,1},{1,2},{2,3},{3,4},{4,5},{5,6},{6,7},{8,9},{9,10},{10,11},{11... | collective-permute-start | bytes 786440 | tf_op jit(solution)/shard_map/ppermute | solution.py:20
  18.8 25.0 %collective-permute-start.1 = (bf16[4,1,128,256]{3,2,1,0:T(8,128)(2,1)S(1)}, bf16[4,1,128,256]{3,2,1,0:T(8,128)(2,1)S(1)}, u32[]{:S(2)}, u32[]{:S(2)}) collective-permute-start(bf16[4,1,128,256]{3,2,1,0:T(8,128)(2,1)S(1)} %get-tuple-element.17), channel_id=1, source_target_pairs={{1,0},{2,1},{3,2},{4,3},{5,4},{6,5},{7,6},{9,8},{10,9},{11,10},{12... | collective-permute-start | bytes 786440 | tf_op jit(solution)/shard_map/ppermute | solution.py:21
  20.1 22.6 %collective-permute-start.2 = (bf16[4,1,64,256]{3,2,1,0:T(8,128)(2,1)S(1)}, bf16[4,1,64,256]{3,2,1,0:T(8,128)(2,1)S(1)}, u32[]{:S(2)}, u32[]{:S(2)}) collective-permute-start(bf16[4,1,64,256]{3,2,1,0:T(8,128)(2,1)S(1)} %get-tuple-element.18), channel_id=1, source_target_pairs={{0,1},{1,2},{2,3},{3,4},{4,5},{5,6},{6,7},{8,9},{9,10},{10,11},{11... | collective-permute-start | bytes 393224 | tf_op jit(solution)/shard_map/ppermute | solution.py:20
  25.2 17.5 %collective-permute-start.3 = (bf16[4,1,64,256]{3,2,1,0:T(8,128)(2,1)S(1)}, bf16[4,1,64,256]{3,2,1,0:T(8,128)(2,1)S(1)}, u32[]{:S(2)}, u32[]{:S(2)}) collective-permute-start(bf16[4,1,64,256]{3,2,1,0:T(8,128)(2,1)S(1)} %get-tuple-element.19), channel_id=1, source_target_pairs={{1,0},{2,1},{3,2},{4,3},{5,4},{6,5},{7,6},{9,8},{10,9},{11,10},{12... | collective-permute-start | bytes 393224 | tf_op jit(solution)/shard_map/ppermute | solution.py:21
  41.1 1.4 copy-start.8
  41.1 1.5 copy-start.9
  45.8 21.2 %copy-start.10 = (pred[32,17]{0,1:T(8,128)(4,1)S(1)}, pred[32,17]{0,1:T(8,128)(4,1)}, u32[]{:S(2)}) copy-start(pred[32,17]{0,1:T(8,128)(4,1)} %constant.45) | copy-start | bytes 1636
  73.2 48.7 %copy-start.11 = (pred[32,9]{0,1:T(8,128)(4,1)S(1)}, pred[32,9]{0,1:T(8,128)(4,1)}, u32[]{:S(2)}) copy-start(pred[32,9]{0,1:T(8,128)(4,1)} %constant.46) | copy-start | bytes 868
  140.7 1.3 copy-start
  144.3 13.1 %copy-start.4 = (f32[256]{0:T(256)S(1)}, f32[256]{0:T(256)}, u32[]{:S(2)}) copy-start(f32[256]{0:T(256)} %param.21) | copy-start | bytes 3076
  144.3 13.1 %copy-start.5 = (f32[256]{0:T(256)S(1)}, f32[256]{0:T(256)}, u32[]{:S(2)}) copy-start(f32[256]{0:T(256)} %param.20) | copy-start | bytes 3076
  157.5 1.8 copy-start.6
  157.5 1.8 copy-start.7
  159.0 1.6 copy-start.1
  163.0 13.9 %copy-start.12 = (pred[32,5]{0,1:T(8,128)(4,1)S(1)}, pred[32,5]{0,1:T(8,128)(4,1)}, u32[]{:S(2)}) copy-start(pred[32,5]{0,1:T(8,128)(4,1)} %constant.47) | copy-start | bytes 484
  181.9 4.9 %copy-start.2 = (f32[2,32,9,256]{3,0,2,1:T(2,128)S(1)}, f32[2,32,9,256]{3,0,2,1:T(2,128)}, u32[]{:S(2)}) copy-start(f32[2,32,9,256]{3,0,2,1:T(2,128)} %copy.83) | copy-start | bytes 1769476
  183.4 8.9 %all-to-all-start = ((f32[8,1,4096]{2,1,0:T(1,128)}), f32[8,1,4096]{2,1,0:T(1,128)S(1)}, u32[]{:S(2)}, u32[]{:S(2)}) async-start(f32[8,1,4096]{2,1,0:T(1,128)} %reshape.117), calls=%async_computation | async-start | bytes 262144 | tf_op jit(solution)/shard_map/all_to_all | solution.py:121
Sparse Core Ops, SparseCore 0:
  10.8 56.1 all-gather.3
  69.9 51.9 all-gather.5
  124.8 52.0 all-gather.7
where the time goes:
time: 202 us
  waiting for transfers between devices  84.8 us (42%)
  blocking collectives  40.7 us (20%)
  local copies, waits for them, and re-layouts  25.7 us (13%)
  between operations  14.3 us (7%)
  starting transfers between devices  13.7 us (7%)
  other arithmetic  12.7 us (6%)
  matrix products  9.72 us (5%)
    all_gather x1, waiting for transfers between devices, local(): lax.all_gather(conv_weight4, ('dp', 'space'), axis=3, tiled=True)  47.8 us
    all_gather x1, waiting for transfers between devices, local(): lax.all_gather(conv_weight3, ('dp', 'space'), axis=3, tiled=True)  19.4 us
    all_gather x1, blocking collectives, local(): gathered5 = lax.all_gather(lateral5, 'space', axis=1, tiled=True)  14.5 us
    psum x1, blocking collectives, norm_levels(): center = lax.psum(group_totals(record[0], G), 'space') / volume  14.4 us
    all_gather x1, waiting for transfers between devices, local(): lax.all_gather(conv_weight5, ('dp', 'space'), axis=3, tiled=True)  13.5 us
    psum x1, blocking collectives, norm_levels(): spread = lax.psum(square_terms(record[0], center, G), 'space') / volume  11.8 us
    conv_general_dilated x3, matrix products, convolve(): lax.conv_general_dilated(padded, kernel, (1, 1), (margin, (1, 1)), dimens...  9.72 us
    ppermute x2, starting transfers between devices, extended(): before = lax.ppermute(last, axis, up)  7.53 us
  transfers between devices with their start and end apart: 8, of which 4 were waited for; matrix products, arithmetic and copies ran while one was open for 18% of the time, Pallas kernels for 0%

commit v1 on v0

v1 whole, which is shorter than its diff:
```python
import functools

import jax
import jax.numpy as jnp
from jax import lax
from jax.experimental import pallas as pl
from jax.experimental.pallas import tpu as pltpu
from jax.sharding import PartitionSpec as P

G = 32
EPSILON = 1e-05
LANES = 128
AXES = ("dp", "space")
F32 = jnp.float32
BF16 = jnp.bfloat16
VMEM = pl.BlockSpec(memory_space=pltpu.VMEM)
ANY = pl.BlockSpec(memory_space=pl.ANY)


def exchange(array, axes, size, mask):
    return lax.ppermute(array, axes, [(i, i ^ mask) for i in range(size)])


def joined(first, second):
    return jnp.concatenate([first, second], axis=0)


def gathered_by_doubling(shards, bits):
    size = lax.axis_size(AXES)
    lead, turning = bits[:-3], bits[-3:]
    swap = functools.partial(exchange, axes=AXES, size=size)
    lengths = [s.shape[0] for s in shards]
    together = jnp.concatenate(shards, axis=0)[None]
    masks = [0]
    for bit in lead:
        together = joined(together, swap(together, mask=bit))
        masks = masks + [m ^ bit for m in masks]
    chunks, start = [], 0
    for length in lengths:
        chunks.append(together[:, start : start + length])
        start += length
    orders = [[turning[(k + step) % 3] for step in range(3)] for k in range(len(chunks))]
    held = [list(masks) for _ in chunks]
    for step in range(2):
        received = [swap(c, mask=o[step]) for c, o in zip(chunks, orders)]
        chunks = [joined(c, r) for c, r in zip(chunks, received)]
        held = [h + [m ^ o[step] for m in h] for h, o in zip(held, orders)]
    result = []
    for chunk, order, owner in zip(chunks, orders, held):
        received = swap(chunk, mask=order[2])
        parts = [chunk, received, swap(chunk, mask=1), swap(received, mask=1)]
        owners = [owner] + [[m ^ x for m in owner] for x in (order[2], 1, order[2] ^ 1)]
        result.append((parts, owners))
    return result


def weight_parts(weights):
    size = lax.axis_size(AXES)
    shards = []
    for weight in weights:
        rows, columns, inner, outer = weight.shape
        shards.append(jnp.transpose(weight, (0, 1, 3, 2)).reshape(rows * columns, outer, inner))
    bits = [1 << k for k in range(size.bit_length() - 1)][::-1][:-1]
    if size == 2 << (len(bits)) and len(bits) >= 3 and shards[0].shape[1] % 8 == 0:
        return gathered_by_doubling(shards, bits)
    result = []
    for shard in shards:
        whole = lax.all_gather(shard, AXES, axis=1, tiled=True)
        taps, outer, inner = whole.shape
        blocks = jnp.transpose(whole.reshape(taps, outer // 8, 8, inner), (1, 0, 2, 3))
        result.append(([blocks], None))
    return result


def halos(top, bottom):
    count = lax.axis_size("space")
    before = lax.ppermute(bottom, "space", [(i, i + 1) for i in range(count - 1)])
    after = lax.ppermute(top, "space", [(i + 1, i) for i in range(count - 1)])
    return before, after


def statistics_of_all(own):
    size = lax.axis_size("space")
    swap = functools.partial(exchange, axes="space", size=size)
    bits = [1 << k for k in range(size.bit_length() - 1)]
    if size != 1 << len(bits):
        return [lax.all_gather(own, "space")]
    held = [own[None]]
    for start in range(0, len(bits), 2) if len(bits) % 2 == 0 else [-1] + list(range(1, len(bits), 2)):
        some = bits[max(start, 0) : start + 2]
        whole = held[0] if len(held) == 1 else jnp.concatenate(held, axis=0)
        masks = some if len(some) == 1 else some + [some[0] | some[1]]
        held = [whole] + [swap(whole, mask=m) for m in masks]
    return held


def call(body, outs, ins, scratch, flops, in_specs=None, out_specs=None):
    moved = sum(a.size * a.dtype.itemsize for a in list(outs) + list(ins))
    return pl.pallas_call(
        body,
        out_shape=outs,
        in_specs=in_specs or [VMEM] * len(ins),
        out_specs=out_specs or [VMEM] * len(outs),
        scratch_shapes=scratch,
        cost_estimate=pl.CostEstimate(flops=flops, bytes_accessed=moved, transcendentals=0),
    )(*ins)


def stretched(scratch, values):
    rows = values.shape[0]
    pieces = []
    for k in range(scratch.shape[0]):
        piece = values[:, k * LANES : (k + 1) * LANES]
        scratch[k, pl.ds(0, rows, stride=2), :] = piece
        scratch[k, pl.ds(1, rows, stride=2), :] = piece
        pieces.append(scratch[k])
    return jnp.concatenate(pieces, axis=1)


def merge_body(l3, l4, l5, m3, m4, top, bottom, fine, middle):
    images, rows5 = l5.shape[0], l5.shape[1]
    for b in range(images):
        for r5 in range(rows5):
            up5 = stretched(middle, l5[b, r5].astype(F32))
            for r4 in (2 * r5, 2 * r5 + 1):
                v4 = (l4[b, r4].astype(F32) + up5).astype(BF16)
                m4[b, r4] = v4
                up4 = stretched(fine, v4.astype(F32))
                for r3 in (2 * r4, 2 * r4 + 1):
                    m3[b, r3] = (l3[b, r3].astype(F32) + up4).astype(BF16)
        start = 0
        for source in (m3, m4, l5):
            width = source.shape[2]
            top[b, start : start + width] = source[b, 0]
            bottom[b, start : start + width] = source[b, source.shape[1] - 1]
            start += width


def merge(l3, l4, l5):
    images, _, width3, channels = l3.shape
    width = width3 + l4.shape[2] + l5.shape[2]
    edge = jax.ShapeDtypeStruct((images, width, channels), BF16)
    outs = [jax.ShapeDtypeStruct(l3.shape, BF16), jax.ShapeDtypeStruct(l4.shape, BF16), edge, edge]
    scratch = [pltpu.VMEM((channels // LANES, w, LANES), F32) for w in (width3, l4.shape[2])]
    return call(merge_body, outs, [l3, l4, l5], scratch, 4 * l3.size)


def spread_body(m3, m4, l5, before, after, x3, x4, x5):
    start = 0
    for source, target in ((m3, x3), (m4, x4), (l5, x5)):
        images, rows, width, channels = source.shape
        place = lax.broadcasted_iota(jnp.int32, (width, channels), 0)
        for r in range(rows + 2):
            for b in range(images):
                if r == 0:
                    middle = before[b, start : start + width]
                elif r == rows + 1:
                    middle = after[b, start : start + width]
                else:
                    middle = source[b, r - 1]
                wide = middle.astype(F32)
                left = jnp.where(place == 0, 0.0, pltpu.roll(wide, 1, 0))
                right = jnp.where(place == width - 1, 0.0, pltpu.roll(wide, width - 1, 0))
                target[b, r, :, 0:channels] = left.astype(BF16)
                target[b, r, :, channels : 2 * channels] = middle
                target[b, r, :, 2 * channels : 3 * channels] = right.astype(BF16)
        start += width


def spread(levels, before, after):
    outs = [
        jax.ShapeDtypeStruct((a.shape[0], a.shape[1] + 2, a.shape[2], 3 * a.shape[3]), BF16)
        for a in levels
    ]
    return call(spread_body, outs, list(levels) + [before, after], [], 8 * sum(o.size for o in outs))


def conv_body(counts, owners, me_ref, *refs):
    levels = len(counts)
    refs = list(refs)
    xs, refs = refs[:levels], refs[levels:]
    parts = []
    for count in counts:
        parts.append(refs[:count])
        refs = refs[count:]
    outs, stats, blocks, kernel = refs[:levels], refs[levels], refs[levels + 1], refs[levels + 2]
    me = me_ref[0]
    taps, block_count, block, inner = blocks.shape
    for level in range(levels):
        x, out = xs[level], outs[level]
        base = 0
        for k, part in enumerate(parts[level]):
            for j in range(part.shape[0]):
                if owners[level] is None:
                    blocks[:, base + j] = part[j]
                else:
                    per = part.shape[2] // block
                    owner = me ^ owners[level][k][j]
                    for i in range(per):
                        blocks[:, owner * per + i] = part[j, :, i * block : (i + 1) * block]
            base += part.shape[0]
        for tap in range(taps):
            kernel[:, tap * inner : (tap + 1) * inner] = blocks[tap].reshape(block_count * block, inner)
        images, rows, width, outer = out.shape
        area = rows * width
        group = max(1, min(images, 512 // area))
        while images % group:
            group -= 1
        for b in range(0, images, group):
            wide = jnp.concatenate(
                [x[b : b + group, a : a + rows].reshape(group * area, 3 * inner) for a in range(3)],
                axis=1,
            )
            value = lax.dot_general(
                wide, kernel[...], (((1,), (1,)), ((), ())), preferred_element_type=F32
            )
            out[b : b + group] = value.reshape(group, rows, width, outer)
            for i in range(group):
                mine = value[i * area : (i + 1) * area]
                mean = jnp.sum(mine, axis=0, keepdims=True) * (1.0 / area)
                deviation = mine - mean
                line = level * 2 * images + b + i
                stats[line : line + 1] = mean
                stats[line + images : line + images + 1] = jnp.sum(
                    deviation * deviation, axis=0, keepdims=True
                )


def convolve(me, xs, weights):
    inner = xs[0].shape[3] // 3
    sample = weights[0][0][0]
    outer = sum(p.shape[0] * p.shape[2] for p in weights[0][0])
    outs = [
        jax.ShapeDtypeStruct((x.shape[0], x.shape[1] - 2, x.shape[2], outer), F32) for x in xs
    ]
    flops = sum(2 * o.size * 9 * inner for o in outs)
    outs.append(jax.ShapeDtypeStruct((2 * xs[0].shape[0] * len(xs), outer), F32))
    body = functools.partial(
        conv_body, [len(w[0]) for w in weights], [w[1] for w in weights]
    )
    ins = [me] + list(xs) + [p for w in weights for p in w[0]]
    scratch = [
        pltpu.VMEM((sample.shape[1], outer // 8, 8, inner), BF16),
        pltpu.VMEM((outer, sample.shape[1] * inner), BF16),
    ]
    specs = [pl.BlockSpec(memory_space=pltpu.SMEM)] + [VMEM] * (len(ins) - 1)
    result = call(body, outs, ins, scratch, flops, in_specs=specs)
    return result[:-1], result[-1]


def group_sums(values, size):
    lanes = values.shape[1]
    lane = lax.broadcasted_iota(jnp.int32, values.shape, 1)
    step = 1
    while step < size:
        up, down = pltpu.roll(values, lanes - step, 1), pltpu.roll(values, step, 1)
        values = values + jnp.where((lane & step) == 0, up, down)
        step *= 2
    return values


def norm_body(levels, pieces, *refs):
    refs = list(refs)
    xs, refs = refs[:levels], refs[levels:]
    affine, refs = refs[: 2 * levels], refs[2 * levels :]
    stats, refs = refs[:pieces], refs[pieces:]
    outs, refs = refs[:levels], refs[levels:]
    ys, sems = refs[:levels], refs[levels]
    images = xs[0].shape[0]
    channels = xs[0].shape[3]
    size = channels // G
    strips = [s[i] for s in stats for i in range(s.shape[0])]
    count = len(strips) * size
    total = group_sums(functools.reduce(jnp.add, strips), size)
    centers = total * (1.0 / count)
    apart = [(s - centers) for s in strips]
    between = group_sums(functools.reduce(jnp.add, [a * a for a in apart]), size)
    copies = []
    for level in range(levels):
        x, y = xs[level], ys[level]
        area = x.shape[1] * x.shape[2]
        first = level * 2 * images
        center = centers[first : first + images]
        spread = (
            total[first + images : first + 2 * images] + between[first : first + images] * area
        ) * (1.0 / (count * area))
        scale = lax.rsqrt(spread + EPSILON) * affine[2 * level][...]
        shift = affine[2 * level + 1][...]
        for b in range(images):
            flat = x[b].reshape(area, channels)
            line = (flat - center[b : b + 1]) * scale[b : b + 1] + shift
            y[b] = line.reshape(x.shape[1:])
            copy = pltpu.make_async_copy(y.at[b], outs[level].at[b], sems.at[level * images + b])
            copy.start()
            copies.append(copy)
    for copy in copies:
        copy.wait()


def normalize(xs, affine, stats):
    outs = [jax.ShapeDtypeStruct(x.shape, F32) for x in xs]
    ins = list(xs) + list(affine) + list(stats)
    scratch = [pltpu.VMEM(x.shape, F32) for x in xs]
    scratch.append(pltpu.SemaphoreType.DMA((len(xs) * xs[0].shape[0],)))
    body = functools.partial(norm_body, len(xs), len(stats))
    return call(
        body, outs, ins, scratch, 8 * sum(x.size for x in xs), out_specs=[ANY] * len(outs)
    )


def local(l3, l4, l5, w3, w4, w5, gain3, shift3, gain4, shift4, gain5, shift5):
    weights = weight_parts([w3, w4, w5])
    m3, m4, top, bottom = merge(l3, l4, l5)
    before, after = halos(top, bottom)
    x3, x4, x5 = spread((m3, m4, l5), before, after)
    me = lax.axis_index(AXES).astype(jnp.int32).reshape(1)
    (f3,), stats3 = convolve(me, [x3], weights[:1])
    (f4,), stats4 = convolve(me, [x4], weights[1:2])
    (f5,), stats5 = convolve(me, [x5], weights[2:])
    stats = statistics_of_all(jnp.concatenate([stats3, stats4, stats5], axis=0))
    affine = [a[None] for a in (gain3, shift3, gain4, shift4, gain5, shift5)]
    return tuple(normalize([f3, f4, f5], affine, stats))


def solution(mesh):
    image = P("dp", "space", None, None)
    weight = P(None, None, None, AXES)
    return jax.shard_map(
        local,
        mesh=mesh,
        in_specs=(image,) * 3 + (weight,) * 3 + (P(),) * 6,
        out_specs=(image,) * 3,
        check_vma=False,
    )
```

time: 202 us -> 82 us (0.41)
  waiting for transfers between devices: 84.8 us -> 28.8 us
  blocking collectives: 40.7 us -> 0 us
  Pallas kernels: 0 us -> 24.9 us
  local copies, waits for them, and re-layouts: 25.7 us -> 2.04 us
  between operations: 14.3 us -> 0.87 us
  other arithmetic: 12.7 us -> 1.7 us
  matrix products: 9.72 us -> 0 us
  starting transfers between devices: 13.7 us -> 23.2 us
    all_gather x3 -> x0, waiting for transfers between devices: 80.6 us -> none  [the longest x1 47.8 us: local(): lax.all_gather(conv_weight4, ('dp', 'space'), axis=3, tiled=True)]
    ppermute x4 -> x22, waiting for transfers between devices: 0.01 us -> 28.8 us  [the longest x20 28.8 us: exchange(): return lax.ppermute(array, axes, [(i, i ^ mask) for i in range(size)])]
    psum x2 -> x0, blocking collectives: 26.2 us -> none  [the longest x1 14.4 us: norm_levels(): center = lax.psum(group_totals(record[0], G), 'space') / volume]
    pallas_call x0 -> x6, Pallas kernels: none -> 24.9 us  [call(): pl.pallas_call(body, out_shape=outs, in_specs=in_specs or [VMEM] * len(in...]
    all_gather x1 -> x0, blocking collectives: 14.5 us -> none  [local(): gathered5 = lax.all_gather(lateral5, 'space', axis=1, tiled=True)]
    ppermute x4 -> x22, starting transfers between devices: 10.1 us -> 23.2 us  [the longest x20 20.6 us: exchange(): return lax.ppermute(array, axes, [(i, i ^ mask) for i in range(size)])]
    conv_general_dilated x3 -> x0, matrix products: 9.72 us -> none  [convolve(): lax.conv_general_dilated(padded, kernel, (1, 1), (margin, (1, 1)), dimens...]
    unnamed x32 -> x30, local copies, waits for them, and re-layouts: 7.38 us -> 2.04 us
  transfers between devices with their start and end apart: 8 -> 22, of which waited for: 4 -> 10; matrix products, arithmetic and copies ran while one was open for 18% -> 0% of each run, Pallas kernels for 0% -> 22%
where the time goes in v1:
time: 82 us; the launch traced here: 81.6 us
  waiting for transfers between devices  28.8 us (35%)
  Pallas kernels  24.9 us (30%)
  starting transfers between devices  23.2 us (28%)
  local copies, waits for them, and re-layouts  2.04 us (2%)
  other arithmetic  1.7 us (2%)
  between operations  0.87 us (1%)
    ppermute x20, waiting for transfers between devices, exchange(): return lax.ppermute(array, axes, [(i, i ^ mask) for i in range(size)])  28.8 us
    pallas_call x6, Pallas kernels, call(): pl.pallas_call(body, out_shape=outs, in_specs=in_specs or [VMEM] * len(in...  24.9 us
    ppermute x20, starting transfers between devices, exchange(): return lax.ppermute(array, axes, [(i, i ^ mask) for i in range(size)])  20.6 us
    unnamed x30, local copies, waits for them, and re-layouts  2.04 us
  transfers between devices with their start and end apart: 22, of which 10 were waited for; matrix products, arithmetic and copies ran while one was open for 0% of the time, Pallas kernels for 22%

profile of v1, /device:TPU:0, one launch (start us, length us, event | category | flops | bytes accessed | tf_op | source)
XLA Modules:
  0.0 81.6 jit_solution(18073805123783448986)
XLA Ops:
  0.6 0.8 %maximum_bitcast_fusion = bf16[1,27,8,256]{3,2,1,0:T(8,128)(2,1)S(1)} fusion(bf16[9,8,256]{2,1,0:T(8,128)(2,1)} %bitcast.20, bf16[9,8,256]{2,1,0:T(8,128)(2,1)} %bitcast.21, bf16[9,8,256]{2,1,0:T(8,128)(2,1)} %bitcast.22), kind=kLoop, calls=%fused_computation.10 | loop fusion | flops 110592 | bytes 221184 | tf_op jit(solution)/shard_map/broadcast_in_dim | solution.py:33
  1.5 4.1 %collective-permute-start.2 = (bf16[1,27,8,256]{3,2,1,0:T(8,128)(2,1)S(1)}, bf16[1,27,8,256]{3,2,1,0:T(8,128)(2,1)S(1)}, u32[]{:S(2)}, u32[]{:S(2)}) collective-permute-start(bf16[1,27,8,256]{3,2,1,0:T(8,128)(2,1)S(1)} %maximum_bitcast_fusion), channel_id=1, source_target_pairs={{0,16},{1,17},{2,18},{3,19},{4,20},{5,21},{6,22},{7,23},{8,24},{9,... | collective-permute-start | bytes 331784 | tf_op jit(solution)/shard_map/ppermute | solution.py:21
  5.6 5.4 %collective-permute-done.2 = bf16[1,27,8,256]{3,2,1,0:T(8,128)(2,1)S(1)} collective-permute-done((bf16[1,27,8,256]{3,2,1,0:T(8,128)(2,1)S(1)}, bf16[1,27,8,256]{3,2,1,0:T(8,128)(2,1)S(1)}, u32[]{:S(2)}, u32[]{:S(2)}) %collective-permute-start.2) | collective-permute-done | bytes 110624 | tf_op jit(solution)/shard_map/ppermute | solution.py:21
  11.0 1.6 %collective-permute-start.8 = (bf16[2,9,8,256]{3,2,1,0:T(8,128)(2,1)S(1)}, bf16[2,9,8,256]{3,2,1,0:T(8,128)(2,1)S(1)}, u32[]{:S(2)}, u32[]{:S(2)}) collective-permute-start(bf16[2,9,8,256]{3,2,1,0:T(8,128)(2,1)S(1)} %get-tuple-element.31), channel_id=1, source_target_pairs={{0,4},{1,5},{2,6},{3,7},{4,0},{5,1},{6,2},{7,3},{8,12},{9,13},{10,... | collective-permute-start | bytes 221192 | tf_op jit(solution)/shard_map/ppermute | solution.py:21
  12.7 2.9 %shard_map.139 = (bf16[4,4,128,256]{3,2,1,0:T(8,128)(2,1)}, bf16[4,2,64,256]{3,2,1,0:T(8,128)(2,1)}, bf16[4,224,256]{2,1,0:T(8,128)(2,1)}, bf16[4,224,256]{2,1,0:T(8,128)(2,1)}) custom-call(bf16[4,4,128,256]{3,2,1,0:T(8,128)(2,1)} %l3.1, bf16[4,2,64,256]{3,2,1,0:T(8,128)(2,1)} %l4.1, bf16[4,1,32,256]{3,2,1,0:T(8,128)(2,1)} %l5.3), custom_call_target="tpu_custom_call" | custom-call | flops 2097152 | bytes 3604480 | tf_op jit(solution)/shard_map/pallas_call | solution.py:99
  15.6 1.3 %collective-permute-start = (bf16[4,224,256]{2,1,0:T(8,128)(2,1)}, bf16[4,224,256]{2,1,0:T(8,128)(2,1)S(1)}, u32[]{:S(2)}, u32[]{:S(2)}) collective-permute-start(bf16[4,224,256]{2,1,0:T(8,128)(2,1)} %get-tuple-element.18), channel_id=1, source_target_pairs={{0,1},{1,2},{2,3},{3,4},{4,5},{5,6},{6,7},{8,9},{9,10},{10,11},{11... | collective-permute-start | bytes 1376264 | tf_op jit(solution)/shard_map/ppermute | solution.py:77
  16.9 1.3 %collective-permute-start.1 = (bf16[4,224,256]{2,1,0:T(8,128)(2,1)}, bf16[4,224,256]{2,1,0:T(8,128)(2,1)S(1)}, u32[]{:S(2)}, u32[]{:S(2)}) collective-permute-start(bf16[4,224,256]{2,1,0:T(8,128)(2,1)} %get-tuple-element.19), channel_id=1, source_target_pairs={{1,0},{2,1},{3,2},{4,3},{5,4},{6,5},{7,6},{9,8},{10,9},{11,10},{12... | collective-permute-start | bytes 1376264 | tf_op jit(solution)/shard_map/ppermute | solution.py:78
  18.2 1.1 %collective-permute-start.3 = (bf16[2,9,8,256]{3,2,1,0:T(8,128)(2,1)S(1)}, bf16[2,9,8,256]{3,2,1,0:T(8,128)(2,1)S(1)}, u32[]{:S(2)}, u32[]{:S(2)}) collective-permute-start(bf16[2,9,8,256]{3,2,1,0:T(8,128)(2,1)S(1)} %get-tuple-element.30), channel_id=1, source_target_pairs={{0,8},{1,9},{2,10},{3,11},{4,12},{5,13},{6,14},{7,15},{8,0},{9,1},... | collective-permute-start | bytes 221192 | tf_op jit(solution)/shard_map/ppermute | solution.py:21
  19.3 4.1 %collective-permute-start.13 = (bf16[2,9,8,256]{3,2,1,0:T(8,128)(2,1)S(1)}, bf16[2,9,8,256]{3,2,1,0:T(8,128)(2,1)S(1)}, u32[]{:S(2)}, u32[]{:S(2)}) collective-permute-start(bf16[2,9,8,256]{3,2,1,0:T(8,128)(2,1)S(1)} %get-tuple-element.29), channel_id=1, source_target_pairs={{0,2},{1,3},{2,0},{3,1},{4,6},{5,7},{6,4},{7,5},{8,10},{9,11},{10,... | collective-permute-start | bytes 221192 | tf_op jit(solution)/shard_map/ppermute | solution.py:21
  23.4 0.0 collective-permute-done.8
  23.4 0.1 collective-permute-start.9
  23.5 0.0 collective-permute-done.3
  23.5 3.5 %collective-permute-start.4 = (bf16[4,9,8,256]{3,2,1,0:T(8,128)(2,1)S(1)}, bf16[4,9,8,256]{3,2,1,0:T(8,128)(2,1)S(1)}, u32[]{:S(2)}, u32[]{:S(2)}) collective-permute-start(bf16[4,9,8,256]{3,2,1,0:T(8,128)(2,1)S(1)} %pad_maximum_fusion.3), channel_id=1, source_target_pairs={{0,4},{1,5},{2,6},{3,7},{4,0},{5,1},{6,2},{7,3},{8,12},{9,13},{10,... | collective-permute-start | bytes 442376 | tf_op jit(solution)/shard_map/ppermute | solution.py:21
  27.0 6.5 %collective-permute-done.13 = bf16[2,9,8,256]{3,2,1,0:T(8,128)(2,1)S(1)} collective-permute-done((bf16[2,9,8,256]{3,2,1,0:T(8,128)(2,1)S(1)}, bf16[2,9,8,256]{3,2,1,0:T(8,128)(2,1)S(1)}, u32[]{:S(2)}, u32[]{:S(2)}) %collective-permute-start.13) | collective-permute-done | bytes 73760 | tf_op jit(solution)/shard_map/ppermute | solution.py:21
  33.6 0.8 collective-permute-start.14
  34.4 1.5 %collective-permute-done.9 = bf16[4,9,8,256]{3,2,1,0:T(8,128)(2,1)S(1)} collective-permute-done((bf16[4,9,8,256]{3,2,1,0:T(8,128)(2,1)S(1)}, bf16[4,9,8,256]{3,2,1,0:T(8,128)(2,1)S(1)}, u32[]{:S(2)}, u32[]{:S(2)}) %collective-permute-start.9) | collective-permute-done | bytes 147488 | tf_op jit(solution)/shard_map/ppermute | solution.py:21
  35.8 0.0 copy-start
  35.9 0.3 collective-permute-start.10
  36.1 0.0 collective-permute-done.4
  36.1 0.0 copy-start.7
  36.2 0.1 collective-permute-start.5
  36.2 2.5 %collective-permute-done.14 = bf16[4,9,8,256]{3,2,1,0:T(8,128)(2,1)S(1)} collective-permute-done((bf16[4,9,8,256]{3,2,1,0:T(8,128)(2,1)S(1)}, bf16[4,9,8,256]{3,2,1,0:T(8,128)(2,1)S(1)}, u32[]{:S(2)}, u32[]{:S(2)}) %collective-permute-start.14) | collective-permute-done | bytes 147488 | tf_op jit(solution)/shard_map/ppermute | solution.py:21
  38.8 0.0 collective-permute-start.11
  38.8 0.0 copy-start.1
  38.8 0.0 collective-permute-done.before
  38.8 0.0 copy-start.2
  38.8 0.1 collective-permute-start.15
  38.9 3.7 %collective-permute-done.10.refs_2_ = bf16[8,9,8,256]{3,2,1,0:T(8,128)(2,1)S(1)} collective-permute-done((bf16[8,9,8,256]{3,2,1,0:T(8,128)(2,1)S(1)}, bf16[8,9,8,256]{3,2,1,0:T(8,128)(2,1)S(1)}, u32[]{:S(2)}, u32[]{:S(2)}) %collective-permute-start.10) | collective-permute-done | bytes 294944 | tf_op jit(solution)/shard_map/ppermute | solution.py:21
  42.6 0.0 collective-permute-start.12
  42.6 0.0 collective-permute-done.1.after
  42.7 0.0 copy-start.3
  42.7 0.5 collective-permute-start.6
  43.2 0.0 collective-permute-done.5.refs_2_
  43.2 0.1 collective-permute-start.7
  43.2 0.0 collective-permute-done.11.refs_3_
  43.2 0.4 collective-permute-start.16
  43.7 4.6 %collective-permute-done.15.refs_2_ = bf16[8,9,8,256]{3,2,1,0:T(8,128)(2,1)S(1)} collective-permute-done((bf16[8,9,8,256]{3,2,1,0:T(8,128)(2,1)S(1)}, bf16[8,9,8,256]{3,2,1,0:T(8,128)(2,1)S(1)}, u32[]{:S(2)}, u32[]{:S(2)}) %collective-permute-start.15) | collective-permute-done | bytes 294944 | tf_op jit(solution)/shard_map/ppermute | solution.py:21
  48.3 0.0 collective-permute-start.17
  48.3 0.0 copy-done.2
  48.3 4.9 %shard_map.140 = (bf16[4,6,128,768]{3,2,1,0:T(8,128)(2,1)}, bf16[4,4,64,768]{3,2,1,0:T(8,128)(2,1)}, bf16[4,3,32,768]{3,2,1,0:T(8,128)(2,1)}) custom-call(bf16[4,4,128,256]{3,2,1,0:T(8,128)(2,1)} %get-tuple-element.16.m3, bf16[4,2,64,256]{3,2,1,0:T(8,128)(2,1)} %get-tuple-element.17.m4, bf16[4,1,32,256]{3,2,1,0:T(8,128)(2,1)} %l5.3, ...), custom_call_target="tpu_custom_call" | custom-call | flops 27525120 | bytes 9175040 | tf_op jit(solution)/shard_map/pallas_call | solution.py:99
  53.3 0.0 collective-permute-done.12.refs_4_
  53.3 0.7 copy-done.6
  54.0 3.5 %shard_map.142 = (f32[4,2,64,256]{3,2,1,0:T(8,128)}, f32[8,256]{1,0:T(8,128)}) custom-call(s32[1]{0:T(128)} %bitcast.me_ref, bf16[4,4,64,768]{3,2,1,0:T(8,128)(2,1)} %get-tuple-element.22.refs_0_, bf16[8,9,8,256]{3,2,1,0:T(8,128)(2,1)} %copy-done, bf16[8,9,8,256]{3,2,1,0:T(8,128)(2,1)} %copy-done.4, bf16[8,9,8,256]{3,2,1,0:T(8,128)(2,1)} %copy-done.5, ...), custom_call_target="tpu_custom_call" | custom-call | flops 603979776 | bytes 3284996 | tf_op jit(solution)/shard_map/pallas_call | solution.py:99
  57.5 0.0 copy-done.1
  57.5 0.0 copy-done.8
  57.5 0.0 collective-permute-done.6.refs_3_
  57.5 0.0 collective-permute-done.7.refs_4_
  57.5 6.8 %shard_map.141 = (f32[4,4,128,256]{3,2,1,0:T(8,128)}, f32[8,256]{1,0:T(8,128)}) custom-call(s32[1]{0:T(128)} %bitcast.me_ref, bf16[4,6,128,768]{3,2,1,0:T(8,128)(2,1)} %get-tuple-element.20.refs_0_, bf16[8,9,8,256]{3,2,1,0:T(8,128)(2,1)} %copy-done.7, bf16[8,9,8,256]{3,2,1,0:T(8,128)(2,1)} %collective-permute-done.5.refs_2_, ...), custom_call_target="tpu_custom_call" | custom-call | flops 2415919104 | bytes 8003588 | tf_op jit(solution)/shard_map/pallas_call | solution.py:99
  64.3 0.0 collective-permute-done.16.refs_3_
  64.3 0.0 collective-permute-done.17.refs_4_
  64.3 0.7 copy-done.9
  65.0 2.7 %shard_map.143 = (f32[4,1,32,256]{3,2,1,0:T(8,128)}, f32[8,256]{1,0:T(8,128)}) custom-call(s32[1]{0:T(128)} %bitcast.me_ref, bf16[4,3,32,768]{3,2,1,0:T(8,128)(2,1)} %get-tuple-element.24.refs_0_, bf16[8,9,8,256]{3,2,1,0:T(8,128)(2,1)} %copy-done.1, bf16[8,9,8,256]{3,2,1,0:T(8,128)(2,1)} %copy-done.8, bf16[8,9,8,256]{3,2,1,0:T(8,128)(2,1)} %copy-done.9, ...), custom_call_target="tpu_custom_call" | custom-call | flops 150994944 | bytes 1908740 | tf_op jit(solution)/shard_map/pallas_call | solution.py:99
  67.8 0.7 maximum_bitcast_fusion.1
  68.5 0.4 collective-permute-start.18
  68.9 0.8 %collective-permute-done.18 = f32[1,24,256]{2,1,0:T(8,128)S(1)} collective-permute-done((f32[1,24,256]{2,1,0:T(8,128)S(1)}, f32[1,24,256]{2,1,0:T(8,128)S(1)}, u32[]{:S(2)}, u32[]{:S(2)}) %collective-permute-start.18) | collective-permute-done | bytes 24608 | tf_op jit(solution)/shard_map/ppermute | solution.py:21
  69.7 0.6 collective-permute-start.19
  70.3 1.5 %collective-permute-start.20 = (f32[2,24,256]{2,1,0:T(8,128)S(1)}, f32[2,24,256]{2,1,0:T(8,128)S(1)}, u32[]{:S(2)}, u32[]{:S(2)}) collective-permute-start(f32[2,24,256]{2,1,0:T(8,128)S(1)} %pad_maximum_fusion.7.refs_9_), channel_id=1, source_target_pairs={{0,4},{1,5},{2,6},{3,7},{4,0},{5,1},{6,2},{7,3},{8,12},{9,13},{10,... | collective-permute-start | bytes 147464 | tf_op jit(solution)/shard_map/ppermute | solution.py:21
  71.9 1.3 %collective-permute-start.21 = (f32[2,24,256]{2,1,0:T(8,128)S(1)}, f32[2,24,256]{2,1,0:T(8,128)S(1)}, u32[]{:S(2)}, u32[]{:S(2)}) collective-permute-start(f32[2,24,256]{2,1,0:T(8,128)S(1)} %pad_maximum_fusion.7.refs_9_), channel_id=1, source_target_pairs={{0,6},{1,7},{2,4},{3,5},{4,2},{5,3},{6,0},{7,1},{8,14},{9,15},{10,... | collective-permute-start | bytes 147464 | tf_op jit(solution)/shard_map/ppermute | solution.py:21
  73.2 0.6 collective-permute-done.19.refs_10_
  73.8 0.6 collective-permute-done.20.refs_11_
  74.4 2.4 %collective-permute-done.21.refs_12_ = f32[2,24,256]{2,1,0:T(8,128)S(1)} collective-permute-done((f32[2,24,256]{2,1,0:T(8,128)S(1)}, f32[2,24,256]{2,1,0:T(8,128)S(1)}, u32[]{:S(2)}, u32[]{:S(2)}) %collective-permute-start.21) | collective-permute-done | bytes 49184 | tf_op jit(solution)/shard_map/ppermute | solution.py:21
  76.9 0.0 copy-done.11
  76.9 0.6 copy-done.13
  77.5 4.1 %shard_map.144 = (f32[4,4,128,256]{3,2,1,0:T(8,128)}, f32[4,2,64,256]{3,2,1,0:T(8,128)}, f32[4,1,32,256]{3,2,1,0:T(8,128)}) custom-call(f32[4,4,128,256]{3,2,1,0:T(8,128)} %get-tuple-element.21.refs_0_, f32[4,2,64,256]{3,2,1,0:T(8,128)} %get-tuple-element.23.refs_1_, f32[4,1,32,256]{3,2,1,0:T(8,128)} %get-tuple-element.25.refs_2_, f32[1,256]{1,0:T(1,128)} %bitcast.23, ...), custom_call_target="tpu_custom_call" | custom-call | flops 5505024 | bytes 5707776 | tf_op jit(solution)/shard_map/pallas_call | solution.py:99
  (26 shorter events, 0.2 us)
Async XLA Ops:
  1.5 9.6 %collective-permute-start.2 = (bf16[1,27,8,256]{3,2,1,0:T(8,128)(2,1)S(1)}, bf16[1,27,8,256]{3,2,1,0:T(8,128)(2,1)S(1)}, u32[]{:S(2)}, u32[]{:S(2)}) collective-permute-start(bf16[1,27,8,256]{3,2,1,0:T(8,128)(2,1)S(1)} %maximum_bitcast_fusion), channel_id=1, source_target_pairs={{0,16},{1,17},{2,18},{3,19},{4,20},{5,21},{6,22},{7,23},{8,24},{9,... | collective-permute-start | bytes 331784 | tf_op jit(solution)/shard_map/ppermute | solution.py:21
  11.0 12.3 %collective-permute-start.8 = (bf16[2,9,8,256]{3,2,1,0:T(8,128)(2,1)S(1)}, bf16[2,9,8,256]{3,2,1,0:T(8,128)(2,1)S(1)}, u32[]{:S(2)}, u32[]{:S(2)}) collective-permute-start(bf16[2,9,8,256]{3,2,1,0:T(8,128)(2,1)S(1)} %get-tuple-element.31), channel_id=1, source_target_pairs={{0,4},{1,5},{2,6},{3,7},{4,0},{5,1},{6,2},{7,3},{8,12},{9,13},{10,... | collective-permute-start | bytes 221192 | tf_op jit(solution)/shard_map/ppermute | solution.py:21
  15.6 23.2 %collective-permute-start = (bf16[4,224,256]{2,1,0:T(8,128)(2,1)}, bf16[4,224,256]{2,1,0:T(8,128)(2,1)S(1)}, u32[]{:S(2)}, u32[]{:S(2)}) collective-permute-start(bf16[4,224,256]{2,1,0:T(8,128)(2,1)} %get-tuple-element.18), channel_id=1, source_target_pairs={{0,1},{1,2},{2,3},{3,4},{4,5},{5,6},{6,7},{8,9},{9,10},{10,11},{11... | collective-permute-start | bytes 1376264 | tf_op jit(solution)/shard_map/ppermute | solution.py:77
  16.9 25.8 %collective-permute-start.1 = (bf16[4,224,256]{2,1,0:T(8,128)(2,1)}, bf16[4,224,256]{2,1,0:T(8,128)(2,1)S(1)}, u32[]{:S(2)}, u32[]{:S(2)}) collective-permute-start(bf16[4,224,256]{2,1,0:T(8,128)(2,1)} %get-tuple-element.19), channel_id=1, source_target_pairs={{1,0},{2,1},{3,2},{4,3},{5,4},{6,5},{7,6},{9,8},{10,9},{11,10},{12... | collective-permute-start | bytes 1376264 | tf_op jit(solution)/shard_map/ppermute | solution.py:78
  18.2 5.3 %collective-permute-start.3 = (bf16[2,9,8,256]{3,2,1,0:T(8,128)(2,1)S(1)}, bf16[2,9,8,256]{3,2,1,0:T(8,128)(2,1)S(1)}, u32[]{:S(2)}, u32[]{:S(2)}) collective-permute-start(bf16[2,9,8,256]{3,2,1,0:T(8,128)(2,1)S(1)} %get-tuple-element.30), channel_id=1, source_target_pairs={{0,8},{1,9},{2,10},{3,11},{4,12},{5,13},{6,14},{7,15},{8,0},{9,1},... | collective-permute-start | bytes 221192 | tf_op jit(solution)/shard_map/ppermute | solution.py:21
  19.3 14.3 %collective-permute-start.13 = (bf16[2,9,8,256]{3,2,1,0:T(8,128)(2,1)S(1)}, bf16[2,9,8,256]{3,2,1,0:T(8,128)(2,1)S(1)}, u32[]{:S(2)}, u32[]{:S(2)}) collective-permute-start(bf16[2,9,8,256]{3,2,1,0:T(8,128)(2,1)S(1)} %get-tuple-element.29), channel_id=1, source_target_pairs={{0,2},{1,3},{2,0},{3,1},{4,6},{5,7},{6,4},{7,5},{8,10},{9,11},{10,... | collective-permute-start | bytes 221192 | tf_op jit(solution)/shard_map/ppermute | solution.py:21
  23.4 12.4 %collective-permute-start.9 = (bf16[4,9,8,256]{3,2,1,0:T(8,128)(2,1)S(1)}, bf16[4,9,8,256]{3,2,1,0:T(8,128)(2,1)S(1)}, u32[]{:S(2)}, u32[]{:S(2)}) collective-permute-start(bf16[4,9,8,256]{3,2,1,0:T(8,128)(2,1)S(1)} %pad_maximum_fusion.4), channel_id=1, source_target_pairs={{0,2},{1,3},{2,0},{3,1},{4,6},{5,7},{6,4},{7,5},{8,10},{9,11},{10,... | collective-permute-start | bytes 442376 | tf_op jit(solution)/shard_map/ppermute | solution.py:21
  23.5 12.6 %collective-permute-start.4 = (bf16[4,9,8,256]{3,2,1,0:T(8,128)(2,1)S(1)}, bf16[4,9,8,256]{3,2,1,0:T(8,128)(2,1)S(1)}, u32[]{:S(2)}, u32[]{:S(2)}) collective-permute-start(bf16[4,9,8,256]{3,2,1,0:T(8,128)(2,1)S(1)} %pad_maximum_fusion.3), channel_id=1, source_target_pairs={{0,4},{1,5},{2,6},{3,7},{4,0},{5,1},{6,2},{7,3},{8,12},{9,13},{10,... | collective-permute-start | bytes 442376 | tf_op jit(solution)/shard_map/ppermute | solution.py:21
  33.6 5.2 %collective-permute-start.14 = (bf16[4,9,8,256]{3,2,1,0:T(8,128)(2,1)S(1)}, bf16[4,9,8,256]{3,2,1,0:T(8,128)(2,1)S(1)}, u32[]{:S(2)}, u32[]{:S(2)}) collective-permute-start(bf16[4,9,8,256]{3,2,1,0:T(8,128)(2,1)S(1)} %pad_maximum_fusion.5), channel_id=1, source_target_pairs={{0,8},{1,9},{2,10},{3,11},{4,12},{5,13},{6,14},{7,15},{8,0},{9,1},... | collective-permute-start | bytes 442376 | tf_op jit(solution)/shard_map/ppermute | solution.py:21
  35.8 17.4 %copy-start = (bf16[8,9,8,256]{3,2,1,0:T(8,128)(2,1)}, bf16[8,9,8,256]{3,2,1,0:T(8,128)(2,1)S(1)}, u32[]{:S(2)}) copy-start(bf16[8,9,8,256]{3,2,1,0:T(8,128)(2,1)S(1)} %pad_maximum_fusion.1.refs_1_) | copy-start | bytes 884740
  35.9 6.8 %collective-permute-start.10 = (bf16[8,9,8,256]{3,2,1,0:T(8,128)(2,1)S(1)}, bf16[8,9,8,256]{3,2,1,0:T(8,128)(2,1)S(1)}, u32[]{:S(2)}, u32[]{:S(2)}) collective-permute-start(bf16[8,9,8,256]{3,2,1,0:T(8,128)(2,1)S(1)} %pad_maximum_fusion.1.refs_1_), channel_id=1, source_target_pairs={{0,8},{1,9},{2,10},{3,11},{4,12},{5,13},{6,14},{7,15},{8,0},{9,1},... | collective-permute-start | bytes 884744 | tf_op jit(solution)/shard_map/ppermute | solution.py:21
  36.1 21.3 %copy-start.7 = (bf16[8,9,8,256]{3,2,1,0:T(8,128)(2,1)}, bf16[8,9,8,256]{3,2,1,0:T(8,128)(2,1)S(1)}, u32[]{:S(2)}) copy-start(bf16[8,9,8,256]{3,2,1,0:T(8,128)(2,1)S(1)} %pad_maximum_fusion.refs_1_) | copy-start | bytes 884740
  36.2 7.0 %collective-permute-start.5 = (bf16[8,9,8,256]{3,2,1,0:T(8,128)(2,1)S(1)}, bf16[8,9,8,256]{3,2,1,0:T(8,128)(2,1)}, u32[]{:S(2)}, u32[]{:S(2)}) collective-permute-start(bf16[8,9,8,256]{3,2,1,0:T(8,128)(2,1)S(1)} %pad_maximum_fusion.refs_1_), channel_id=1, source_target_pairs={{0,2},{1,3},{2,0},{3,1},{4,6},{5,7},{6,4},{7,5},{8,10},{9,11},{10,... | collective-permute-start | bytes 884744 | tf_op jit(solution)/shard_map/ppermute | solution.py:21
  38.8 4.5 %collective-permute-start.11 = (bf16[8,9,8,256]{3,2,1,0:T(8,128)(2,1)S(1)}, bf16[8,9,8,256]{3,2,1,0:T(8,128)(2,1)S(1)}, u32[]{:S(2)}, u32[]{:S(2)}) collective-permute-start(bf16[8,9,8,256]{3,2,1,0:T(8,128)(2,1)S(1)} %pad_maximum_fusion.1.refs_1_), channel_id=1, source_target_pairs={{0,1},{1,0},{2,3},{3,2},{4,5},{5,4},{6,7},{7,6},{8,9},{9,8},{10,11... | collective-permute-start | bytes 884744 | tf_op jit(solution)/shard_map/ppermute | solution.py:21
  38.8 18.7 %copy-start.1 = (bf16[8,9,8,256]{3,2,1,0:T(8,128)(2,1)}, bf16[8,9,8,256]{3,2,1,0:T(8,128)(2,1)S(1)}, u32[]{:S(2)}) copy-start(bf16[8,9,8,256]{3,2,1,0:T(8,128)(2,1)S(1)} %pad_maximum_fusion.2.refs_1_) | copy-start | bytes 884740
  38.8 9.5 %copy-start.2 = (bf16[4,224,256]{2,1,0:T(8,128)(2,1)}, bf16[4,224,256]{2,1,0:T(8,128)(2,1)S(1)}, u32[]{:S(2)}) copy-start(bf16[4,224,256]{2,1,0:T(8,128)(2,1)S(1)} %collective-permute-done.before) | copy-start | bytes 1376260
  38.8 9.5 %collective-permute-start.15 = (bf16[8,9,8,256]{3,2,1,0:T(8,128)(2,1)S(1)}, bf16[8,9,8,256]{3,2,1,0:T(8,128)(2,1)S(1)}, u32[]{:S(2)}, u32[]{:S(2)}) collective-permute-start(bf16[8,9,8,256]{3,2,1,0:T(8,128)(2,1)S(1)} %pad_maximum_fusion.2.refs_1_), channel_id=1, source_target_pairs={{0,4},{1,5},{2,6},{3,7},{4,0},{5,1},{6,2},{7,3},{8,12},{9,13},{10,... | collective-permute-start | bytes 884744 | tf_op jit(solution)/shard_map/ppermute | solution.py:21
  42.6 10.6 %copy-start.4 = (bf16[8,9,8,256]{3,2,1,0:T(8,128)(2,1)}, bf16[8,9,8,256]{3,2,1,0:T(8,128)(2,1)S(1)}, u32[]{:S(2)}) copy-start(bf16[8,9,8,256]{3,2,1,0:T(8,128)(2,1)S(1)} %collective-permute-done.10.refs_2_) | copy-start | bytes 884740
  42.6 10.6 %collective-permute-start.12 = (bf16[8,9,8,256]{3,2,1,0:T(8,128)(2,1)S(1)}, bf16[8,9,8,256]{3,2,1,0:T(8,128)(2,1)S(1)}, u32[]{:S(2)}, u32[]{:S(2)}) collective-permute-start(bf16[8,9,8,256]{3,2,1,0:T(8,128)(2,1)S(1)} %collective-permute-done.10.refs_2_), channel_id=1, source_target_pairs={{0,1},{1,0},{2,3},{3,2},{4,5},{5,4},{6,7},{7,6},{8,9},{9,8},{10,11... | collective-permute-start | bytes 884744 | tf_op jit(solution)/shard_map/ppermute | solution.py:21
  42.7 5.7 %copy-start.3 = (bf16[4,224,256]{2,1,0:T(8,128)(2,1)}, bf16[4,224,256]{2,1,0:T(8,128)(2,1)S(1)}, u32[]{:S(2)}) copy-start(bf16[4,224,256]{2,1,0:T(8,128)(2,1)S(1)} %collective-permute-done.1.after) | copy-start | bytes 1376260
  42.7 14.8 %collective-permute-start.6 = (bf16[8,9,8,256]{3,2,1,0:T(8,128)(2,1)S(1)}, bf16[8,9,8,256]{3,2,1,0:T(8,128)(2,1)}, u32[]{:S(2)}, u32[]{:S(2)}) collective-permute-start(bf16[8,9,8,256]{3,2,1,0:T(8,128)(2,1)S(1)} %pad_maximum_fusion.refs_1_), channel_id=1, source_target_pairs={{0,1},{1,0},{2,3},{3,2},{4,5},{5,4},{6,7},{7,6},{8,9},{9,8},{10,11... | collective-permute-start | bytes 884744 | tf_op jit(solution)/shard_map/ppermute | solution.py:21
  43.2 14.3 %collective-permute-start.7 = (bf16[8,9,8,256]{3,2,1,0:T(8,128)(2,1)}, bf16[8,9,8,256]{3,2,1,0:T(8,128)(2,1)}, u32[]{:S(2)}, u32[]{:S(2)}) collective-permute-start(bf16[8,9,8,256]{3,2,1,0:T(8,128)(2,1)} %collective-permute-done.5.refs_2_), channel_id=1, source_target_pairs={{0,1},{1,0},{2,3},{3,2},{4,5},{5,4},{6,7},{7,6},{8,9},{9,8},{10,11... | collective-permute-start | bytes 884744 | tf_op jit(solution)/shard_map/ppermute | solution.py:21
  43.2 10.0 %copy-start.5 = (bf16[8,9,8,256]{3,2,1,0:T(8,128)(2,1)}, bf16[8,9,8,256]{3,2,1,0:T(8,128)(2,1)S(1)}, u32[]{:S(2)}) copy-start(bf16[8,9,8,256]{3,2,1,0:T(8,128)(2,1)S(1)} %collective-permute-done.11.refs_3_) | copy-start | bytes 884740
  43.2 21.0 %collective-permute-start.16 = (bf16[8,9,8,256]{3,2,1,0:T(8,128)(2,1)S(1)}, bf16[8,9,8,256]{3,2,1,0:T(8,128)(2,1)S(1)}, u32[]{:S(2)}, u32[]{:S(2)}) collective-permute-start(bf16[8,9,8,256]{3,2,1,0:T(8,128)(2,1)S(1)} %pad_maximum_fusion.2.refs_1_), channel_id=1, source_target_pairs={{0,1},{1,0},{2,3},{3,2},{4,5},{5,4},{6,7},{7,6},{8,9},{9,8},{10,11... | collective-permute-start | bytes 884744 | tf_op jit(solution)/shard_map/ppermute | solution.py:21
  48.3 9.1 %copy-start.8 = (bf16[8,9,8,256]{3,2,1,0:T(8,128)(2,1)}, bf16[8,9,8,256]{3,2,1,0:T(8,128)(2,1)S(1)}, u32[]{:S(2)}) copy-start(bf16[8,9,8,256]{3,2,1,0:T(8,128)(2,1)S(1)} %collective-permute-done.15.refs_2_) | copy-start | bytes 884740
  48.3 16.0 %collective-permute-start.17 = (bf16[8,9,8,256]{3,2,1,0:T(8,128)(2,1)S(1)}, bf16[8,9,8,256]{3,2,1,0:T(8,128)(2,1)}, u32[]{:S(2)}, u32[]{:S(2)}) collective-permute-start(bf16[8,9,8,256]{3,2,1,0:T(8,128)(2,1)S(1)} %collective-permute-done.15.refs_2_), channel_id=1, source_target_pairs={{0,1},{1,0},{2,3},{3,2},{4,5},{5,4},{6,7},{7,6},{8,9},{9,8},{10,11... | collective-permute-start | bytes 884744 | tf_op jit(solution)/shard_map/ppermute | solution.py:21
  53.3 0.7 copy-start.6
  57.5 10.3 %copy-start.14 = (f32[8,256]{1,0:T(8,128)S(1)}, f32[8,256]{1,0:T(8,128)}, u32[]{:S(2)}) copy-start(f32[8,256]{1,0:T(8,128)} %get-tuple-element.27) | copy-start | bytes 24580
  64.3 0.7 copy-start.9
  68.5 1.3 %collective-permute-start.18 = (f32[1,24,256]{2,1,0:T(8,128)S(1)}, f32[1,24,256]{2,1,0:T(8,128)S(1)}, u32[]{:S(2)}, u32[]{:S(2)}) collective-permute-start(f32[1,24,256]{2,1,0:T(8,128)S(1)} %maximum_bitcast_fusion.1), channel_id=1, source_target_pairs={{0,1},{1,0},{2,3},{3,2},{4,5},{5,4},{6,7},{7,6},{8,9},{9,8},{10,11... | collective-permute-start | bytes 73736 | tf_op jit(solution)/shard_map/ppermute | solution.py:21
  69.7 7.1 %copy-start.10 = (f32[2,24,256]{2,1,0:T(8,128)}, f32[2,24,256]{2,1,0:T(8,128)S(1)}, u32[]{:S(2)}) copy-start(f32[2,24,256]{2,1,0:T(8,128)S(1)} %pad_maximum_fusion.7.refs_9_) | copy-start | bytes 147460
  69.7 4.1 %collective-permute-start.19 = (f32[2,24,256]{2,1,0:T(8,128)S(1)}, f32[2,24,256]{2,1,0:T(8,128)S(1)}, u32[]{:S(2)}, u32[]{:S(2)}) collective-permute-start(f32[2,24,256]{2,1,0:T(8,128)S(1)} %pad_maximum_fusion.7.refs_9_), channel_id=1, source_target_pairs={{0,2},{1,3},{2,0},{3,1},{4,6},{5,7},{6,4},{7,5},{8,10},{9,11},{10,... | collective-permute-start | bytes 147464 | tf_op jit(solution)/shard_map/ppermute | solution.py:21
  70.3 4.1 %collective-permute-start.20 = (f32[2,24,256]{2,1,0:T(8,128)S(1)}, f32[2,24,256]{2,1,0:T(8,128)S(1)}, u32[]{:S(2)}, u32[]{:S(2)}) collective-permute-start(f32[2,24,256]{2,1,0:T(8,128)S(1)} %pad_maximum_fusion.7.refs_9_), channel_id=1, source_target_pairs={{0,4},{1,5},{2,6},{3,7},{4,0},{5,1},{6,2},{7,3},{8,12},{9,13},{10,... | collective-permute-start | bytes 147464 | tf_op jit(solution)/shard_map/ppermute | solution.py:21
  71.9 5.0 %collective-permute-start.21 = (f32[2,24,256]{2,1,0:T(8,128)S(1)}, f32[2,24,256]{2,1,0:T(8,128)S(1)}, u32[]{:S(2)}, u32[]{:S(2)}) collective-permute-start(f32[2,24,256]{2,1,0:T(8,128)S(1)} %pad_maximum_fusion.7.refs_9_), channel_id=1, source_target_pairs={{0,6},{1,7},{2,4},{3,5},{4,2},{5,3},{6,0},{7,1},{8,14},{9,15},{10,... | collective-permute-start | bytes 147464 | tf_op jit(solution)/shard_map/ppermute | solution.py:21
  73.8 3.0 %copy-start.11 = (f32[2,24,256]{2,1,0:T(8,128)}, f32[2,24,256]{2,1,0:T(8,128)S(1)}, u32[]{:S(2)}) copy-start(f32[2,24,256]{2,1,0:T(8,128)S(1)} %collective-permute-done.19.refs_10_) | copy-start | bytes 147460
  74.4 2.5 %copy-start.12 = (f32[2,24,256]{2,1,0:T(8,128)}, f32[2,24,256]{2,1,0:T(8,128)S(1)}, u32[]{:S(2)}) copy-start(f32[2,24,256]{2,1,0:T(8,128)S(1)} %collective-permute-done.20.refs_11_) | copy-start | bytes 147460
  76.9 0.6 copy-start.13

commit v2 on v1

--- a/solution.py
+++ b/solution.py
@@ -6,6 +6,7 @@
 from jax.experimental import pallas as pl
 from jax.experimental.pallas import tpu as pltpu
 from jax.sharding import PartitionSpec as P
+
 
 G = 32
 EPSILON = 1e-05
@@ -17,40 +18,43 @@
 ANY = pl.BlockSpec(memory_space=pl.ANY)
 
 
-def exchange(array, axes, size, mask):
-    return lax.ppermute(array, axes, [(i, i ^ mask) for i in range(size)])
+def exchange(array, axes, size, masks):
+    return lax.ppermute(array, axes, [(i, i ^ masks[i % 2]) for i in range(size)])
 
 
 def joined(first, second):
     return jnp.concatenate([first, second], axis=0)
 
 
-def gathered_by_doubling(shards, bits):
+def gathered_in_chains(shards, bits):
     size = lax.axis_size(AXES)
-    lead, turning = bits[:-3], bits[-3:]
-    swap = functools.partial(exchange, axes=AXES, size=size)
+    lead, (p, q, r) = bits[:-3], bits[-3:]
     lengths = [s.shape[0] for s in shards]
     together = jnp.concatenate(shards, axis=0)[None]
-    masks = [0]
-    for bit in lead:
-        together = joined(together, swap(together, mask=bit))
-        masks = masks + [m ^ bit for m in masks]
-    chunks, start = [], 0
-    for length in lengths:
-        chunks.append(together[:, start : start + length])
-        start += length
-    orders = [[turning[(k + step) % 3] for step in range(3)] for k in range(len(chunks))]
-    held = [list(masks) for _ in chunks]
-    for step in range(2):
-        received = [swap(c, mask=o[step]) for c, o in zip(chunks, orders)]
-        chunks = [joined(c, r) for c, r in zip(chunks, received)]
-        held = [h + [m ^ o[step] for m in h] for h, o in zip(held, orders)]
+    for k, bit in enumerate(lead):
+        received = exchange(together, AXES, size, (bit, bit))
+        if k + 1 < len(lead):
+            together = joined(together, received)
+    cut = lengths[0]
+    halves = [(together[:, :cut], received[:, :cut]), (together[:, cut:], received[:, cut:])]
+    orders = [[(q, r), (r, q), (p, p)], [(p, p), (q, r), (r, q)]]
+    swapped = [(len(lead), len(lead) + 1), (len(lead) + 1, len(lead) + 2)]
     result = []
-    for chunk, order, owner in zip(chunks, orders, held):
-        received = swap(chunk, mask=order[2])
-        parts = [chunk, received, swap(chunk, mask=1), swap(received, mask=1)]
-        owners = [owner] + [[m ^ x for m in owner] for x in (order[2], 1, order[2] ^ 1)]
-        result.append((parts, owners))
+    for pair, order, places, members in zip(
+        halves, orders, swapped, (range(1), range(1, len(shards)))
+    ):
+        chunk = joined(*pair)
+        for step in (0, 1):
+            received = exchange(chunk, AXES, size, order[step])
+            chunk = joined(chunk, received)
+        received = exchange(chunk, AXES, size, order[2])
+        near = exchange(chunk, AXES, size, (1, 1))
+        far = exchange(received, AXES, size, (1, 1))
+        steps = [(bit, bit) for bit in lead] + order
+        start = 0
+        for k in members:
+            result.append(([chunk, received, near, far], start, steps, places))
+            start += lengths[k]
     return result
 
 
@@ -61,15 +65,12 @@
         rows, columns, inner, outer = weight.shape
         shards.append(jnp.transpose(weight, (0, 1, 3, 2)).reshape(rows * columns, outer, inner))
     bits = [1 << k for k in range(size.bit_length() - 1)][::-1][:-1]
-    if size == 2 << (len(bits)) and len(bits) >= 3 and shards[0].shape[1] % 8 == 0:
-        return gathered_by_doubling(shards, bits)
-    result = []
-    for shard in shards:
-        whole = lax.all_gather(shard, AXES, axis=1, tiled=True)
-        taps, outer, inner = whole.shape
-        blocks = jnp.transpose(whole.reshape(taps, outer // 8, 8, inner), (1, 0, 2, 3))
-        result.append(([blocks], None))
-    return result
+    paired = lax.axis_size("space") % 2 == 0
+    if paired and size == 2 << len(bits) and len(bits) > 3 and shards[0].shape[1] == 8:
+        return gathered_in_chains(shards, bits)
+    return [
+        ([lax.all_gather(shard, AXES, axis=1, tiled=True)], 0, None, None) for shard in shards
+    ]
 
 
 def halos(top, bottom):
@@ -81,7 +82,6 @@
 
 def statistics_of_all(own):
     size = lax.axis_size("space")
-    swap = functools.partial(exchange, axes="space", size=size)
     bits = [1 << k for k in range(size.bit_length() - 1)]
     if size != 1 << len(bits):
         return [lax.all_gather(own, "space")]
@@ -90,7 +90,7 @@
         some = bits[max(start, 0) : start + 2]
         whole = held[0] if len(held) == 1 else jnp.concatenate(held, axis=0)
         masks = some if len(some) == 1 else some + [some[0] | some[1]]
-        held = [whole] + [swap(whole, mask=m) for m in masks]
+        held = [whole] + [exchange(whole, "space", size, (m, m)) for m in masks]
     return held
 
 
@@ -102,6 +102,7 @@
         in_specs=in_specs or [VMEM] * len(ins),
         out_specs=out_specs or [VMEM] * len(outs),
         scratch_shapes=scratch,
+        compiler_params=pltpu.CompilerParams(vmem_limit_bytes=20 << 20),
         cost_estimate=pl.CostEstimate(flops=flops, bytes_accessed=moved, transcendentals=0),
     )(*ins)
 
@@ -175,32 +176,47 @@
     return call(spread_body, outs, list(levels) + [before, after], [], 8 * sum(o.size for o in outs))
 
 
-def conv_body(counts, owners, me_ref, *refs):
-    levels = len(counts)
+def lay_out(kernel, parts, start, steps, places, me, taps):
+    inner = kernel.shape[1] // taps
+    if steps is None:
+        for tap in range(taps):
+            kernel[:, tap * inner : (tap + 1) * inner] = parts[0][tap]
+        return
+    held, received, near, far = parts
+    block = held.shape[2]
+    core = me & 1
+    depth = len(steps)
+    first, second = places
+    for j in range(1 << depth):
+        flags = [(j >> k) & 1 for k in range(depth)]
+        even = sum(step[0] for step, flag in zip(steps, flags) if flag)
+        odd = sum(step[1] for step, flag in zip(steps, flags) if flag)
+        chip = (me ^ (even + core * (odd - even))) >> 1
+        other = list(flags)
+        other[first], other[second] = flags[second], flags[first]
+        place = sum(flag << k for k, flag in enumerate(other[:-1]))
+        mine = (received if flags[-1] else held)[j % (1 << (depth - 1)), start : start + taps]
+        theirs = (far if other[-1] else near)[place, start : start + taps]
+        mine, theirs = mine.astype(F32), theirs.astype(F32)
+        low, high = jnp.where(core == 0, mine, theirs), jnp.where(core == 0, theirs, mine)
+        both = jnp.concatenate([low, high], axis=1).astype(BF16)
+        row = pl.multiple_of(chip * (2 * block), 2 * block)
+        for tap in range(taps):
+            kernel[pl.ds(row, 2 * block), tap * inner : (tap + 1) * inner] = both[tap]
+
+
+def conv_body(counts, layouts, me_ref, *refs):
+    levels = len(layouts)
     refs = list(refs)
     xs, refs = refs[:levels], refs[levels:]
-    parts = []
-    for count in counts:
-        parts.append(refs[:count])
-        refs = refs[count:]
-    outs, stats, blocks, kernel = refs[:levels], refs[levels], refs[levels + 1], refs[levels + 2]
+    parts, refs = refs[:counts], refs[counts:]
+    outs, stats, kernels = refs[:levels], refs[levels], refs[levels + 1 :]
     me = me_ref[0]
-    taps, block_count, block, inner = blocks.shape
     for level in range(levels):
-        x, out = xs[level], outs[level]
-        base = 0
-        for k, part in enumerate(parts[level]):
-            for j in range(part.shape[0]):
-                if owners[level] is None:
-                    blocks[:, base + j] = part[j]
-                else:
-                    per = part.shape[2] // block
-                    owner = me ^ owners[level][k][j]
-                    for i in range(per):
-                        blocks[:, owner * per + i] = part[j, :, i * block : (i + 1) * block]
-            base += part.shape[0]
-        for tap in range(taps):
-            kernel[:, tap * inner : (tap + 1) * inner] = blocks[tap].reshape(block_count * block, inner)
+        x, out, kernel = xs[level], outs[level], kernels[level]
+        first, last, start, steps, places = layouts[level]
+        inner = x.shape[3] // 3
+        lay_out(kernel, parts[first:last], start, steps, places, me, kernel.shape[1] // inner)
         images, rows, width, outer = out.shape
         area = rows * width
         group = max(1, min(images, 512 // area))
@@ -226,23 +242,22 @@
                 )
 
 
-def convolve(me, xs, weights):
+def convolve(me, xs, weights, outer):
     inner = xs[0].shape[3] // 3
-    sample = weights[0][0][0]
-    outer = sum(p.shape[0] * p.shape[2] for p in weights[0][0])
     outs = [
         jax.ShapeDtypeStruct((x.shape[0], x.shape[1] - 2, x.shape[2], outer), F32) for x in xs
     ]
     flops = sum(2 * o.size * 9 * inner for o in outs)
     outs.append(jax.ShapeDtypeStruct((2 * xs[0].shape[0] * len(xs), outer), F32))
-    body = functools.partial(
-        conv_body, [len(w[0]) for w in weights], [w[1] for w in weights]
-    )
-    ins = [me] + list(xs) + [p for w in weights for p in w[0]]
-    scratch = [
-        pltpu.VMEM((sample.shape[1], outer // 8, 8, inner), BF16),
-        pltpu.VMEM((outer, sample.shape[1] * inner), BF16),
-    ]
+    arrays, layouts, before = [], [], None
+    for parts, start, steps, places in weights:
+        if parts is not before:
+            arrays.extend(parts)
+        before = parts
+        layouts.append((len(arrays) - len(parts), len(arrays), start, steps, places))
+    body = functools.partial(conv_body, len(arrays), layouts)
+    ins = [me] + list(xs) + arrays
+    scratch = [pltpu.VMEM((outer, 9 * inner), BF16) for _ in xs]
     specs = [pl.BlockSpec(memory_space=pltpu.SMEM)] + [VMEM] * (len(ins) - 1)
     result = call(body, outs, ins, scratch, flops, in_specs=specs)
     return result[:-1], result[-1]
@@ -310,14 +325,14 @@
 
 def local(l3, l4, l5, w3, w4, w5, gain3, shift3, gain4, shift4, gain5, shift5):
     weights = weight_parts([w3, w4, w5])
+    outer = shift3.shape[0]
     m3, m4, top, bottom = merge(l3, l4, l5)
     before, after = halos(top, bottom)
     x3, x4, x5 = spread((m3, m4, l5), before, after)
     me = lax.axis_index(AXES).astype(jnp.int32).reshape(1)
-    (f3,), stats3 = convolve(me, [x3], weights[:1])
-    (f4,), stats4 = convolve(me, [x4], weights[1:2])
-    (f5,), stats5 = convolve(me, [x5], weights[2:])
-    stats = statistics_of_all(jnp.concatenate([stats3, stats4, stats5], axis=0))
+    (f3,), stats3 = convolve(me, [x3], weights[:1], outer)
+    (f4, f5), stats45 = convolve(me, [x4, x5], weights[1:], outer)
+    stats = statistics_of_all(jnp.concatenate([stats3, stats45], axis=0))
     affine = [a[None] for a in (gain3, shift3, gain4, shift4, gain5, shift5)]
     return tuple(normalize([f3, f4, f5], affine, stats))
 

time: 82 us -> 70.2 us (0.86)
  Pallas kernels: 24.9 us -> 11.1 us
  starting transfers between devices: 23.2 us -> 24.4 us
    pallas_call x6 -> x5, Pallas kernels: 24.9 us -> 11.1 us  [call(): pl.pallas_call(body, out_shape=outs, in_specs=in_specs or [VMEM] * len(in...]
    ppermute x20 -> x15, starting transfers between devices: 20.6 us -> 21.8 us  [exchange(): lax.ppermute(array, axes, [(i, i ^ masks[i % 2]) for i in range(size)])]
    unnamed x30 -> x26, local copies, waits for them, and re-layouts: 2.04 us -> 2.79 us
    ppermute x20 -> x15, waiting for transfers between devices: 28.8 us -> 28.9 us  [exchange(): lax.ppermute(array, axes, [(i, i ^ masks[i % 2]) for i in range(size)])]
  transfers between devices with their start and end apart: 22 -> 17, of which waited for: 10 -> 9; matrix products, arithmetic and copies ran while one was open for 0% -> 1% of each run, Pallas kernels for 22% -> 11%
where the time goes in v2:
time: 70.2 us; the launch traced here: 69.9 us
  waiting for transfers between devices  28.9 us (41%)
  starting transfers between devices  24.4 us (35%)
  Pallas kernels  11.1 us (16%)
  local copies, waits for them, and re-layouts  2.81 us (4%)
  other arithmetic  1.83 us (3%)
  between operations  0.85 us (1%)
    ppermute x15, waiting for transfers between devices, exchange(): lax.ppermute(array, axes, [(i, i ^ masks[i % 2]) for i in range(size)])  28.9 us
    ppermute x15, starting transfers between devices, exchange(): lax.ppermute(array, axes, [(i, i ^ masks[i % 2]) for i in range(size)])  21.8 us
    pallas_call x5, Pallas kernels, call(): pl.pallas_call(body, out_shape=outs, in_specs=in_specs or [VMEM] * len(in...  11.1 us
    unnamed x26, local copies, waits for them, and re-layouts  2.79 us
  transfers between devices with their start and end apart: 17, of which 9 were waited for; matrix products, arithmetic and copies ran while one was open for 1% of the time, Pallas kernels for 11%

profile of v2, /device:TPU:0, one launch (start us, length us, event | category | flops | bytes accessed | tf_op | source)
XLA Modules:
  0.0 69.9 jit_solution(18034157902960968278)
XLA Ops:
  0.6 0.0 copy-start
  0.6 0.0 copy-start.5
  0.7 0.0 copy-start.6
  0.7 0.9 %maximum_bitcast_fusion = bf16[1,27,8,256]{3,2,1,0:T(8,128)(2,1)S(1)} fusion(bf16[9,8,256]{2,1,0:T(8,128)(2,1)} %bitcast.26, bf16[9,8,256]{2,1,0:T(8,128)(2,1)} %bitcast.27, bf16[9,8,256]{2,1,0:T(8,128)(2,1)} %bitcast.28), kind=kLoop, calls=%fused_computation.5 | loop fusion | flops 110592 | bytes 221184 | tf_op jit(solution)/shard_map/broadcast_in_dim | solution.py:33
  1.6 4.1 %collective-permute-start.2 = (bf16[1,27,8,256]{3,2,1,0:T(8,128)(2,1)S(1)}, bf16[1,27,8,256]{3,2,1,0:T(8,128)(2,1)S(1)}, u32[]{:S(2)}, u32[]{:S(2)}) collective-permute-start(bf16[1,27,8,256]{3,2,1,0:T(8,128)(2,1)S(1)} %maximum_bitcast_fusion), channel_id=1, source_target_pairs={{0,16},{1,17},{2,18},{3,19},{4,20},{5,21},{6,22},{7,23},{8,24},{9,... | collective-permute-start | bytes 331784 | tf_op jit(solution)/shard_map/ppermute | solution.py:22
  5.7 5.4 %collective-permute-done.2 = bf16[1,27,8,256]{3,2,1,0:T(8,128)(2,1)S(1)} collective-permute-done((bf16[1,27,8,256]{3,2,1,0:T(8,128)(2,1)S(1)}, bf16[1,27,8,256]{3,2,1,0:T(8,128)(2,1)S(1)}, u32[]{:S(2)}, u32[]{:S(2)}) %collective-permute-start.2) | collective-permute-done | bytes 110624 | tf_op jit(solution)/shard_map/ppermute | solution.py:22
  11.2 0.8 %collective-permute-start.8 = (bf16[2,18,8,256]{3,2,1,0:T(8,128)(2,1)S(1)}, bf16[2,18,8,256]{3,2,1,0:T(8,128)(2,1)S(1)}, u32[]{:S(2)}, u32[]{:S(2)}) collective-permute-start(bf16[2,18,8,256]{3,2,1,0:T(8,128)(2,1)S(1)} %pad_maximum_fusion.4), channel_id=1, source_target_pairs={{0,8},{1,9},{2,10},{3,11},{4,12},{5,13},{6,14},{7,15},{8,0},{9,1},... | collective-permute-start | bytes 442376 | tf_op jit(solution)/shard_map/ppermute | solution.py:22
  12.0 4.4 %collective-permute-done.8 = bf16[2,18,8,256]{3,2,1,0:T(8,128)(2,1)S(1)} collective-permute-done((bf16[2,18,8,256]{3,2,1,0:T(8,128)(2,1)S(1)}, bf16[2,18,8,256]{3,2,1,0:T(8,128)(2,1)S(1)}, u32[]{:S(2)}, u32[]{:S(2)}) %collective-permute-start.8) | collective-permute-done | bytes 147488 | tf_op jit(solution)/shard_map/ppermute | solution.py:22
  16.4 1.6 %collective-permute-start.9 = (bf16[4,18,8,256]{3,2,1,0:T(8,128)(2,1)S(1)}, bf16[4,18,8,256]{3,2,1,0:T(8,128)(2,1)S(1)}, u32[]{:S(2)}, u32[]{:S(2)}) collective-permute-start(bf16[4,18,8,256]{3,2,1,0:T(8,128)(2,1)S(1)} %pad_maximum_fusion.2), channel_id=1, source_target_pairs={{0,4},{1,3},{2,6},{3,1},{4,0},{5,7},{6,2},{7,5},{8,12},{9,11},{10,... | collective-permute-start | bytes 884744 | tf_op jit(solution)/shard_map/ppermute | solution.py:22
  18.1 0.5 collective-permute-start.3
  18.6 4.6 %collective-permute-done.9 = bf16[4,18,8,256]{3,2,1,0:T(8,128)(2,1)S(1)} collective-permute-done((bf16[4,18,8,256]{3,2,1,0:T(8,128)(2,1)S(1)}, bf16[4,18,8,256]{3,2,1,0:T(8,128)(2,1)S(1)}, u32[]{:S(2)}, u32[]{:S(2)}) %collective-permute-start.9) | collective-permute-done | bytes 294944 | tf_op jit(solution)/shard_map/ppermute | solution.py:22
  23.2 0.1 pad_maximum_fusion.refs_2_.refs_6_
  23.3 1.7 %collective-permute-start.10 = (bf16[8,18,8,256]{3,2,1,0:T(8,128)(2,1)S(1)}, bf16[8,18,8,256]{3,2,1,0:T(8,128)(2,1)S(1)}, u32[]{:S(2)}, u32[]{:S(2)}) collective-permute-start(bf16[8,18,8,256]{3,2,1,0:T(8,128)(2,1)S(1)} %pad_maximum_fusion.refs_2_.refs_6_), channel_id=1, source_target_pairs={{0,2},{1,5},{2,0},{3,7},{4,6},{5,1},{6,4},{7,3},{8,10},{9,13},{10,... | collective-permute-start | bytes 1769480 | tf_op jit(solution)/shard_map/ppermute | solution.py:22
  25.0 0.0 collective-permute-done.3
  25.0 1.5 %collective-permute-start.4 = (bf16[4,9,8,256]{3,2,1,0:T(8,128)(2,1)S(1)}, bf16[4,9,8,256]{3,2,1,0:T(8,128)(2,1)S(1)}, u32[]{:S(2)}, u32[]{:S(2)}) collective-permute-start(bf16[4,9,8,256]{3,2,1,0:T(8,128)(2,1)S(1)} %pad_maximum_fusion.3), channel_id=1, source_target_pairs={{0,2},{1,5},{2,0},{3,7},{4,6},{5,1},{6,4},{7,3},{8,10},{9,13},{10,... | collective-permute-start | bytes 442376 | tf_op jit(solution)/shard_map/ppermute | solution.py:22
  26.6 0.0 copy-done
  26.6 0.0 copy-done.5
  26.6 0.0 copy-done.6
  26.6 1.1 %shard_map.139 = (bf16[4,4,128,256]{3,2,1,0:T(8,128)(2,1)S(1)}, bf16[4,2,64,256]{3,2,1,0:T(8,128)(2,1)S(1)}, bf16[4,224,256]{2,1,0:T(8,128)(2,1)}, bf16[4,224,256]{2,1,0:T(8,128)(2,1)S(1)}) custom-call(bf16[4,4,128,256]{3,2,1,0:T(8,128)(2,1)S(1)} %copy-done, bf16[4,2,64,256]{3,2,1,0:T(8,128)(2,1)S(1)} %copy-done.5, bf16[4,1,32,256]{3,2,1,0:T(8,128)(2,1)S(1)} %copy-done.6), custom_call_target="tpu_custom_call" | custom-call | flops 2097152 | bytes 3604480 | tf_op jit(solution)/shard_map/pallas_call | solution.py:99
  27.7 1.3 %collective-permute-start = (bf16[4,224,256]{2,1,0:T(8,128)(2,1)S(1)}, bf16[4,224,256]{2,1,0:T(8,128)(2,1)S(1)}, u32[]{:S(2)}, u32[]{:S(2)}) collective-permute-start(bf16[4,224,256]{2,1,0:T(8,128)(2,1)S(1)} %get-tuple-element.17), channel_id=1, source_target_pairs={{0,1},{1,2},{2,3},{3,4},{4,5},{5,6},{6,7},{8,9},{9,10},{10,11},{11... | collective-permute-start | bytes 1376264 | tf_op jit(solution)/shard_map/ppermute | solution.py:78
  29.0 8.4 %collective-permute-done.4 = bf16[4,9,8,256]{3,2,1,0:T(8,128)(2,1)S(1)} collective-permute-done((bf16[4,9,8,256]{3,2,1,0:T(8,128)(2,1)S(1)}, bf16[4,9,8,256]{3,2,1,0:T(8,128)(2,1)S(1)}, u32[]{:S(2)}, u32[]{:S(2)}) %collective-permute-start.4) | collective-permute-done | bytes 147488 | tf_op jit(solution)/shard_map/ppermute | solution.py:22
  37.4 0.8 %pad_maximum_fusion.1.refs_1_ = bf16[8,9,8,256]{3,2,1,0:T(8,128)(2,1)} fusion(bf16[4,9,8,256]{3,2,1,0:T(8,128)(2,1)S(1)} %collective-permute-done.4, bf16[2,9,8,256]{3,2,1,0:T(8,128)(2,1)S(1)} %collective-permute-done.3, bf16[1,9,8,256]{3,2,1,0:T(8,128)(2,1)S(1)} %slice.17, bf16[1,9,8,256]{3,2,1,0:T(8,128)(2,1)S(1)} %slice.16), kind=kLoop, calls=%fused_computation.1 | loop fusion | flops 442368 | bytes 589824 | tf_op jit(solution)/shard_map/concatenate | solution.py:26
  38.1 1.2 %collective-permute-start.5 = (bf16[8,9,8,256]{3,2,1,0:T(8,128)(2,1)}, bf16[8,9,8,256]{3,2,1,0:T(8,128)(2,1)}, u32[]{:S(2)}, u32[]{:S(2)}) collective-permute-start(bf16[8,9,8,256]{3,2,1,0:T(8,128)(2,1)} %pad_maximum_fusion.1.refs_1_), channel_id=1, source_target_pairs={{0,8},{1,9},{2,10},{3,11},{4,12},{5,13},{6,14},{7,15},{8,0},{9,1},... | collective-permute-start | bytes 884744 | tf_op jit(solution)/shard_map/ppermute | solution.py:22
  39.3 0.0 copy-done.3
  39.3 1.3 %collective-permute-start.1 = (bf16[4,224,256]{2,1,0:T(8,128)(2,1)}, bf16[4,224,256]{2,1,0:T(8,128)(2,1)}, u32[]{:S(2)}, u32[]{:S(2)}) collective-permute-start(bf16[4,224,256]{2,1,0:T(8,128)(2,1)} %get-tuple-element.18), channel_id=1, source_target_pairs={{1,0},{2,1},{3,2},{4,3},{5,4},{6,5},{7,6},{9,8},{10,9},{11,10},{12... | collective-permute-start | bytes 1376264 | tf_op jit(solution)/shard_map/ppermute | solution.py:79
  40.6 1.2 %collective-permute-start.11 = (bf16[8,18,8,256]{3,2,1,0:T(8,128)(2,1)S(1)}, bf16[8,18,8,256]{3,2,1,0:T(8,128)(2,1)S(1)}, u32[]{:S(2)}, u32[]{:S(2)}) collective-permute-start(bf16[8,18,8,256]{3,2,1,0:T(8,128)(2,1)S(1)} %pad_maximum_fusion.refs_2_.refs_6_), channel_id=1, source_target_pairs={{0,1},{1,0},{2,3},{3,2},{4,5},{5,4},{6,7},{7,6},{8,9},{9,8},{10,11... | collective-permute-start | bytes 1769480 | tf_op jit(solution)/shard_map/ppermute | solution.py:22
  41.8 0.0 collective-permute-done.10.refs_3_.refs_7_
  41.8 0.1 collective-permute-start.12
  41.9 0.0 collective-permute-done.before
  41.9 0.8 %copy-done.1 = bf16[4,224,256]{2,1,0:T(8,128)(2,1)} copy-done((bf16[4,224,256]{2,1,0:T(8,128)(2,1)}, bf16[4,224,256]{2,1,0:T(8,128)(2,1)S(1)}, u32[]{:S(2)}) %copy-start.1) | copy-done | bytes 458776
  42.6 0.4 collective-permute-start.6
  43.0 2.1 %collective-permute-done.5.refs_2_ = bf16[8,9,8,256]{3,2,1,0:T(8,128)(2,1)} collective-permute-done((bf16[8,9,8,256]{3,2,1,0:T(8,128)(2,1)}, bf16[8,9,8,256]{3,2,1,0:T(8,128)(2,1)}, u32[]{:S(2)}, u32[]{:S(2)}) %collective-permute-start.5) | collective-permute-done | bytes 294944 | tf_op jit(solution)/shard_map/ppermute | solution.py:22
  45.2 0.0 collective-permute-start.7
  45.2 0.0 collective-permute-done.1.after
  45.2 1.0 %copy-done.2 = bf16[4,224,256]{2,1,0:T(8,128)(2,1)S(1)} copy-done((bf16[4,224,256]{2,1,0:T(8,128)(2,1)S(1)}, bf16[4,224,256]{2,1,0:T(8,128)(2,1)}, u32[]{:S(2)}) %copy-start.2) | copy-done | bytes 458776
  46.2 0.9 %copy-done.4 = bf16[4,2,64,256]{3,2,1,0:T(8,128)(2,1)S(1)} copy-done((bf16[4,2,64,256]{3,2,1,0:T(8,128)(2,1)S(1)}, bf16[4,2,64,256]{3,2,1,0:T(8,128)(2,1)}, u32[]{:S(2)}) %copy-start.4) | copy-done | bytes 262168
  47.1 2.0 %shard_map.140 = (bf16[4,6,128,768]{3,2,1,0:T(8,128)(2,1)S(1)}, bf16[4,4,64,768]{3,2,1,0:T(8,128)(2,1)S(1)}, bf16[4,3,32,768]{3,2,1,0:T(8,128)(2,1)S(1)}) custom-call(bf16[4,4,128,256]{3,2,1,0:T(8,128)(2,1)S(1)} %get-tuple-element.15.m3, bf16[4,2,64,256]{3,2,1,0:T(8,128)(2,1)S(1)} %copy-done.4, bf16[4,1,32,256]{3,2,1,0:T(8,128)(2,1)S(1)} %copy-done.6, ...), custom_call_target="tpu_custom_call" | custom-call | flops 27525120 | bytes 9175040 | tf_op jit(solution)/shard_map/pallas_call | solution.py:99
  49.1 0.0 collective-permute-done.6.refs_3_
  49.1 0.0 collective-permute-done.7.refs_4_
  49.1 4.3 %shard_map.141 = (f32[4,4,128,256]{3,2,1,0:T(8,128)S(1)}, f32[8,256]{1,0:T(8,128)S(1)}) custom-call(s32[1]{0:T(128)} %bitcast.me_ref, bf16[4,6,128,768]{3,2,1,0:T(8,128)(2,1)S(1)} %get-tuple-element.19.refs_0_, bf16[8,9,8,256]{3,2,1,0:T(8,128)(2,1)} %pad_maximum_fusion.1.refs_1_, bf16[8,9,8,256]{3,2,1,0:T(8,128)(2,1)} %collective-permute-done.5.refs_2_, ...), custom_call_target="tpu_custom_call" | custom-call | flops 2415919104 | bytes 8003588 | tf_op jit(solution)/shard_map/pallas_call | solution.py:99
  53.4 0.0 collective-permute-done.11.refs_4_.refs_8_
  53.4 0.0 collective-permute-done.12.refs_5_.refs_9_
  53.4 0.0 copy-start.7
  53.5 0.0 copy-start.8
  53.5 0.0 copy-start.9
  53.5 0.0 copy-start.10
  53.5 0.0 copy-start.11
  53.5 0.0 copy-start.12
  53.5 1.5 %shard_map.142 = (f32[4,2,64,256]{3,2,1,0:T(8,128)S(1)}, f32[4,1,32,256]{3,2,1,0:T(8,128)S(1)}, f32[16,256]{1,0:T(8,128)S(1)}) custom-call(s32[1]{0:T(128)} %bitcast.me_ref, bf16[4,4,64,768]{3,2,1,0:T(8,128)(2,1)S(1)} %get-tuple-element.21.refs_0_, bf16[4,3,32,768]{3,2,1,0:T(8,128)(2,1)S(1)} %get-tuple-element.22.refs_1_, ...), custom_call_target="tpu_custom_call" | custom-call | flops 754974720 | bytes 7553028 | tf_op jit(solution)/shard_map/pallas_call | solution.py:99
  55.0 5.1 %collective-permute-start.13 = (f32[1,24,256]{2,1,0:T(8,128)S(1)}, f32[1,24,256]{2,1,0:T(8,128)S(1)}, u32[]{:S(2)}, u32[]{:S(2)}) collective-permute-start(f32[1,24,256]{2,1,0:T(8,128)S(1)} %maximum_bitcast_fusion.1), channel_id=1, source_target_pairs={{0,1},{1,0},{2,3},{3,2},{4,5},{5,4},{6,7},{7,6},{8,9},{9,8},{10,11... | collective-permute-start | bytes 73736 | tf_op jit(solution)/shard_map/ppermute | solution.py:22
  60.2 0.8 %collective-permute-done.13 = f32[1,24,256]{2,1,0:T(8,128)S(1)} collective-permute-done((f32[1,24,256]{2,1,0:T(8,128)S(1)}, f32[1,24,256]{2,1,0:T(8,128)S(1)}, u32[]{:S(2)}, u32[]{:S(2)}) %collective-permute-start.13) | collective-permute-done | bytes 24608 | tf_op jit(solution)/shard_map/ppermute | solution.py:22
  61.1 0.5 collective-permute-start.14
  61.5 1.1 %collective-permute-start.15 = (f32[2,24,256]{2,1,0:T(8,128)S(1)}, f32[2,24,256]{2,1,0:T(8,128)S(1)}, u32[]{:S(2)}, u32[]{:S(2)}) collective-permute-start(f32[2,24,256]{2,1,0:T(8,128)S(1)} %pad_maximum_fusion.6.refs_9_), channel_id=1, source_target_pairs={{0,4},{1,5},{2,6},{3,7},{4,0},{5,1},{6,2},{7,3},{8,12},{9,13},{10,... | collective-permute-start | bytes 147464 | tf_op jit(solution)/shard_map/ppermute | solution.py:22
  62.6 1.9 %collective-permute-start.16 = (f32[2,24,256]{2,1,0:T(8,128)S(1)}, f32[2,24,256]{2,1,0:T(8,128)S(1)}, u32[]{:S(2)}, u32[]{:S(2)}) collective-permute-start(f32[2,24,256]{2,1,0:T(8,128)S(1)} %pad_maximum_fusion.6.refs_9_), channel_id=1, source_target_pairs={{0,6},{1,7},{2,4},{3,5},{4,2},{5,3},{6,0},{7,1},{8,14},{9,15},{10,... | collective-permute-start | bytes 147464 | tf_op jit(solution)/shard_map/ppermute | solution.py:22
  64.5 0.6 collective-permute-done.14.refs_10_
  65.1 0.5 collective-permute-done.15.refs_11_
  65.6 2.0 %collective-permute-done.16.refs_12_ = f32[2,24,256]{2,1,0:T(8,128)S(1)} collective-permute-done((f32[2,24,256]{2,1,0:T(8,128)S(1)}, f32[2,24,256]{2,1,0:T(8,128)S(1)}, u32[]{:S(2)}, u32[]{:S(2)}) %collective-permute-start.16) | collective-permute-done | bytes 49184 | tf_op jit(solution)/shard_map/ppermute | solution.py:22
  67.6 0.0 copy-done.7
  67.6 0.0 copy-done.8
  67.6 0.0 copy-done.9
  67.6 0.0 copy-done.10
  67.6 0.0 copy-done.11
  67.7 0.0 copy-done.12
  67.7 2.2 %shard_map.143 = (f32[4,4,128,256]{3,2,1,0:T(8,128)}, f32[4,2,64,256]{3,2,1,0:T(8,128)}, f32[4,1,32,256]{3,2,1,0:T(8,128)}) custom-call(f32[4,4,128,256]{3,2,1,0:T(8,128)S(1)} %get-tuple-element.20.refs_0_, f32[4,2,64,256]{3,2,1,0:T(8,128)S(1)} %get-tuple-element.23.refs_1_, f32[4,1,32,256]{3,2,1,0:T(8,128)S(1)} %get-tuple-element.24.refs_2_, ...), custom_call_target="tpu_custom_call" | custom-call | flops 5505024 | bytes 5707776 | tf_op jit(solution)/shard_map/pallas_call | solution.py:99
  (14 shorter events, 0.1 us)
Async XLA Ops:
  0.6 25.9 %copy-start = (bf16[4,4,128,256]{3,2,1,0:T(8,128)(2,1)S(1)}, bf16[4,4,128,256]{3,2,1,0:T(8,128)(2,1)}, u32[]{:S(2)}) copy-start(bf16[4,4,128,256]{3,2,1,0:T(8,128)(2,1)} %l3.1) | copy-start | bytes 3145732
  0.6 25.9 %copy-start.5 = (bf16[4,2,64,256]{3,2,1,0:T(8,128)(2,1)S(1)}, bf16[4,2,64,256]{3,2,1,0:T(8,128)(2,1)}, u32[]{:S(2)}) copy-start(bf16[4,2,64,256]{3,2,1,0:T(8,128)(2,1)} %l4.1) | copy-start | bytes 786436
  0.7 25.9 %copy-start.6 = (bf16[4,1,32,256]{3,2,1,0:T(8,128)(2,1)S(1)}, bf16[4,1,32,256]{3,2,1,0:T(8,128)(2,1)}, u32[]{:S(2)}) copy-start(bf16[4,1,32,256]{3,2,1,0:T(8,128)(2,1)} %l5.3) | copy-start | bytes 196612
  1.6 9.6 %collective-permute-start.2 = (bf16[1,27,8,256]{3,2,1,0:T(8,128)(2,1)S(1)}, bf16[1,27,8,256]{3,2,1,0:T(8,128)(2,1)S(1)}, u32[]{:S(2)}, u32[]{:S(2)}) collective-permute-start(bf16[1,27,8,256]{3,2,1,0:T(8,128)(2,1)S(1)} %maximum_bitcast_fusion), channel_id=1, source_target_pairs={{0,16},{1,17},{2,18},{3,19},{4,20},{5,21},{6,22},{7,23},{8,24},{9,... | collective-permute-start | bytes 331784 | tf_op jit(solution)/shard_map/ppermute | solution.py:22
  11.2 5.2 %collective-permute-start.8 = (bf16[2,18,8,256]{3,2,1,0:T(8,128)(2,1)S(1)}, bf16[2,18,8,256]{3,2,1,0:T(8,128)(2,1)S(1)}, u32[]{:S(2)}, u32[]{:S(2)}) collective-permute-start(bf16[2,18,8,256]{3,2,1,0:T(8,128)(2,1)S(1)} %pad_maximum_fusion.4), channel_id=1, source_target_pairs={{0,8},{1,9},{2,10},{3,11},{4,12},{5,13},{6,14},{7,15},{8,0},{9,1},... | collective-permute-start | bytes 442376 | tf_op jit(solution)/shard_map/ppermute | solution.py:22
  16.4 6.8 %collective-permute-start.9 = (bf16[4,18,8,256]{3,2,1,0:T(8,128)(2,1)S(1)}, bf16[4,18,8,256]{3,2,1,0:T(8,128)(2,1)S(1)}, u32[]{:S(2)}, u32[]{:S(2)}) collective-permute-start(bf16[4,18,8,256]{3,2,1,0:T(8,128)(2,1)S(1)} %pad_maximum_fusion.2), channel_id=1, source_target_pairs={{0,4},{1,3},{2,6},{3,1},{4,0},{5,7},{6,2},{7,5},{8,12},{9,11},{10,... | collective-permute-start | bytes 884744 | tf_op jit(solution)/shard_map/ppermute | solution.py:22
  18.1 6.9 %collective-permute-start.3 = (bf16[2,9,8,256]{3,2,1,0:T(8,128)(2,1)S(1)}, bf16[2,9,8,256]{3,2,1,0:T(8,128)(2,1)S(1)}, u32[]{:S(2)}, u32[]{:S(2)}) collective-permute-start(bf16[2,9,8,256]{3,2,1,0:T(8,128)(2,1)S(1)} %pad_maximum_fusion.5), channel_id=1, source_target_pairs={{0,4},{1,3},{2,6},{3,1},{4,0},{5,7},{6,2},{7,5},{8,12},{9,11},{10,... | collective-permute-start | bytes 221192 | tf_op jit(solution)/shard_map/ppermute | solution.py:22
  23.3 18.5 %collective-permute-start.10 = (bf16[8,18,8,256]{3,2,1,0:T(8,128)(2,1)S(1)}, bf16[8,18,8,256]{3,2,1,0:T(8,128)(2,1)S(1)}, u32[]{:S(2)}, u32[]{:S(2)}) collective-permute-start(bf16[8,18,8,256]{3,2,1,0:T(8,128)(2,1)S(1)} %pad_maximum_fusion.refs_2_.refs_6_), channel_id=1, source_target_pairs={{0,2},{1,5},{2,0},{3,7},{4,6},{5,1},{6,4},{7,3},{8,10},{9,13},{10,... | collective-permute-start | bytes 1769480 | tf_op jit(solution)/shard_map/ppermute | solution.py:22
  25.0 12.3 %collective-permute-start.4 = (bf16[4,9,8,256]{3,2,1,0:T(8,128)(2,1)S(1)}, bf16[4,9,8,256]{3,2,1,0:T(8,128)(2,1)S(1)}, u32[]{:S(2)}, u32[]{:S(2)}) collective-permute-start(bf16[4,9,8,256]{3,2,1,0:T(8,128)(2,1)S(1)} %pad_maximum_fusion.3), channel_id=1, source_target_pairs={{0,2},{1,5},{2,0},{3,7},{4,6},{5,1},{6,4},{7,3},{8,10},{9,13},{10,... | collective-permute-start | bytes 442376 | tf_op jit(solution)/shard_map/ppermute | solution.py:22
  27.7 11.6 %copy-start.3 = (bf16[4,2,64,256]{3,2,1,0:T(8,128)(2,1)}, bf16[4,2,64,256]{3,2,1,0:T(8,128)(2,1)S(1)}, u32[]{:S(2)}) copy-start(bf16[4,2,64,256]{3,2,1,0:T(8,128)(2,1)S(1)} %get-tuple-element.16.m4) | copy-start | bytes 786436
  27.7 14.2 %collective-permute-start = (bf16[4,224,256]{2,1,0:T(8,128)(2,1)S(1)}, bf16[4,224,256]{2,1,0:T(8,128)(2,1)S(1)}, u32[]{:S(2)}, u32[]{:S(2)}) collective-permute-start(bf16[4,224,256]{2,1,0:T(8,128)(2,1)S(1)} %get-tuple-element.17), channel_id=1, source_target_pairs={{0,1},{1,2},{2,3},{3,4},{4,5},{5,6},{6,7},{8,9},{9,10},{10,11},{11... | collective-permute-start | bytes 1376264 | tf_op jit(solution)/shard_map/ppermute | solution.py:78
  38.1 7.0 %collective-permute-start.5 = (bf16[8,9,8,256]{3,2,1,0:T(8,128)(2,1)}, bf16[8,9,8,256]{3,2,1,0:T(8,128)(2,1)}, u32[]{:S(2)}, u32[]{:S(2)}) collective-permute-start(bf16[8,9,8,256]{3,2,1,0:T(8,128)(2,1)} %pad_maximum_fusion.1.refs_1_), channel_id=1, source_target_pairs={{0,8},{1,9},{2,10},{3,11},{4,12},{5,13},{6,14},{7,15},{8,0},{9,1},... | collective-permute-start | bytes 884744 | tf_op jit(solution)/shard_map/ppermute | solution.py:22
  39.3 5.9 %collective-permute-start.1 = (bf16[4,224,256]{2,1,0:T(8,128)(2,1)}, bf16[4,224,256]{2,1,0:T(8,128)(2,1)}, u32[]{:S(2)}, u32[]{:S(2)}) collective-permute-start(bf16[4,224,256]{2,1,0:T(8,128)(2,1)} %get-tuple-element.18), channel_id=1, source_target_pairs={{1,0},{2,1},{3,2},{4,3},{5,4},{6,5},{7,6},{9,8},{10,9},{11,10},{12... | collective-permute-start | bytes 1376264 | tf_op jit(solution)/shard_map/ppermute | solution.py:79
  40.6 12.9 %collective-permute-start.11 = (bf16[8,18,8,256]{3,2,1,0:T(8,128)(2,1)S(1)}, bf16[8,18,8,256]{3,2,1,0:T(8,128)(2,1)S(1)}, u32[]{:S(2)}, u32[]{:S(2)}) collective-permute-start(bf16[8,18,8,256]{3,2,1,0:T(8,128)(2,1)S(1)} %pad_maximum_fusion.refs_2_.refs_6_), channel_id=1, source_target_pairs={{0,1},{1,0},{2,3},{3,2},{4,5},{5,4},{6,7},{7,6},{8,9},{9,8},{10,11... | collective-permute-start | bytes 1769480 | tf_op jit(solution)/shard_map/ppermute | solution.py:22
  41.8 11.7 %collective-permute-start.12 = (bf16[8,18,8,256]{3,2,1,0:T(8,128)(2,1)S(1)}, bf16[8,18,8,256]{3,2,1,0:T(8,128)(2,1)S(1)}, u32[]{:S(2)}, u32[]{:S(2)}) collective-permute-start(bf16[8,18,8,256]{3,2,1,0:T(8,128)(2,1)S(1)} %collective-permute-done.10.refs_3_.refs_7_), channel_id=1, source_target_pairs={{0,1},{1,0},{2,3},{3,2},{4,5},{5,4},{6,7},{7,6},{8,9},{9,8},{10,11... | collective-permute-start | bytes 1769480 | tf_op jit(solution)/shard_map/ppermute | solution.py:22
  41.9 0.8 %copy-start.1 = (bf16[4,224,256]{2,1,0:T(8,128)(2,1)}, bf16[4,224,256]{2,1,0:T(8,128)(2,1)S(1)}, u32[]{:S(2)}) copy-start(bf16[4,224,256]{2,1,0:T(8,128)(2,1)S(1)} %collective-permute-done.before) | copy-start | bytes 1376260
  42.6 6.5 %collective-permute-start.6 = (bf16[8,9,8,256]{3,2,1,0:T(8,128)(2,1)}, bf16[8,9,8,256]{3,2,1,0:T(8,128)(2,1)}, u32[]{:S(2)}, u32[]{:S(2)}) collective-permute-start(bf16[8,9,8,256]{3,2,1,0:T(8,128)(2,1)} %pad_maximum_fusion.1.refs_1_), channel_id=1, source_target_pairs={{0,1},{1,0},{2,3},{3,2},{4,5},{5,4},{6,7},{7,6},{8,9},{9,8},{10,11... | collective-permute-start | bytes 884744 | tf_op jit(solution)/shard_map/ppermute | solution.py:22
  45.2 3.9 %collective-permute-start.7 = (bf16[8,9,8,256]{3,2,1,0:T(8,128)(2,1)}, bf16[8,9,8,256]{3,2,1,0:T(8,128)(2,1)}, u32[]{:S(2)}, u32[]{:S(2)}) collective-permute-start(bf16[8,9,8,256]{3,2,1,0:T(8,128)(2,1)} %collective-permute-done.5.refs_2_), channel_id=1, source_target_pairs={{0,1},{1,0},{2,3},{3,2},{4,5},{5,4},{6,7},{7,6},{8,9},{9,8},{10,11... | collective-permute-start | bytes 884744 | tf_op jit(solution)/shard_map/ppermute | solution.py:22
  45.2 1.0 %copy-start.2 = (bf16[4,224,256]{2,1,0:T(8,128)(2,1)S(1)}, bf16[4,224,256]{2,1,0:T(8,128)(2,1)}, u32[]{:S(2)}) copy-start(bf16[4,224,256]{2,1,0:T(8,128)(2,1)} %copy-done.1) | copy-start | bytes 1376260
  46.2 0.9 %copy-start.4 = (bf16[4,2,64,256]{3,2,1,0:T(8,128)(2,1)S(1)}, bf16[4,2,64,256]{3,2,1,0:T(8,128)(2,1)}, u32[]{:S(2)}) copy-start(bf16[4,2,64,256]{3,2,1,0:T(8,128)(2,1)} %copy-done.3) | copy-start | bytes 786436
  53.4 14.2 %copy-start.7 = (f32[256]{0:T(256)S(1)}, f32[256]{0:T(256)}, u32[]{:S(2)}) copy-start(f32[256]{0:T(256)} %param.18) | copy-start | bytes 3076
  53.5 14.2 %copy-start.8 = (f32[256]{0:T(256)S(1)}, f32[256]{0:T(256)}, u32[]{:S(2)}) copy-start(f32[256]{0:T(256)} %param.19) | copy-start | bytes 3076
  53.5 14.2 %copy-start.9 = (f32[256]{0:T(256)S(1)}, f32[256]{0:T(256)}, u32[]{:S(2)}) copy-start(f32[256]{0:T(256)} %param.20) | copy-start | bytes 3076
  53.5 14.2 %copy-start.10 = (f32[256]{0:T(256)S(1)}, f32[256]{0:T(256)}, u32[]{:S(2)}) copy-start(f32[256]{0:T(256)} %param.21) | copy-start | bytes 3076
  53.5 14.2 %copy-start.11 = (f32[256]{0:T(256)S(1)}, f32[256]{0:T(256)}, u32[]{:S(2)}) copy-start(f32[256]{0:T(256)} %param.22) | copy-start | bytes 3076
  53.5 14.2 %copy-start.12 = (f32[256]{0:T(256)S(1)}, f32[256]{0:T(256)}, u32[]{:S(2)}) copy-start(f32[256]{0:T(256)} %param.23) | copy-start | bytes 3076
  55.0 6.0 %collective-permute-start.13 = (f32[1,24,256]{2,1,0:T(8,128)S(1)}, f32[1,24,256]{2,1,0:T(8,128)S(1)}, u32[]{:S(2)}, u32[]{:S(2)}) collective-permute-start(f32[1,24,256]{2,1,0:T(8,128)S(1)} %maximum_bitcast_fusion.1), channel_id=1, source_target_pairs={{0,1},{1,0},{2,3},{3,2},{4,5},{5,4},{6,7},{7,6},{8,9},{9,8},{10,11... | collective-permute-start | bytes 73736 | tf_op jit(solution)/shard_map/ppermute | solution.py:22
  61.1 4.1 %collective-permute-start.14 = (f32[2,24,256]{2,1,0:T(8,128)S(1)}, f32[2,24,256]{2,1,0:T(8,128)S(1)}, u32[]{:S(2)}, u32[]{:S(2)}) collective-permute-start(f32[2,24,256]{2,1,0:T(8,128)S(1)} %pad_maximum_fusion.6.refs_9_), channel_id=1, source_target_pairs={{0,2},{1,3},{2,0},{3,1},{4,6},{5,7},{6,4},{7,5},{8,10},{9,11},{10,... | collective-permute-start | bytes 147464 | tf_op jit(solution)/shard_map/ppermute | solution.py:22
  61.5 4.1 %collective-permute-start.15 = (f32[2,24,256]{2,1,0:T(8,128)S(1)}, f32[2,24,256]{2,1,0:T(8,128)S(1)}, u32[]{:S(2)}, u32[]{:S(2)}) collective-permute-start(f32[2,24,256]{2,1,0:T(8,128)S(1)} %pad_maximum_fusion.6.refs_9_), channel_id=1, source_target_pairs={{0,4},{1,5},{2,6},{3,7},{4,0},{5,1},{6,2},{7,3},{8,12},{9,13},{10,... | collective-permute-start | bytes 147464 | tf_op jit(solution)/shard_map/ppermute | solution.py:22
  62.6 5.0 %collective-permute-start.16 = (f32[2,24,256]{2,1,0:T(8,128)S(1)}, f32[2,24,256]{2,1,0:T(8,128)S(1)}, u32[]{:S(2)}, u32[]{:S(2)}) collective-permute-start(f32[2,24,256]{2,1,0:T(8,128)S(1)} %pad_maximum_fusion.6.refs_9_), channel_id=1, source_target_pairs={{0,6},{1,7},{2,4},{3,5},{4,2},{5,3},{6,0},{7,1},{8,14},{9,15},{10,... | collective-permute-start | bytes 147464 | tf_op jit(solution)/shard_map/ppermute | solution.py:22

commit v3 on v2

--- a/solution.py
+++ b/solution.py
@@ -22,28 +22,49 @@
     return lax.ppermute(array, axes, [(i, i ^ masks[i % 2]) for i in range(size)])
 
 
-def joined(first, second):
-    return jnp.concatenate([first, second], axis=0)
-
-
-def gathered_in_chains(shards, bits):
+def join_body(*refs):
+    target, start = refs[-1], 0
+    for ref in refs[:-1]:
+        target[start : start + ref.shape[0]] = ref[...]
+        start += ref.shape[0]
+
+
+def joined(*arrays):
+    count = sum(a.shape[0] for a in arrays)
+    out = jax.ShapeDtypeStruct((count,) + arrays[0].shape[1:], arrays[0].dtype)
+    return call(join_body, [out], list(arrays), [], out.size, room=1)[0]
+
+
+def halve_body(cut, first, second, *targets):
+    for target, lo, hi in ((targets[0], 0, cut), (targets[1], cut, first.shape[1])):
+        count = first.shape[0]
+        target[:count] = first[:, lo:hi]
+        target[count:] = second[:, lo:hi]
+
+
+def halved(first, second, cut):
+    count, length = first.shape[:2]
+    outs = [
+        jax.ShapeDtypeStruct((2 * count, n) + first.shape[2:], first.dtype)
+        for n in (cut, length - cut)
+    ]
+    return call(functools.partial(halve_body, cut), outs, [first, second], [], 2 * first.size, room=1)
+
+
+def gathered_in_chains(together, lengths, bits):
     size = lax.axis_size(AXES)
     lead, (p, q, r) = bits[:-3], bits[-3:]
-    lengths = [s.shape[0] for s in shards]
-    together = jnp.concatenate(shards, axis=0)[None]
     for k, bit in enumerate(lead):
         received = exchange(together, AXES, size, (bit, bit))
         if k + 1 < len(lead):
             together = joined(together, received)
-    cut = lengths[0]
-    halves = [(together[:, :cut], received[:, :cut]), (together[:, cut:], received[:, cut:])]
+    chunks = halved(together, received, lengths[0])
     orders = [[(q, r), (r, q), (p, p)], [(p, p), (q, r), (r, q)]]
     swapped = [(len(lead), len(lead) + 1), (len(lead) + 1, len(lead) + 2)]
     result = []
-    for pair, order, places, members in zip(
-        halves, orders, swapped, (range(1), range(1, len(shards)))
+    for chunk, order, places, members in zip(
+        chunks, orders, swapped, (range(1), range(1, len(lengths)))
     ):
-        chunk = joined(*pair)
         for step in (0, 1):
             received = exchange(chunk, AXES, size, order[step])
             chunk = joined(chunk, received)
@@ -67,16 +88,28 @@
     bits = [1 << k for k in range(size.bit_length() - 1)][::-1][:-1]
     paired = lax.axis_size("space") % 2 == 0
     if paired and size == 2 << len(bits) and len(bits) > 3 and shards[0].shape[1] == 8:
-        return gathered_in_chains(shards, bits)
+        together = jnp.concatenate(shards, axis=0)[None]
+        return gathered_in_chains(together, [s.shape[0] for s in shards], bits)
     return [
         ([lax.all_gather(shard, AXES, axis=1, tiled=True)], 0, None, None) for shard in shards
     ]
 
 
-def halos(top, bottom):
+def starts_of(*levels):
+    starts, start = [], 0
+    for level in levels:
+        starts.append(start)
+        start += level.shape[2]
+    return starts
+
+
+def halos(*levels):
     count = lax.axis_size("space")
-    before = lax.ppermute(bottom, "space", [(i, i + 1) for i in range(count - 1)])
-    after = lax.ppermute(top, "space", [(i + 1, i) for i in range(count - 1)])
+    ahead = [(i, i + 1) for i in range(count - 1)]
+    top = jnp.concatenate([a[:, 0] for a in levels], axis=1)
+    bottom = jnp.concatenate([a[:, -1] for a in levels], axis=1)
+    before = lax.ppermute(bottom, "space", ahead)
+    after = lax.ppermute(top, "space", [(j, i) for i, j in ahead])
     return before, after
 
 
@@ -88,13 +121,13 @@
     held = [own[None]]
     for start in range(0, len(bits), 2) if len(bits) % 2 == 0 else [-1] + list(range(1, len(bits), 2)):
         some = bits[max(start, 0) : start + 2]
-        whole = held[0] if len(held) == 1 else jnp.concatenate(held, axis=0)
+        whole = held[0] if len(held) == 1 else joined(*held)
         masks = some if len(some) == 1 else some + [some[0] | some[1]]
         held = [whole] + [exchange(whole, "space", size, (m, m)) for m in masks]
     return held
 
 
-def call(body, outs, ins, scratch, flops, in_specs=None, out_specs=None):
+def call(body, outs, ins, scratch, flops, in_specs=None, out_specs=None, room=8):
     moved = sum(a.size * a.dtype.itemsize for a in list(outs) + list(ins))
     return pl.pallas_call(
         body,
@@ -102,7 +135,7 @@
         in_specs=in_specs or [VMEM] * len(ins),
         out_specs=out_specs or [VMEM] * len(outs),
         scratch_shapes=scratch,
-        compiler_params=pltpu.CompilerParams(vmem_limit_bytes=20 << 20),
+        compiler_params=pltpu.CompilerParams(vmem_limit_bytes=room << 20),
         cost_estimate=pl.CostEstimate(flops=flops, bytes_accessed=moved, transcendentals=0),
     )(*ins)
 
@@ -118,62 +151,53 @@
     return jnp.concatenate(pieces, axis=1)
 
 
-def merge_body(l3, l4, l5, m3, m4, top, bottom, fine, middle):
+def prepare_body(l3, l4, l5, before, after, x3, x4, x5, fine, middle):
     images, rows5 = l5.shape[0], l5.shape[1]
+    channels = l5.shape[3]
+
+    def put(target, b, row, wide):
+        width = wide.shape[0]
+        column = lax.broadcasted_iota(jnp.int32, wide.shape, 0)
+        left = jnp.where(column == 0, 0.0, pltpu.roll(wide, 1, 0))
+        right = jnp.where(column == width - 1, 0.0, pltpu.roll(wide, width - 1, 0))
+        for k, piece in enumerate((left, wide, right)):
+            target[b, row, :, k * channels : (k + 1) * channels] = piece.astype(BF16)
+
+    def rounded(values):
+        return values.astype(BF16).astype(F32)
+
+    starts = starts_of(l3, l4, l5)
     for b in range(images):
+        for side, halo in enumerate((before, after)):
+            rows = []
+            for source, start in zip((l3, l4, l5), starts):
+                rows.append(halo[b, start : start + source.shape[2]].astype(F32))
+            put(x5, b, side * (x5.shape[1] - 1), rows[2])
+            v4 = rounded(rows[1] + stretched(middle, rows[2]))
+            put(x4, b, side * (x4.shape[1] - 1), v4)
+            put(x3, b, side * (x3.shape[1] - 1), rounded(rows[0] + stretched(fine, v4)))
         for r5 in range(rows5):
-            up5 = stretched(middle, l5[b, r5].astype(F32))
+            v5 = l5[b, r5].astype(F32)
+            put(x5, b, 1 + r5, v5)
+            up5 = stretched(middle, v5)
             for r4 in (2 * r5, 2 * r5 + 1):
-                v4 = (l4[b, r4].astype(F32) + up5).astype(BF16)
-                m4[b, r4] = v4
-                up4 = stretched(fine, v4.astype(F32))
+                v4 = rounded(l4[b, r4].astype(F32) + up5)
+                put(x4, b, 1 + r4, v4)
+                up4 = stretched(fine, v4)
                 for r3 in (2 * r4, 2 * r4 + 1):
-                    m3[b, r3] = (l3[b, r3].astype(F32) + up4).astype(BF16)
-        start = 0
-        for source in (m3, m4, l5):
-            width = source.shape[2]
-            top[b, start : start + width] = source[b, 0]
-            bottom[b, start : start + width] = source[b, source.shape[1] - 1]
-            start += width
-
-
-def merge(l3, l4, l5):
-    images, _, width3, channels = l3.shape
-    width = width3 + l4.shape[2] + l5.shape[2]
-    edge = jax.ShapeDtypeStruct((images, width, channels), BF16)
-    outs = [jax.ShapeDtypeStruct(l3.shape, BF16), jax.ShapeDtypeStruct(l4.shape, BF16), edge, edge]
-    scratch = [pltpu.VMEM((channels // LANES, w, LANES), F32) for w in (width3, l4.shape[2])]
-    return call(merge_body, outs, [l3, l4, l5], scratch, 4 * l3.size)
-
-
-def spread_body(m3, m4, l5, before, after, x3, x4, x5):
-    start = 0
-    for source, target in ((m3, x3), (m4, x4), (l5, x5)):
-        images, rows, width, channels = source.shape
-        place = lax.broadcasted_iota(jnp.int32, (width, channels), 0)
-        for r in range(rows + 2):
-            for b in range(images):
-                if r == 0:
-                    middle = before[b, start : start + width]
-                elif r == rows + 1:
-                    middle = after[b, start : start + width]
-                else:
-                    middle = source[b, r - 1]
-                wide = middle.astype(F32)
-                left = jnp.where(place == 0, 0.0, pltpu.roll(wide, 1, 0))
-                right = jnp.where(place == width - 1, 0.0, pltpu.roll(wide, width - 1, 0))
-                target[b, r, :, 0:channels] = left.astype(BF16)
-                target[b, r, :, channels : 2 * channels] = middle
-                target[b, r, :, 2 * channels : 3 * channels] = right.astype(BF16)
-        start += width
-
-
-def spread(levels, before, after):
+                    put(x3, b, 1 + r3, rounded(l3[b, r3].astype(F32) + up4))
+
+
+def prepare(l3, l4, l5, before, after):
+    levels = (l3, l4, l5)
+    channels = l3.shape[3]
     outs = [
-        jax.ShapeDtypeStruct((a.shape[0], a.shape[1] + 2, a.shape[2], 3 * a.shape[3]), BF16)
+        jax.ShapeDtypeStruct((a.shape[0], a.shape[1] + 2, a.shape[2], 3 * channels), BF16)
         for a in levels
     ]
-    return call(spread_body, outs, list(levels) + [before, after], [], 8 * sum(o.size for o in outs))
+    scratch = [pltpu.VMEM((channels // LANES, a.shape[2], LANES), F32) for a in (l3, l4)]
+    ins = [l3, l4, l5, before, after]
+    return call(prepare_body, outs, ins, scratch, 8 * sum(o.size for o in outs), room=2)
 
 
 def lay_out(kernel, parts, start, steps, places, me, taps):
@@ -205,13 +229,13 @@
             kernel[pl.ds(row, 2 * block), tap * inner : (tap + 1) * inner] = both[tap]
 
 
-def conv_body(counts, layouts, me_ref, *refs):
+def conv_body(counts, layouts, *refs):
     levels = len(layouts)
     refs = list(refs)
     xs, refs = refs[:levels], refs[levels:]
     parts, refs = refs[:counts], refs[counts:]
     outs, stats, kernels = refs[:levels], refs[levels], refs[levels + 1 :]
-    me = me_ref[0]
+    me = lax.axis_index("dp") * lax.axis_size("space") + lax.axis_index("space")
     for level in range(levels):
         x, out, kernel = xs[level], outs[level], kernels[level]
         first, last, start, steps, places = layouts[level]
@@ -242,7 +266,7 @@
                 )
 
 
-def convolve(me, xs, weights, outer):
+def convolve(xs, weights, outer):
     inner = xs[0].shape[3] // 3
     outs = [
         jax.ShapeDtypeStruct((x.shape[0], x.shape[1] - 2, x.shape[2], outer), F32) for x in xs
@@ -256,10 +280,9 @@
         before = parts
         layouts.append((len(arrays) - len(parts), len(arrays), start, steps, places))
     body = functools.partial(conv_body, len(arrays), layouts)
-    ins = [me] + list(xs) + arrays
+    ins = list(xs) + arrays
     scratch = [pltpu.VMEM((outer, 9 * inner), BF16) for _ in xs]
-    specs = [pl.BlockSpec(memory_space=pltpu.SMEM)] + [VMEM] * (len(ins) - 1)
-    result = call(body, outs, ins, scratch, flops, in_specs=specs)
+    result = call(body, outs, ins, scratch, flops)
     return result[:-1], result[-1]
 
 
@@ -326,13 +349,11 @@
 def local(l3, l4, l5, w3, w4, w5, gain3, shift3, gain4, shift4, gain5, shift5):
     weights = weight_parts([w3, w4, w5])
     outer = shift3.shape[0]
-    m3, m4, top, bottom = merge(l3, l4, l5)
-    before, after = halos(top, bottom)
-    x3, x4, x5 = spread((m3, m4, l5), before, after)
-    me = lax.axis_index(AXES).astype(jnp.int32).reshape(1)
-    (f3,), stats3 = convolve(me, [x3], weights[:1], outer)
-    (f4, f5), stats45 = convolve(me, [x4, x5], weights[1:], outer)
-    stats = statistics_of_all(jnp.concatenate([stats3, stats45], axis=0))
+    before, after = halos(l3, l4, l5)
+    x3, x4, x5 = prepare(l3, l4, l5, before, after)
+    (f3,), stats3 = convolve([x3], weights[:1], outer)
+    (f4, f5), stats45 = convolve([x4, x5], weights[1:], outer)
+    stats = statistics_of_all(joined(stats3, stats45))
     affine = [a[None] for a in (gain3, shift3, gain4, shift4, gain5, shift5)]
     return tuple(normalize([f3, f4, f5], affine, stats))
 

time: 70.2 us -> 66.9 us (0.953)
  Pallas kernels: 11.1 us -> 8.47 us
  waiting for transfers between devices: 28.9 us -> 30.9 us
  local copies, waits for them, and re-layouts: 2.81 us -> 1.13 us
  other arithmetic: 1.83 us -> 0.92 us
    unnamed x26 -> x18, local copies, waits for them, and re-layouts: 2.79 us -> 0.05 us
    pallas_call x5 -> x11, Pallas kernels: 11.1 us -> 8.47 us  [call(): pl.pallas_call(body, out_shape=outs, in_specs=in_specs or [VMEM] * len(in...]
    ppermute x15, waiting for transfers between devices: 28.9 us -> 30.9 us  [exchange(): lax.ppermute(array, axes, [(i, i ^ masks[i % 2]) for i in range(size)])]
    squeeze x0 -> x2, local copies, waits for them, and re-layouts: none -> 1.08 us  [halos(): top = jnp.concatenate([a[:, 0] for a in levels], axis=1)]
    concatenate x7 -> x1, other arithmetic: 0.9 us -> 0.06 us  [halos(): top = jnp.concatenate([a[:, 0] for a in levels], axis=1)]
  transfers between devices with their start and end apart: 17 -> 17, of which waited for: 9 -> 11; matrix products, arithmetic and copies ran while one was open for 1% -> 2% of each run, Pallas kernels for 11% -> 7%
where the time goes in v3:
time: 66.9 us; the launch traced here: 66.7 us
  waiting for transfers between devices  30.9 us (46%)
  starting transfers between devices  24.5 us (37%)
  Pallas kernels  8.47 us (13%)
  local copies, waits for them, and re-layouts  1.13 us (2%)
  other arithmetic  0.92 us (1%)
  between operations  0.84 us (1%)
    ppermute x15, waiting for transfers between devices, exchange(): lax.ppermute(array, axes, [(i, i ^ masks[i % 2]) for i in range(size)])  30.9 us
    ppermute x15, starting transfers between devices, exchange(): lax.ppermute(array, axes, [(i, i ^ masks[i % 2]) for i in range(size)])  21.9 us
    pallas_call x11, Pallas kernels, call(): pl.pallas_call(body, out_shape=outs, in_specs=in_specs or [VMEM] * len(in...  8.47 us
  transfers between devices with their start and end apart: 17, of which 11 were waited for; matrix products, arithmetic and copies ran while one was open for 2% of the time, Pallas kernels for 7%

profile of v3, /device:TPU:0, one launch (start us, length us, event | category | flops | bytes accessed | tf_op | source)
XLA Modules:
  0.0 66.7 jit_solution(2618704839484358040)
XLA Ops:
  0.6 0.0 copy-start.1
  0.6 0.0 copy-start.2
  0.7 0.9 %maximum_bitcast_fusion.first = bf16[1,27,8,256]{3,2,1,0:T(8,128)(2,1)S(1)} fusion(bf16[9,8,256]{2,1,0:T(8,128)(2,1)} %bitcast.44, bf16[9,8,256]{2,1,0:T(8,128)(2,1)} %bitcast.45, bf16[9,8,256]{2,1,0:T(8,128)(2,1)} %bitcast.46), kind=kLoop, calls=%fused_computation.6 | loop fusion | flops 110592 | bytes 221184 | tf_op jit(solution)/shard_map/broadcast_in_dim | solution.py:91
  1.5 4.1 %collective-permute-start.2 = (bf16[1,27,8,256]{3,2,1,0:T(8,128)(2,1)S(1)}, bf16[1,27,8,256]{3,2,1,0:T(8,128)(2,1)S(1)}, u32[]{:S(2)}, u32[]{:S(2)}) collective-permute-start(bf16[1,27,8,256]{3,2,1,0:T(8,128)(2,1)S(1)} %maximum_bitcast_fusion.first), channel_id=1, source_target_pairs={{0,16},{1,17},{2,18},{3,19},{4,20},{5,21},{6,22},{7,23},{8,24},{9,... | collective-permute-start | bytes 331784 | tf_op jit(solution)/shard_map/ppermute | solution.py:22
  5.6 5.4 %collective-permute-done.2.second = bf16[1,27,8,256]{3,2,1,0:T(8,128)(2,1)S(1)} collective-permute-done((bf16[1,27,8,256]{3,2,1,0:T(8,128)(2,1)S(1)}, bf16[1,27,8,256]{3,2,1,0:T(8,128)(2,1)S(1)}, u32[]{:S(2)}, u32[]{:S(2)}) %collective-permute-start.2) | collective-permute-done | bytes 110624 | tf_op jit(solution)/shard_map/ppermute | solution.py:22
  11.1 0.8 %collective-permute-start.8 = (bf16[2,18,8,256]{3,2,1,0:T(8,128)(2,1)S(1)}, bf16[2,18,8,256]{3,2,1,0:T(8,128)(2,1)S(1)}, u32[]{:S(2)}, u32[]{:S(2)}) collective-permute-start(bf16[2,18,8,256]{3,2,1,0:T(8,128)(2,1)S(1)} %get-tuple-element.18.refs_0_), channel_id=1, source_target_pairs={{0,8},{1,9},{2,10},{3,11},{4,12},{5,13},{6,14},{7,15},{8,0},{9,1},... | collective-permute-start | bytes 442376 | tf_op jit(solution)/shard_map/ppermute | solution.py:22
  11.9 4.4 %collective-permute-done.8.refs_1_ = bf16[2,18,8,256]{3,2,1,0:T(8,128)(2,1)S(1)} collective-permute-done((bf16[2,18,8,256]{3,2,1,0:T(8,128)(2,1)S(1)}, bf16[2,18,8,256]{3,2,1,0:T(8,128)(2,1)S(1)}, u32[]{:S(2)}, u32[]{:S(2)}) %collective-permute-start.8) | collective-permute-done | bytes 147488 | tf_op jit(solution)/shard_map/ppermute | solution.py:22
  16.3 1.6 %collective-permute-start.9 = (bf16[4,18,8,256]{3,2,1,0:T(8,128)(2,1)S(1)}, bf16[4,18,8,256]{3,2,1,0:T(8,128)(2,1)S(1)}, u32[]{:S(2)}, u32[]{:S(2)}) collective-permute-start(bf16[4,18,8,256]{3,2,1,0:T(8,128)(2,1)S(1)} %shard_map.144.refs_0_), channel_id=1, source_target_pairs={{0,4},{1,3},{2,6},{3,1},{4,0},{5,7},{6,2},{7,5},{8,12},{9,11},{10,... | collective-permute-start | bytes 884744 | tf_op jit(solution)/shard_map/ppermute | solution.py:22
  18.0 1.1 %slice_bitcast_fusion = (bf16[4,128,256]{2,1,0:T(8,128)(2,1)S(1)}, bf16[4,128,256]{2,1,0:T(8,128)(2,1)S(1)}) fusion(bf16[4,4,128,256]{3,2,1,0:T(8,128)(2,1)} %l3.1), kind=kLoop, calls=%fused_computation.2 | loop fusion | bytes 1048576 | tf_op jit(solution)/shard_map/squeeze | solution.py:109
  19.0 0.0 copy-start
  19.0 4.1 %collective-permute-done.9.refs_1_ = bf16[4,18,8,256]{3,2,1,0:T(8,128)(2,1)S(1)} collective-permute-done((bf16[4,18,8,256]{3,2,1,0:T(8,128)(2,1)S(1)}, bf16[4,18,8,256]{3,2,1,0:T(8,128)(2,1)S(1)}, u32[]{:S(2)}, u32[]{:S(2)}) %collective-permute-start.9) | collective-permute-done | bytes 294944 | tf_op jit(solution)/shard_map/ppermute | solution.py:22
  23.2 1.7 %collective-permute-start.10 = (bf16[8,18,8,256]{3,2,1,0:T(8,128)(2,1)S(1)}, bf16[8,18,8,256]{3,2,1,0:T(8,128)(2,1)S(1)}, u32[]{:S(2)}, u32[]{:S(2)}) collective-permute-start(bf16[8,18,8,256]{3,2,1,0:T(8,128)(2,1)S(1)} %shard_map.145.refs_2_.refs_6_), channel_id=1, source_target_pairs={{0,2},{1,5},{2,0},{3,7},{4,6},{5,1},{6,4},{7,3},{8,10},{9,13},{10,... | collective-permute-start | bytes 1769480 | tf_op jit(solution)/shard_map/ppermute | solution.py:22
  24.9 0.0 copy-done.1
  25.0 1.6 %collective-permute-start.3 = (bf16[2,9,8,256]{3,2,1,0:T(8,128)(2,1)S(1)}, bf16[2,9,8,256]{3,2,1,0:T(8,128)(2,1)S(1)}, u32[]{:S(2)}, u32[]{:S(2)}) collective-permute-start(bf16[2,9,8,256]{3,2,1,0:T(8,128)(2,1)S(1)} %get-tuple-element.14.refs_0_), channel_id=1, source_target_pairs={{0,4},{1,3},{2,6},{3,1},{4,0},{5,7},{6,2},{7,5},{8,12},{9,11},{10,... | collective-permute-start | bytes 221192 | tf_op jit(solution)/shard_map/ppermute | solution.py:22
  26.5 0.0 copy-done.2
  26.5 0.1 pad_maximum_fusion
  26.6 1.3 %collective-permute-start = (bf16[4,224,256]{2,1,0:T(8,128)(2,1)S(1)}, bf16[4,224,256]{2,1,0:T(8,128)(2,1)S(1)}, u32[]{:S(2)}, u32[]{:S(2)}) collective-permute-start(bf16[4,224,256]{2,1,0:T(8,128)(2,1)S(1)} %get-tuple-element.28), channel_id=1, source_target_pairs={{0,1},{1,2},{2,3},{3,4},{4,5},{5,6},{6,7},{8,9},{9,10},{10,11},{11... | collective-permute-start | bytes 1376264 | tf_op jit(solution)/shard_map/ppermute | solution.py:111
  27.9 2.2 %collective-permute-done.3.refs_1_ = bf16[2,9,8,256]{3,2,1,0:T(8,128)(2,1)S(1)} collective-permute-done((bf16[2,9,8,256]{3,2,1,0:T(8,128)(2,1)S(1)}, bf16[2,9,8,256]{3,2,1,0:T(8,128)(2,1)S(1)}, u32[]{:S(2)}, u32[]{:S(2)}) %collective-permute-start.3) | collective-permute-done | bytes 73760 | tf_op jit(solution)/shard_map/ppermute | solution.py:22
  30.2 0.4 collective-permute-start.4
  30.6 7.7 %collective-permute-done.4.refs_1_ = bf16[4,9,8,256]{3,2,1,0:T(8,128)(2,1)S(1)} collective-permute-done((bf16[4,9,8,256]{3,2,1,0:T(8,128)(2,1)S(1)}, bf16[4,9,8,256]{3,2,1,0:T(8,128)(2,1)S(1)}, u32[]{:S(2)}, u32[]{:S(2)}) %collective-permute-start.4) | collective-permute-done | bytes 147488 | tf_op jit(solution)/shard_map/ppermute | solution.py:22
  38.3 1.3 %collective-permute-start.5 = (bf16[8,9,8,256]{3,2,1,0:T(8,128)(2,1)S(1)}, bf16[8,9,8,256]{3,2,1,0:T(8,128)(2,1)S(1)}, u32[]{:S(2)}, u32[]{:S(2)}) collective-permute-start(bf16[8,9,8,256]{3,2,1,0:T(8,128)(2,1)S(1)} %shard_map.142.refs_1_), channel_id=1, source_target_pairs={{0,8},{1,9},{2,10},{3,11},{4,12},{5,13},{6,14},{7,15},{8,0},{9,1},... | collective-permute-start | bytes 884744 | tf_op jit(solution)/shard_map/ppermute | solution.py:22
  39.6 1.3 %collective-permute-start.1 = (bf16[4,224,256]{2,1,0:T(8,128)(2,1)S(1)}, bf16[4,224,256]{2,1,0:T(8,128)(2,1)S(1)}, u32[]{:S(2)}, u32[]{:S(2)}) collective-permute-start(bf16[4,224,256]{2,1,0:T(8,128)(2,1)S(1)} %get-tuple-element.27), channel_id=1, source_target_pairs={{1,0},{2,1},{3,2},{4,3},{5,4},{6,5},{7,6},{9,8},{10,9},{11,10},{12... | collective-permute-start | bytes 1376264 | tf_op jit(solution)/shard_map/ppermute | solution.py:112
  40.9 1.2 %collective-permute-start.11 = (bf16[8,18,8,256]{3,2,1,0:T(8,128)(2,1)S(1)}, bf16[8,18,8,256]{3,2,1,0:T(8,128)(2,1)S(1)}, u32[]{:S(2)}, u32[]{:S(2)}) collective-permute-start(bf16[8,18,8,256]{3,2,1,0:T(8,128)(2,1)S(1)} %shard_map.145.refs_2_.refs_6_), channel_id=1, source_target_pairs={{0,1},{1,0},{2,3},{3,2},{4,5},{5,4},{6,7},{7,6},{8,9},{9,8},{10,11... | collective-permute-start | bytes 1769480 | tf_op jit(solution)/shard_map/ppermute | solution.py:22
  42.1 0.0 collective-permute-done.10.refs_3_.refs_7_
  42.1 0.1 collective-permute-start.12
  42.2 0.0 collective-permute-done.before
  42.2 0.4 collective-permute-start.6
  42.6 2.5 %collective-permute-done.5.refs_2_ = bf16[8,9,8,256]{3,2,1,0:T(8,128)(2,1)S(1)} collective-permute-done((bf16[8,9,8,256]{3,2,1,0:T(8,128)(2,1)S(1)}, bf16[8,9,8,256]{3,2,1,0:T(8,128)(2,1)S(1)}, u32[]{:S(2)}, u32[]{:S(2)}) %collective-permute-start.5) | collective-permute-done | bytes 294944 | tf_op jit(solution)/shard_map/ppermute | solution.py:22
  45.1 0.0 collective-permute-start.7
  45.1 0.0 collective-permute-done.1.after
  45.1 0.0 copy-done
  45.1 1.5 %shard_map.139 = (bf16[4,6,128,768]{3,2,1,0:T(8,128)(2,1)S(1)}, bf16[4,4,64,768]{3,2,1,0:T(8,128)(2,1)S(1)}, bf16[4,3,32,768]{3,2,1,0:T(8,128)(2,1)S(1)}) custom-call(bf16[4,4,128,256]{3,2,1,0:T(8,128)(2,1)S(1)} %copy-done, bf16[4,2,64,256]{3,2,1,0:T(8,128)(2,1)S(1)} %copy-done.1, bf16[4,1,32,256]{3,2,1,0:T(8,128)(2,1)S(1)} %copy-done.2, ...), custom_call_target="tpu_custom_call" | custom-call | flops 27525120 | bytes 9175040 | tf_op jit(solution)/shard_map/pallas_call | solution.py:132
  46.6 0.0 collective-permute-done.6.refs_3_
  46.6 0.1 collective-permute-done.7.refs_4_
  46.7 3.1 %shard_map.143 = (f32[4,4,128,256]{3,2,1,0:T(8,128)S(1)}, f32[8,256]{1,0:T(8,128)S(1)}) custom-call(bf16[4,6,128,768]{3,2,1,0:T(8,128)(2,1)S(1)} %get-tuple-element.13.refs_0_, bf16[8,9,8,256]{3,2,1,0:T(8,128)(2,1)S(1)} %shard_map.142.refs_1_, bf16[8,9,8,256]{3,2,1,0:T(8,128)(2,1)S(1)} %collective-permute-done.5.refs_2_, ...), custom_call_target="tpu_custom_call" | custom-call | flops 2415919104 | bytes 8003584 | tf_op jit(solution)/shard_map/pallas_call | solution.py:132
  49.8 0.0 collective-permute-done.11.refs_4_.refs_8_
  49.8 0.0 collective-permute-done.12.refs_5_.refs_9_
  49.8 0.0 copy-start.3
  49.8 0.0 copy-start.4
  49.8 0.0 copy-start.5
  49.8 0.0 copy-start.6
  49.8 0.0 copy-start.7
  49.8 0.0 copy-start.8
  49.8 1.5 %shard_map.146 = (f32[4,2,64,256]{3,2,1,0:T(8,128)S(1)}, f32[4,1,32,256]{3,2,1,0:T(8,128)S(1)}, f32[16,256]{1,0:T(8,128)S(1)}) custom-call(bf16[4,4,64,768]{3,2,1,0:T(8,128)(2,1)S(1)} %get-tuple-element.16.refs_0_, bf16[4,3,32,768]{3,2,1,0:T(8,128)(2,1)S(1)} %get-tuple-element.17.refs_1_, bf16[8,18,8,256]{3,2,1,0:T(8,128)(2,1)S(1)} %shard_map.145.refs_2_.refs_6_, ...), custom_call_target="tpu_custom_call" | custom-call | flops 754974720 | bytes 7553024 | tf_op jit(solution)/shard_map/pallas_call | solution.py:132
  51.4 5.1 %collective-permute-start.13 = (f32[1,24,256]{2,1,0:T(8,128)S(1)}, f32[1,24,256]{2,1,0:T(8,128)S(1)}, u32[]{:S(2)}, u32[]{:S(2)}) collective-permute-start(f32[1,24,256]{2,1,0:T(8,128)S(1)} %bitcast.36), channel_id=1, source_target_pairs={{0,1},{1,0},{2,3},{3,2},{4,5},{5,4},{6,7},{7,6},{8,9},{9,8},{10,11... | collective-permute-start | bytes 73736 | tf_op jit(solution)/shard_map/ppermute | solution.py:22
  56.5 0.8 %collective-permute-done.13.refs_1_ = f32[1,24,256]{2,1,0:T(8,128)S(1)} collective-permute-done((f32[1,24,256]{2,1,0:T(8,128)S(1)}, f32[1,24,256]{2,1,0:T(8,128)S(1)}, u32[]{:S(2)}, u32[]{:S(2)}) %collective-permute-start.13) | collective-permute-done | bytes 24608 | tf_op jit(solution)/shard_map/ppermute | solution.py:22
  57.3 1.1 %collective-permute-start.14 = (f32[2,24,256]{2,1,0:T(8,128)S(1)}, f32[2,24,256]{2,1,0:T(8,128)S(1)}, u32[]{:S(2)}, u32[]{:S(2)}) collective-permute-start(f32[2,24,256]{2,1,0:T(8,128)S(1)} %shard_map.148.refs_9_), channel_id=1, source_target_pairs={{0,2},{1,3},{2,0},{3,1},{4,6},{5,7},{6,4},{7,5},{8,10},{9,11},{10,... | collective-permute-start | bytes 147464 | tf_op jit(solution)/shard_map/ppermute | solution.py:22
  58.4 1.1 %collective-permute-start.15 = (f32[2,24,256]{2,1,0:T(8,128)S(1)}, f32[2,24,256]{2,1,0:T(8,128)S(1)}, u32[]{:S(2)}, u32[]{:S(2)}) collective-permute-start(f32[2,24,256]{2,1,0:T(8,128)S(1)} %shard_map.148.refs_9_), channel_id=1, source_target_pairs={{0,4},{1,5},{2,6},{3,7},{4,0},{5,1},{6,2},{7,3},{8,12},{9,13},{10,... | collective-permute-start | bytes 147464 | tf_op jit(solution)/shard_map/ppermute | solution.py:22
  59.5 1.4 %collective-permute-start.16 = (f32[2,24,256]{2,1,0:T(8,128)S(1)}, f32[2,24,256]{2,1,0:T(8,128)S(1)}, u32[]{:S(2)}, u32[]{:S(2)}) collective-permute-start(f32[2,24,256]{2,1,0:T(8,128)S(1)} %shard_map.148.refs_9_), channel_id=1, source_target_pairs={{0,6},{1,7},{2,4},{3,5},{4,2},{5,3},{6,0},{7,1},{8,14},{9,15},{10,... | collective-permute-start | bytes 147464 | tf_op jit(solution)/shard_map/ppermute | solution.py:22
  60.9 0.6 collective-permute-done.14.refs_10_
  61.4 1.1 %collective-permute-done.15.refs_11_ = f32[2,24,256]{2,1,0:T(8,128)S(1)} collective-permute-done((f32[2,24,256]{2,1,0:T(8,128)S(1)}, f32[2,24,256]{2,1,0:T(8,128)S(1)}, u32[]{:S(2)}, u32[]{:S(2)}) %collective-permute-start.15) | collective-permute-done | bytes 49184 | tf_op jit(solution)/shard_map/ppermute | solution.py:22
  62.5 2.0 %collective-permute-done.16.refs_12_ = f32[2,24,256]{2,1,0:T(8,128)S(1)} collective-permute-done((f32[2,24,256]{2,1,0:T(8,128)S(1)}, f32[2,24,256]{2,1,0:T(8,128)S(1)}, u32[]{:S(2)}, u32[]{:S(2)}) %collective-permute-start.16) | collective-permute-done | bytes 49184 | tf_op jit(solution)/shard_map/ppermute | solution.py:22
  64.5 0.0 copy-done.3
  64.5 0.0 copy-done.4
  64.5 0.0 copy-done.5
  64.5 0.0 copy-done.6
  64.5 0.0 copy-done.7
  64.5 0.0 copy-done.8
  64.5 2.2 %shard_map.149 = (f32[4,4,128,256]{3,2,1,0:T(8,128)}, f32[4,2,64,256]{3,2,1,0:T(8,128)}, f32[4,1,32,256]{3,2,1,0:T(8,128)}) custom-call(f32[4,4,128,256]{3,2,1,0:T(8,128)S(1)} %get-tuple-element.15.refs_0_, f32[4,2,64,256]{3,2,1,0:T(8,128)S(1)} %get-tuple-element.19.refs_1_, f32[4,1,32,256]{3,2,1,0:T(8,128)S(1)} %get-tuple-element.20.refs_2_, ...), custom_call_target="tpu_custom_call" | custom-call | flops 5505024 | bytes 5707776 | tf_op jit(solution)/shard_map/pallas_call | solution.py:132
  (8 shorter events, 0.1 us)
Async XLA Ops:
  0.6 24.3 %copy-start.1 = (bf16[4,2,64,256]{3,2,1,0:T(8,128)(2,1)S(1)}, bf16[4,2,64,256]{3,2,1,0:T(8,128)(2,1)}, u32[]{:S(2)}) copy-start(bf16[4,2,64,256]{3,2,1,0:T(8,128)(2,1)} %l4.1) | copy-start | bytes 786436
  0.6 25.9 %copy-start.2 = (bf16[4,1,32,256]{3,2,1,0:T(8,128)(2,1)S(1)}, bf16[4,1,32,256]{3,2,1,0:T(8,128)(2,1)}, u32[]{:S(2)}) copy-start(bf16[4,1,32,256]{3,2,1,0:T(8,128)(2,1)} %l5.1) | copy-start | bytes 196612
  1.5 9.6 %collective-permute-start.2 = (bf16[1,27,8,256]{3,2,1,0:T(8,128)(2,1)S(1)}, bf16[1,27,8,256]{3,2,1,0:T(8,128)(2,1)S(1)}, u32[]{:S(2)}, u32[]{:S(2)}) collective-permute-start(bf16[1,27,8,256]{3,2,1,0:T(8,128)(2,1)S(1)} %maximum_bitcast_fusion.first), channel_id=1, source_target_pairs={{0,16},{1,17},{2,18},{3,19},{4,20},{5,21},{6,22},{7,23},{8,24},{9,... | collective-permute-start | bytes 331784 | tf_op jit(solution)/shard_map/ppermute | solution.py:22
  11.1 5.2 %collective-permute-start.8 = (bf16[2,18,8,256]{3,2,1,0:T(8,128)(2,1)S(1)}, bf16[2,18,8,256]{3,2,1,0:T(8,128)(2,1)S(1)}, u32[]{:S(2)}, u32[]{:S(2)}) collective-permute-start(bf16[2,18,8,256]{3,2,1,0:T(8,128)(2,1)S(1)} %get-tuple-element.18.refs_0_), channel_id=1, source_target_pairs={{0,8},{1,9},{2,10},{3,11},{4,12},{5,13},{6,14},{7,15},{8,0},{9,1},... | collective-permute-start | bytes 442376 | tf_op jit(solution)/shard_map/ppermute | solution.py:22
  16.3 6.8 %collective-permute-start.9 = (bf16[4,18,8,256]{3,2,1,0:T(8,128)(2,1)S(1)}, bf16[4,18,8,256]{3,2,1,0:T(8,128)(2,1)S(1)}, u32[]{:S(2)}, u32[]{:S(2)}) collective-permute-start(bf16[4,18,8,256]{3,2,1,0:T(8,128)(2,1)S(1)} %shard_map.144.refs_0_), channel_id=1, source_target_pairs={{0,4},{1,3},{2,6},{3,1},{4,0},{5,7},{6,2},{7,5},{8,12},{9,11},{10,... | collective-permute-start | bytes 884744 | tf_op jit(solution)/shard_map/ppermute | solution.py:22
  19.0 26.1 %copy-start = (bf16[4,4,128,256]{3,2,1,0:T(8,128)(2,1)S(1)}, bf16[4,4,128,256]{3,2,1,0:T(8,128)(2,1)}, u32[]{:S(2)}) copy-start(bf16[4,4,128,256]{3,2,1,0:T(8,128)(2,1)} %l3.1) | copy-start | bytes 3145732
  23.2 18.9 %collective-permute-start.10 = (bf16[8,18,8,256]{3,2,1,0:T(8,128)(2,1)S(1)}, bf16[8,18,8,256]{3,2,1,0:T(8,128)(2,1)S(1)}, u32[]{:S(2)}, u32[]{:S(2)}) collective-permute-start(bf16[8,18,8,256]{3,2,1,0:T(8,128)(2,1)S(1)} %shard_map.145.refs_2_.refs_6_), channel_id=1, source_target_pairs={{0,2},{1,5},{2,0},{3,7},{4,6},{5,1},{6,4},{7,3},{8,10},{9,13},{10,... | collective-permute-start | bytes 1769480 | tf_op jit(solution)/shard_map/ppermute | solution.py:22
  25.0 5.2 %collective-permute-start.3 = (bf16[2,9,8,256]{3,2,1,0:T(8,128)(2,1)S(1)}, bf16[2,9,8,256]{3,2,1,0:T(8,128)(2,1)S(1)}, u32[]{:S(2)}, u32[]{:S(2)}) collective-permute-start(bf16[2,9,8,256]{3,2,1,0:T(8,128)(2,1)S(1)} %get-tuple-element.14.refs_0_), channel_id=1, source_target_pairs={{0,4},{1,3},{2,6},{3,1},{4,0},{5,7},{6,2},{7,5},{8,12},{9,11},{10,... | collective-permute-start | bytes 221192 | tf_op jit(solution)/shard_map/ppermute | solution.py:22
  26.6 15.6 %collective-permute-start = (bf16[4,224,256]{2,1,0:T(8,128)(2,1)S(1)}, bf16[4,224,256]{2,1,0:T(8,128)(2,1)S(1)}, u32[]{:S(2)}, u32[]{:S(2)}) collective-permute-start(bf16[4,224,256]{2,1,0:T(8,128)(2,1)S(1)} %get-tuple-element.28), channel_id=1, source_target_pairs={{0,1},{1,2},{2,3},{3,4},{4,5},{5,6},{6,7},{8,9},{9,10},{10,11},{11... | collective-permute-start | bytes 1376264 | tf_op jit(solution)/shard_map/ppermute | solution.py:111
  30.2 8.1 %collective-permute-start.4 = (bf16[4,9,8,256]{3,2,1,0:T(8,128)(2,1)S(1)}, bf16[4,9,8,256]{3,2,1,0:T(8,128)(2,1)S(1)}, u32[]{:S(2)}, u32[]{:S(2)}) collective-permute-start(bf16[4,9,8,256]{3,2,1,0:T(8,128)(2,1)S(1)} %shard_map.141.refs_0_), channel_id=1, source_target_pairs={{0,2},{1,5},{2,0},{3,7},{4,6},{5,1},{6,4},{7,3},{8,10},{9,13},{10,... | collective-permute-start | bytes 442376 | tf_op jit(solution)/shard_map/ppermute | solution.py:22
  38.3 6.8 %collective-permute-start.5 = (bf16[8,9,8,256]{3,2,1,0:T(8,128)(2,1)S(1)}, bf16[8,9,8,256]{3,2,1,0:T(8,128)(2,1)S(1)}, u32[]{:S(2)}, u32[]{:S(2)}) collective-permute-start(bf16[8,9,8,256]{3,2,1,0:T(8,128)(2,1)S(1)} %shard_map.142.refs_1_), channel_id=1, source_target_pairs={{0,8},{1,9},{2,10},{3,11},{4,12},{5,13},{6,14},{7,15},{8,0},{9,1},... | collective-permute-start | bytes 884744 | tf_op jit(solution)/shard_map/ppermute | solution.py:22
  39.6 5.5 %collective-permute-start.1 = (bf16[4,224,256]{2,1,0:T(8,128)(2,1)S(1)}, bf16[4,224,256]{2,1,0:T(8,128)(2,1)S(1)}, u32[]{:S(2)}, u32[]{:S(2)}) collective-permute-start(bf16[4,224,256]{2,1,0:T(8,128)(2,1)S(1)} %get-tuple-element.27), channel_id=1, source_target_pairs={{1,0},{2,1},{3,2},{4,3},{5,4},{6,5},{7,6},{9,8},{10,9},{11,10},{12... | collective-permute-start | bytes 1376264 | tf_op jit(solution)/shard_map/ppermute | solution.py:112
  40.9 8.9 %collective-permute-start.11 = (bf16[8,18,8,256]{3,2,1,0:T(8,128)(2,1)S(1)}, bf16[8,18,8,256]{3,2,1,0:T(8,128)(2,1)S(1)}, u32[]{:S(2)}, u32[]{:S(2)}) collective-permute-start(bf16[8,18,8,256]{3,2,1,0:T(8,128)(2,1)S(1)} %shard_map.145.refs_2_.refs_6_), channel_id=1, source_target_pairs={{0,1},{1,0},{2,3},{3,2},{4,5},{5,4},{6,7},{7,6},{8,9},{9,8},{10,11... | collective-permute-start | bytes 1769480 | tf_op jit(solution)/shard_map/ppermute | solution.py:22
  42.1 7.7 %collective-permute-start.12 = (bf16[8,18,8,256]{3,2,1,0:T(8,128)(2,1)S(1)}, bf16[8,18,8,256]{3,2,1,0:T(8,128)(2,1)S(1)}, u32[]{:S(2)}, u32[]{:S(2)}) collective-permute-start(bf16[8,18,8,256]{3,2,1,0:T(8,128)(2,1)S(1)} %collective-permute-done.10.refs_3_.refs_7_), channel_id=1, source_target_pairs={{0,1},{1,0},{2,3},{3,2},{4,5},{5,4},{6,7},{7,6},{8,9},{9,8},{10,11... | collective-permute-start | bytes 1769480 | tf_op jit(solution)/shard_map/ppermute | solution.py:22
  42.2 4.5 %collective-permute-start.6 = (bf16[8,9,8,256]{3,2,1,0:T(8,128)(2,1)S(1)}, bf16[8,9,8,256]{3,2,1,0:T(8,128)(2,1)S(1)}, u32[]{:S(2)}, u32[]{:S(2)}) collective-permute-start(bf16[8,9,8,256]{3,2,1,0:T(8,128)(2,1)S(1)} %shard_map.142.refs_1_), channel_id=1, source_target_pairs={{0,1},{1,0},{2,3},{3,2},{4,5},{5,4},{6,7},{7,6},{8,9},{9,8},{10,11... | collective-permute-start | bytes 884744 | tf_op jit(solution)/shard_map/ppermute | solution.py:22
  45.1 1.6 %collective-permute-start.7 = (bf16[8,9,8,256]{3,2,1,0:T(8,128)(2,1)S(1)}, bf16[8,9,8,256]{3,2,1,0:T(8,128)(2,1)S(1)}, u32[]{:S(2)}, u32[]{:S(2)}) collective-permute-start(bf16[8,9,8,256]{3,2,1,0:T(8,128)(2,1)S(1)} %collective-permute-done.5.refs_2_), channel_id=1, source_target_pairs={{0,1},{1,0},{2,3},{3,2},{4,5},{5,4},{6,7},{7,6},{8,9},{9,8},{10,11... | collective-permute-start | bytes 884744 | tf_op jit(solution)/shard_map/ppermute | solution.py:22
  49.8 14.7 %copy-start.3 = (f32[256]{0:T(256)S(1)}, f32[256]{0:T(256)}, u32[]{:S(2)}) copy-start(f32[256]{0:T(256)} %param.18) | copy-start | bytes 3076
  49.8 14.7 %copy-start.4 = (f32[256]{0:T(256)S(1)}, f32[256]{0:T(256)}, u32[]{:S(2)}) copy-start(f32[256]{0:T(256)} %param.19) | copy-start | bytes 3076
  49.8 14.7 %copy-start.5 = (f32[256]{0:T(256)S(1)}, f32[256]{0:T(256)}, u32[]{:S(2)}) copy-start(f32[256]{0:T(256)} %param.20) | copy-start | bytes 3076
  49.8 14.7 %copy-start.6 = (f32[256]{0:T(256)S(1)}, f32[256]{0:T(256)}, u32[]{:S(2)}) copy-start(f32[256]{0:T(256)} %param.21) | copy-start | bytes 3076
  49.8 14.7 %copy-start.7 = (f32[256]{0:T(256)S(1)}, f32[256]{0:T(256)}, u32[]{:S(2)}) copy-start(f32[256]{0:T(256)} %param.22) | copy-start | bytes 3076
  49.8 14.7 %copy-start.8 = (f32[256]{0:T(256)S(1)}, f32[256]{0:T(256)}, u32[]{:S(2)}) copy-start(f32[256]{0:T(256)} %param.23) | copy-start | bytes 3076
  51.4 5.9 %collective-permute-start.13 = (f32[1,24,256]{2,1,0:T(8,128)S(1)}, f32[1,24,256]{2,1,0:T(8,128)S(1)}, u32[]{:S(2)}, u32[]{:S(2)}) collective-permute-start(f32[1,24,256]{2,1,0:T(8,128)S(1)} %bitcast.36), channel_id=1, source_target_pairs={{0,1},{1,0},{2,3},{3,2},{4,5},{5,4},{6,7},{7,6},{8,9},{9,8},{10,11... | collective-permute-start | bytes 73736 | tf_op jit(solution)/shard_map/ppermute | solution.py:22
  57.3 4.1 %collective-permute-start.14 = (f32[2,24,256]{2,1,0:T(8,128)S(1)}, f32[2,24,256]{2,1,0:T(8,128)S(1)}, u32[]{:S(2)}, u32[]{:S(2)}) collective-permute-start(f32[2,24,256]{2,1,0:T(8,128)S(1)} %shard_map.148.refs_9_), channel_id=1, source_target_pairs={{0,2},{1,3},{2,0},{3,1},{4,6},{5,7},{6,4},{7,5},{8,10},{9,11},{10,... | collective-permute-start | bytes 147464 | tf_op jit(solution)/shard_map/ppermute | solution.py:22
  58.4 4.1 %collective-permute-start.15 = (f32[2,24,256]{2,1,0:T(8,128)S(1)}, f32[2,24,256]{2,1,0:T(8,128)S(1)}, u32[]{:S(2)}, u32[]{:S(2)}) collective-permute-start(f32[2,24,256]{2,1,0:T(8,128)S(1)} %shard_map.148.refs_9_), channel_id=1, source_target_pairs={{0,4},{1,5},{2,6},{3,7},{4,0},{5,1},{6,2},{7,3},{8,12},{9,13},{10,... | collective-permute-start | bytes 147464 | tf_op jit(solution)/shard_map/ppermute | solution.py:22
  59.5 5.0 %collective-permute-start.16 = (f32[2,24,256]{2,1,0:T(8,128)S(1)}, f32[2,24,256]{2,1,0:T(8,128)S(1)}, u32[]{:S(2)}, u32[]{:S(2)}) collective-permute-start(f32[2,24,256]{2,1,0:T(8,128)S(1)} %shard_map.148.refs_9_), channel_id=1, source_target_pairs={{0,6},{1,7},{2,4},{3,5},{4,2},{5,3},{6,0},{7,1},{8,14},{9,15},{10,... | collective-permute-start | bytes 147464 | tf_op jit(solution)/shard_map/ppermute | solution.py:22

commit v4 on v3

--- a/solution.py
+++ b/solution.py
@@ -62,9 +62,7 @@
     orders = [[(q, r), (r, q), (p, p)], [(p, p), (q, r), (r, q)]]
     swapped = [(len(lead), len(lead) + 1), (len(lead) + 1, len(lead) + 2)]
     result = []
-    for chunk, order, places, members in zip(
-        chunks, orders, swapped, (range(1), range(1, len(lengths)))
-    ):
+    for chunk, order, places, members in zip(chunks, orders, swapped, (range(1), range(1, len(lengths)))):
         for step in (0, 1):
             received = exchange(chunk, AXES, size, order[step])
             chunk = joined(chunk, received)
@@ -103,11 +101,31 @@
     return starts
 
 
+def edges_body(l3, l4, l5, top, bottom, sems):
+    copies = []
+    for source, start in zip((l3, l4, l5), starts_of(l3, l4, l5)):
+        rows, width = source.shape[1:3]
+        for target, row in ((top, 0), (bottom, rows - 1)):
+            copies.append(
+                pltpu.make_async_copy(
+                    source.at[:, row], target.at[:, start : start + width], sems.at[len(copies)]
+                )
+            )
+            copies[-1].start()
+    for copy in copies:
+        copy.wait()
+
+
 def halos(*levels):
     count = lax.axis_size("space")
     ahead = [(i, i + 1) for i in range(count - 1)]
-    top = jnp.concatenate([a[:, 0] for a in levels], axis=1)
-    bottom = jnp.concatenate([a[:, -1] for a in levels], axis=1)
+    width = sum(a.shape[2] for a in levels)
+    edge = jax.ShapeDtypeStruct((levels[0].shape[0], width, levels[0].shape[3]), BF16)
+    kept = [pltpu.with_memory_space_constraint(a, pltpu.HBM) for a in levels]
+    scratch = [pltpu.SemaphoreType.DMA((2 * len(levels),))]
+    top, bottom = call(
+        edges_body, [edge, edge], kept, scratch, edge.size, in_specs=[ANY] * len(kept), room=1
+    )
     before = lax.ppermute(bottom, "space", ahead)
     after = lax.ppermute(top, "space", [(j, i) for i, j in ahead])
     return before, after

time: 66.9 us -> 66.4 us (level)
  Pallas kernels: 8.47 us -> 9.65 us
  local copies, waits for them, and re-layouts: 1.13 us -> 0.06 us
  waiting for transfers between devices: 30.9 us -> 29.9 us
    pallas_call x11 -> x12, Pallas kernels: 8.47 us -> 9.65 us  [call(): pl.pallas_call(body, out_shape=outs, in_specs=in_specs or [VMEM] * len(in...]
    squeeze x2 -> x0, local copies, waits for them, and re-layouts: 1.08 us -> none  [halos(): top = jnp.concatenate([a[:, 0] for a in levels], axis=1)]
    ppermute x15, waiting for transfers between devices: 30.9 us -> 29.9 us  [exchange(): lax.ppermute(array, axes, [(i, i ^ masks[i % 2]) for i in range(size)])]
  transfers between devices with their start and end apart: 17 -> 17, of which waited for: 11 -> 10; matrix products, arithmetic and copies ran while one was open for 2% -> 0% of each run, Pallas kernels for 7% -> 9%
where the time goes in v4:
time: 66.4 us; the launch traced here: 66.2 us
  waiting for transfers between devices  29.9 us (45%)
  starting transfers between devices  24.9 us (38%)
  Pallas kernels  9.65 us (15%)
  between operations  0.85 us (1%)
  other arithmetic  0.82 us (1%)
    ppermute x15, waiting for transfers between devices, exchange(): lax.ppermute(array, axes, [(i, i ^ masks[i % 2]) for i in range(size)])  29.9 us
    ppermute x15, starting transfers between devices, exchange(): lax.ppermute(array, axes, [(i, i ^ masks[i % 2]) for i in range(size)])  22.3 us
    pallas_call x12, Pallas kernels, call(): pl.pallas_call(body, out_shape=outs, in_specs=in_specs or [VMEM] * len(in...  9.65 us
  transfers between devices with their start and end apart: 17, of which 10 were waited for; matrix products, arithmetic and copies ran while one was open for 0% of the time, Pallas kernels for 9%

profile of v4, /device:TPU:0, one launch (start us, length us, event | category | flops | bytes accessed | tf_op | source)
XLA Modules:
  0.0 66.2 jit_solution(15874237085893859970)
XLA Ops:
  0.6 0.8 %maximum_bitcast_fusion.first = bf16[1,27,8,256]{3,2,1,0:T(8,128)(2,1)S(1)} fusion(bf16[9,8,256]{2,1,0:T(8,128)(2,1)} %bitcast.26, bf16[9,8,256]{2,1,0:T(8,128)(2,1)} %bitcast.27, bf16[9,8,256]{2,1,0:T(8,128)(2,1)} %bitcast.28), kind=kLoop, calls=%fused_computation | loop fusion | flops 110592 | bytes 221184 | tf_op jit(solution)/shard_map/broadcast_in_dim | solution.py:89
  1.5 0.0 copy-start
  1.5 0.0 copy-start.1
  1.5 0.0 copy-start.2
  1.5 4.1 %collective-permute-start.2 = (bf16[1,27,8,256]{3,2,1,0:T(8,128)(2,1)S(1)}, bf16[1,27,8,256]{3,2,1,0:T(8,128)(2,1)S(1)}, u32[]{:S(2)}, u32[]{:S(2)}) collective-permute-start(bf16[1,27,8,256]{3,2,1,0:T(8,128)(2,1)S(1)} %maximum_bitcast_fusion.first), channel_id=1, source_target_pairs={{0,16},{1,17},{2,18},{3,19},{4,20},{5,21},{6,22},{7,23},{8,24},{9,... | collective-permute-start | bytes 331784 | tf_op jit(solution)/shard_map/ppermute | solution.py:22
  5.6 5.4 %collective-permute-done.2.second = bf16[1,27,8,256]{3,2,1,0:T(8,128)(2,1)S(1)} collective-permute-done((bf16[1,27,8,256]{3,2,1,0:T(8,128)(2,1)S(1)}, bf16[1,27,8,256]{3,2,1,0:T(8,128)(2,1)S(1)}, u32[]{:S(2)}, u32[]{:S(2)}) %collective-permute-start.2) | collective-permute-done | bytes 110624 | tf_op jit(solution)/shard_map/ppermute | solution.py:22
  11.1 0.8 %collective-permute-start.8 = (bf16[2,18,8,256]{3,2,1,0:T(8,128)(2,1)S(1)}, bf16[2,18,8,256]{3,2,1,0:T(8,128)(2,1)S(1)}, u32[]{:S(2)}, u32[]{:S(2)}) collective-permute-start(bf16[2,18,8,256]{3,2,1,0:T(8,128)(2,1)S(1)} %get-tuple-element.22.refs_0_), channel_id=1, source_target_pairs={{0,8},{1,9},{2,10},{3,11},{4,12},{5,13},{6,14},{7,15},{8,0},{9,1},... | collective-permute-start | bytes 442376 | tf_op jit(solution)/shard_map/ppermute | solution.py:22
  11.9 4.4 %collective-permute-done.8.refs_1_ = bf16[2,18,8,256]{3,2,1,0:T(8,128)(2,1)S(1)} collective-permute-done((bf16[2,18,8,256]{3,2,1,0:T(8,128)(2,1)S(1)}, bf16[2,18,8,256]{3,2,1,0:T(8,128)(2,1)S(1)}, u32[]{:S(2)}, u32[]{:S(2)}) %collective-permute-start.8) | collective-permute-done | bytes 147488 | tf_op jit(solution)/shard_map/ppermute | solution.py:22
  16.3 1.6 %collective-permute-start.9 = (bf16[4,18,8,256]{3,2,1,0:T(8,128)(2,1)S(1)}, bf16[4,18,8,256]{3,2,1,0:T(8,128)(2,1)S(1)}, u32[]{:S(2)}, u32[]{:S(2)}) collective-permute-start(bf16[4,18,8,256]{3,2,1,0:T(8,128)(2,1)S(1)} %shard_map.145.refs_0_), channel_id=1, source_target_pairs={{0,4},{1,3},{2,6},{3,1},{4,0},{5,7},{6,2},{7,5},{8,12},{9,11},{10,... | collective-permute-start | bytes 884744 | tf_op jit(solution)/shard_map/ppermute | solution.py:22
  17.9 5.2 %collective-permute-done.9.refs_1_ = bf16[4,18,8,256]{3,2,1,0:T(8,128)(2,1)S(1)} collective-permute-done((bf16[4,18,8,256]{3,2,1,0:T(8,128)(2,1)S(1)}, bf16[4,18,8,256]{3,2,1,0:T(8,128)(2,1)S(1)}, u32[]{:S(2)}, u32[]{:S(2)}) %collective-permute-start.9) | collective-permute-done | bytes 294944 | tf_op jit(solution)/shard_map/ppermute | solution.py:22
  23.2 1.7 %collective-permute-start.10 = (bf16[8,18,8,256]{3,2,1,0:T(8,128)(2,1)S(1)}, bf16[8,18,8,256]{3,2,1,0:T(8,128)(2,1)S(1)}, u32[]{:S(2)}, u32[]{:S(2)}) collective-permute-start(bf16[8,18,8,256]{3,2,1,0:T(8,128)(2,1)S(1)} %shard_map.146.refs_2_.refs_6_), channel_id=1, source_target_pairs={{0,2},{1,5},{2,0},{3,7},{4,6},{5,1},{6,4},{7,3},{8,10},{9,13},{10,... | collective-permute-start | bytes 1769480 | tf_op jit(solution)/shard_map/ppermute | solution.py:22
  24.9 1.5 %collective-permute-start.3 = (bf16[2,9,8,256]{3,2,1,0:T(8,128)(2,1)S(1)}, bf16[2,9,8,256]{3,2,1,0:T(8,128)(2,1)S(1)}, u32[]{:S(2)}, u32[]{:S(2)}) collective-permute-start(bf16[2,9,8,256]{3,2,1,0:T(8,128)(2,1)S(1)} %get-tuple-element.18.refs_0_), channel_id=1, source_target_pairs={{0,4},{1,3},{2,6},{3,1},{4,0},{5,7},{6,2},{7,5},{8,12},{9,11},{10,... | collective-permute-start | bytes 221192 | tf_op jit(solution)/shard_map/ppermute | solution.py:22
  26.4 1.2 %shard_map.139 = (bf16[4,224,256]{2,1,0:T(8,128)(2,1)S(1)}, bf16[4,224,256]{2,1,0:T(8,128)(2,1)S(1)}) custom-call(bf16[4,4,128,256]{3,2,1,0:T(8,128)(2,1)} %l3.3, bf16[4,2,64,256]{3,2,1,0:T(8,128)(2,1)} %l4.3, bf16[4,1,32,256]{3,2,1,0:T(8,128)(2,1)} %l5.3), custom_call_target="tpu_custom_call" | custom-call | flops 229376 | bytes 2293760 | tf_op jit(solution)/shard_map/pallas_call | solution.py:150
  27.6 1.3 %collective-permute-start = (bf16[4,224,256]{2,1,0:T(8,128)(2,1)S(1)}, bf16[4,224,256]{2,1,0:T(8,128)(2,1)S(1)}, u32[]{:S(2)}, u32[]{:S(2)}) collective-permute-start(bf16[4,224,256]{2,1,0:T(8,128)(2,1)S(1)} %get-tuple-element.15), channel_id=1, source_target_pairs={{0,1},{1,2},{2,3},{3,4},{4,5},{5,6},{6,7},{8,9},{9,10},{10,11},{11... | collective-permute-start | bytes 1376264 | tf_op jit(solution)/shard_map/ppermute | solution.py:129
  28.9 1.1 %collective-permute-done.3.refs_1_ = bf16[2,9,8,256]{3,2,1,0:T(8,128)(2,1)S(1)} collective-permute-done((bf16[2,9,8,256]{3,2,1,0:T(8,128)(2,1)S(1)}, bf16[2,9,8,256]{3,2,1,0:T(8,128)(2,1)S(1)}, u32[]{:S(2)}, u32[]{:S(2)}) %collective-permute-start.3) | collective-permute-done | bytes 73760 | tf_op jit(solution)/shard_map/ppermute | solution.py:22
  30.1 0.4 collective-permute-start.4
  30.5 6.8 %collective-permute-done.4.refs_1_ = bf16[4,9,8,256]{3,2,1,0:T(8,128)(2,1)S(1)} collective-permute-done((bf16[4,9,8,256]{3,2,1,0:T(8,128)(2,1)S(1)}, bf16[4,9,8,256]{3,2,1,0:T(8,128)(2,1)S(1)}, u32[]{:S(2)}, u32[]{:S(2)}) %collective-permute-start.4) | collective-permute-done | bytes 147488 | tf_op jit(solution)/shard_map/ppermute | solution.py:22
  37.3 1.3 %collective-permute-start.5 = (bf16[8,9,8,256]{3,2,1,0:T(8,128)(2,1)S(1)}, bf16[8,9,8,256]{3,2,1,0:T(8,128)(2,1)S(1)}, u32[]{:S(2)}, u32[]{:S(2)}) collective-permute-start(bf16[8,9,8,256]{3,2,1,0:T(8,128)(2,1)S(1)} %shard_map.143.refs_1_), channel_id=1, source_target_pairs={{0,8},{1,9},{2,10},{3,11},{4,12},{5,13},{6,14},{7,15},{8,0},{9,1},... | collective-permute-start | bytes 884744 | tf_op jit(solution)/shard_map/ppermute | solution.py:22
  38.6 1.3 %collective-permute-start.1 = (bf16[4,224,256]{2,1,0:T(8,128)(2,1)S(1)}, bf16[4,224,256]{2,1,0:T(8,128)(2,1)S(1)}, u32[]{:S(2)}, u32[]{:S(2)}) collective-permute-start(bf16[4,224,256]{2,1,0:T(8,128)(2,1)S(1)} %get-tuple-element.16), channel_id=1, source_target_pairs={{1,0},{2,1},{3,2},{4,3},{5,4},{6,5},{7,6},{9,8},{10,9},{11,10},{12... | collective-permute-start | bytes 1376264 | tf_op jit(solution)/shard_map/ppermute | solution.py:130
  39.8 1.2 %collective-permute-start.11 = (bf16[8,18,8,256]{3,2,1,0:T(8,128)(2,1)S(1)}, bf16[8,18,8,256]{3,2,1,0:T(8,128)(2,1)S(1)}, u32[]{:S(2)}, u32[]{:S(2)}) collective-permute-start(bf16[8,18,8,256]{3,2,1,0:T(8,128)(2,1)S(1)} %shard_map.146.refs_2_.refs_6_), channel_id=1, source_target_pairs={{0,1},{1,0},{2,3},{3,2},{4,5},{5,4},{6,7},{7,6},{8,9},{9,8},{10,11... | collective-permute-start | bytes 1769480 | tf_op jit(solution)/shard_map/ppermute | solution.py:22
  41.0 0.0 collective-permute-done.10.refs_3_.refs_7_
  41.0 0.1 collective-permute-start.12
  41.1 0.0 collective-permute-done.before
  41.1 0.4 collective-permute-start.6
  41.6 2.5 %collective-permute-done.5.refs_2_ = bf16[8,9,8,256]{3,2,1,0:T(8,128)(2,1)S(1)} collective-permute-done((bf16[8,9,8,256]{3,2,1,0:T(8,128)(2,1)S(1)}, bf16[8,9,8,256]{3,2,1,0:T(8,128)(2,1)S(1)}, u32[]{:S(2)}, u32[]{:S(2)}) %collective-permute-start.5) | collective-permute-done | bytes 294944 | tf_op jit(solution)/shard_map/ppermute | solution.py:22
  44.1 0.0 collective-permute-start.7
  44.1 0.0 collective-permute-done.1.after
  44.1 0.0 copy-done
  44.1 0.0 copy-done.1
  44.1 0.0 copy-done.2
  44.1 1.5 %shard_map.140 = (bf16[4,6,128,768]{3,2,1,0:T(8,128)(2,1)S(1)}, bf16[4,4,64,768]{3,2,1,0:T(8,128)(2,1)S(1)}, bf16[4,3,32,768]{3,2,1,0:T(8,128)(2,1)S(1)}) custom-call(bf16[4,4,128,256]{3,2,1,0:T(8,128)(2,1)S(1)} %copy-done, bf16[4,2,64,256]{3,2,1,0:T(8,128)(2,1)S(1)} %copy-done.1, bf16[4,1,32,256]{3,2,1,0:T(8,128)(2,1)S(1)} %copy-done.2, ...), custom_call_target="tpu_custom_call" | custom-call | flops 27525120 | bytes 9175040 | tf_op jit(solution)/shard_map/pallas_call | solution.py:150
  45.6 0.0 collective-permute-done.6.refs_3_
  45.6 0.0 collective-permute-done.7.refs_4_
  45.6 3.1 %shard_map.144 = (f32[4,4,128,256]{3,2,1,0:T(8,128)S(1)}, f32[8,256]{1,0:T(8,128)S(1)}) custom-call(bf16[4,6,128,768]{3,2,1,0:T(8,128)(2,1)S(1)} %get-tuple-element.17.refs_0_, bf16[8,9,8,256]{3,2,1,0:T(8,128)(2,1)S(1)} %shard_map.143.refs_1_, bf16[8,9,8,256]{3,2,1,0:T(8,128)(2,1)S(1)} %collective-permute-done.5.refs_2_, ...), custom_call_target="tpu_custom_call" | custom-call | flops 2415919104 | bytes 8003584 | tf_op jit(solution)/shard_map/pallas_call | solution.py:150
  48.8 0.0 collective-permute-done.11.refs_4_.refs_8_
  48.8 0.0 collective-permute-done.12.refs_5_.refs_9_
  48.8 0.0 copy-start.3
  48.8 0.0 copy-start.4
  48.8 0.0 copy-start.5
  48.8 0.0 copy-start.6
  48.8 0.0 copy-start.7
  48.8 0.0 copy-start.8
  48.8 1.5 %shard_map.147 = (f32[4,2,64,256]{3,2,1,0:T(8,128)S(1)}, f32[4,1,32,256]{3,2,1,0:T(8,128)S(1)}, f32[16,256]{1,0:T(8,128)S(1)}) custom-call(bf16[4,4,64,768]{3,2,1,0:T(8,128)(2,1)S(1)} %get-tuple-element.20.refs_0_, bf16[4,3,32,768]{3,2,1,0:T(8,128)(2,1)S(1)} %get-tuple-element.21.refs_1_, bf16[8,18,8,256]{3,2,1,0:T(8,128)(2,1)S(1)} %shard_map.146.refs_2_.refs_6_, ...), custom_call_target="tpu_custom_call" | custom-call | flops 754974720 | bytes 7553024 | tf_op jit(solution)/shard_map/pallas_call | solution.py:150
  50.4 5.1 %collective-permute-start.13 = (f32[1,24,256]{2,1,0:T(8,128)S(1)}, f32[1,24,256]{2,1,0:T(8,128)S(1)}, u32[]{:S(2)}, u32[]{:S(2)}) collective-permute-start(f32[1,24,256]{2,1,0:T(8,128)S(1)} %bitcast.18), channel_id=1, source_target_pairs={{0,1},{1,0},{2,3},{3,2},{4,5},{5,4},{6,7},{7,6},{8,9},{9,8},{10,11... | collective-permute-start | bytes 73736 | tf_op jit(solution)/shard_map/ppermute | solution.py:22
  55.5 0.8 %collective-permute-done.13.refs_1_ = f32[1,24,256]{2,1,0:T(8,128)S(1)} collective-permute-done((f32[1,24,256]{2,1,0:T(8,128)S(1)}, f32[1,24,256]{2,1,0:T(8,128)S(1)}, u32[]{:S(2)}, u32[]{:S(2)}) %collective-permute-start.13) | collective-permute-done | bytes 24608 | tf_op jit(solution)/shard_map/ppermute | solution.py:22
  56.3 1.5 %collective-permute-start.14 = (f32[2,24,256]{2,1,0:T(8,128)S(1)}, f32[2,24,256]{2,1,0:T(8,128)S(1)}, u32[]{:S(2)}, u32[]{:S(2)}) collective-permute-start(f32[2,24,256]{2,1,0:T(8,128)S(1)} %shard_map.149.refs_9_), channel_id=1, source_target_pairs={{0,2},{1,3},{2,0},{3,1},{4,6},{5,7},{6,4},{7,5},{8,10},{9,11},{10,... | collective-permute-start | bytes 147464 | tf_op jit(solution)/shard_map/ppermute | solution.py:22
  57.8 1.1 %collective-permute-start.15 = (f32[2,24,256]{2,1,0:T(8,128)S(1)}, f32[2,24,256]{2,1,0:T(8,128)S(1)}, u32[]{:S(2)}, u32[]{:S(2)}) collective-permute-start(f32[2,24,256]{2,1,0:T(8,128)S(1)} %shard_map.149.refs_9_), channel_id=1, source_target_pairs={{0,4},{1,5},{2,6},{3,7},{4,0},{5,1},{6,2},{7,3},{8,12},{9,13},{10,... | collective-permute-start | bytes 147464 | tf_op jit(solution)/shard_map/ppermute | solution.py:22
  58.9 1.4 %collective-permute-start.16 = (f32[2,24,256]{2,1,0:T(8,128)S(1)}, f32[2,24,256]{2,1,0:T(8,128)S(1)}, u32[]{:S(2)}, u32[]{:S(2)}) collective-permute-start(f32[2,24,256]{2,1,0:T(8,128)S(1)} %shard_map.149.refs_9_), channel_id=1, source_target_pairs={{0,6},{1,7},{2,4},{3,5},{4,2},{5,3},{6,0},{7,1},{8,14},{9,15},{10,... | collective-permute-start | bytes 147464 | tf_op jit(solution)/shard_map/ppermute | solution.py:22
  60.3 0.1 collective-permute-done.14.refs_10_
  60.4 1.5 %collective-permute-done.15.refs_11_ = f32[2,24,256]{2,1,0:T(8,128)S(1)} collective-permute-done((f32[2,24,256]{2,1,0:T(8,128)S(1)}, f32[2,24,256]{2,1,0:T(8,128)S(1)}, u32[]{:S(2)}, u32[]{:S(2)}) %collective-permute-start.15) | collective-permute-done | bytes 49184 | tf_op jit(solution)/shard_map/ppermute | solution.py:22
  61.9 2.0 %collective-permute-done.16.refs_12_ = f32[2,24,256]{2,1,0:T(8,128)S(1)} collective-permute-done((f32[2,24,256]{2,1,0:T(8,128)S(1)}, f32[2,24,256]{2,1,0:T(8,128)S(1)}, u32[]{:S(2)}, u32[]{:S(2)}) %collective-permute-start.16) | collective-permute-done | bytes 49184 | tf_op jit(solution)/shard_map/ppermute | solution.py:22
  63.9 0.0 copy-done.3
  63.9 0.0 copy-done.4
  63.9 0.0 copy-done.5
  63.9 0.0 copy-done.6
  63.9 0.0 copy-done.7
  63.9 0.0 copy-done.8
  64.0 2.2 %shard_map.150 = (f32[4,4,128,256]{3,2,1,0:T(8,128)}, f32[4,2,64,256]{3,2,1,0:T(8,128)}, f32[4,1,32,256]{3,2,1,0:T(8,128)}) custom-call(f32[4,4,128,256]{3,2,1,0:T(8,128)S(1)} %get-tuple-element.19.refs_0_, f32[4,2,64,256]{3,2,1,0:T(8,128)S(1)} %get-tuple-element.23.refs_1_, f32[4,1,32,256]{3,2,1,0:T(8,128)S(1)} %get-tuple-element.24.refs_2_, ...), custom_call_target="tpu_custom_call" | custom-call | flops 5505024 | bytes 5707776 | tf_op jit(solution)/shard_map/pallas_call | solution.py:150
  (7 shorter events, 0.1 us)
Async XLA Ops:
  1.5 42.6 %copy-start = (bf16[4,4,128,256]{3,2,1,0:T(8,128)(2,1)S(1)}, bf16[4,4,128,256]{3,2,1,0:T(8,128)(2,1)}, u32[]{:S(2)}) copy-start(bf16[4,4,128,256]{3,2,1,0:T(8,128)(2,1)} %l3.3) | copy-start | bytes 3145732
  1.5 42.6 %copy-start.1 = (bf16[4,2,64,256]{3,2,1,0:T(8,128)(2,1)S(1)}, bf16[4,2,64,256]{3,2,1,0:T(8,128)(2,1)}, u32[]{:S(2)}) copy-start(bf16[4,2,64,256]{3,2,1,0:T(8,128)(2,1)} %l4.3) | copy-start | bytes 786436
  1.5 42.6 %copy-start.2 = (bf16[4,1,32,256]{3,2,1,0:T(8,128)(2,1)S(1)}, bf16[4,1,32,256]{3,2,1,0:T(8,128)(2,1)}, u32[]{:S(2)}) copy-start(bf16[4,1,32,256]{3,2,1,0:T(8,128)(2,1)} %l5.3) | copy-start | bytes 196612
  1.5 9.6 %collective-permute-start.2 = (bf16[1,27,8,256]{3,2,1,0:T(8,128)(2,1)S(1)}, bf16[1,27,8,256]{3,2,1,0:T(8,128)(2,1)S(1)}, u32[]{:S(2)}, u32[]{:S(2)}) collective-permute-start(bf16[1,27,8,256]{3,2,1,0:T(8,128)(2,1)S(1)} %maximum_bitcast_fusion.first), channel_id=1, source_target_pairs={{0,16},{1,17},{2,18},{3,19},{4,20},{5,21},{6,22},{7,23},{8,24},{9,... | collective-permute-start | bytes 331784 | tf_op jit(solution)/shard_map/ppermute | solution.py:22
  11.1 5.2 %collective-permute-start.8 = (bf16[2,18,8,256]{3,2,1,0:T(8,128)(2,1)S(1)}, bf16[2,18,8,256]{3,2,1,0:T(8,128)(2,1)S(1)}, u32[]{:S(2)}, u32[]{:S(2)}) collective-permute-start(bf16[2,18,8,256]{3,2,1,0:T(8,128)(2,1)S(1)} %get-tuple-element.22.refs_0_), channel_id=1, source_target_pairs={{0,8},{1,9},{2,10},{3,11},{4,12},{5,13},{6,14},{7,15},{8,0},{9,1},... | collective-permute-start | bytes 442376 | tf_op jit(solution)/shard_map/ppermute | solution.py:22
  16.3 6.8 %collective-permute-start.9 = (bf16[4,18,8,256]{3,2,1,0:T(8,128)(2,1)S(1)}, bf16[4,18,8,256]{3,2,1,0:T(8,128)(2,1)S(1)}, u32[]{:S(2)}, u32[]{:S(2)}) collective-permute-start(bf16[4,18,8,256]{3,2,1,0:T(8,128)(2,1)S(1)} %shard_map.145.refs_0_), channel_id=1, source_target_pairs={{0,4},{1,3},{2,6},{3,1},{4,0},{5,7},{6,2},{7,5},{8,12},{9,11},{10,... | collective-permute-start | bytes 884744 | tf_op jit(solution)/shard_map/ppermute | solution.py:22
  23.2 17.9 %collective-permute-start.10 = (bf16[8,18,8,256]{3,2,1,0:T(8,128)(2,1)S(1)}, bf16[8,18,8,256]{3,2,1,0:T(8,128)(2,1)S(1)}, u32[]{:S(2)}, u32[]{:S(2)}) collective-permute-start(bf16[8,18,8,256]{3,2,1,0:T(8,128)(2,1)S(1)} %shard_map.146.refs_2_.refs_6_), channel_id=1, source_target_pairs={{0,2},{1,5},{2,0},{3,7},{4,6},{5,1},{6,4},{7,3},{8,10},{9,13},{10,... | collective-permute-start | bytes 1769480 | tf_op jit(solution)/shard_map/ppermute | solution.py:22
  24.9 5.1 %collective-permute-start.3 = (bf16[2,9,8,256]{3,2,1,0:T(8,128)(2,1)S(1)}, bf16[2,9,8,256]{3,2,1,0:T(8,128)(2,1)S(1)}, u32[]{:S(2)}, u32[]{:S(2)}) collective-permute-start(bf16[2,9,8,256]{3,2,1,0:T(8,128)(2,1)S(1)} %get-tuple-element.18.refs_0_), channel_id=1, source_target_pairs={{0,4},{1,3},{2,6},{3,1},{4,0},{5,7},{6,2},{7,5},{8,12},{9,11},{10,... | collective-permute-start | bytes 221192 | tf_op jit(solution)/shard_map/ppermute | solution.py:22
  27.6 13.5 %collective-permute-start = (bf16[4,224,256]{2,1,0:T(8,128)(2,1)S(1)}, bf16[4,224,256]{2,1,0:T(8,128)(2,1)S(1)}, u32[]{:S(2)}, u32[]{:S(2)}) collective-permute-start(bf16[4,224,256]{2,1,0:T(8,128)(2,1)S(1)} %get-tuple-element.15), channel_id=1, source_target_pairs={{0,1},{1,2},{2,3},{3,4},{4,5},{5,6},{6,7},{8,9},{9,10},{10,11},{11... | collective-permute-start | bytes 1376264 | tf_op jit(solution)/shard_map/ppermute | solution.py:129
  30.1 7.2 %collective-permute-start.4 = (bf16[4,9,8,256]{3,2,1,0:T(8,128)(2,1)S(1)}, bf16[4,9,8,256]{3,2,1,0:T(8,128)(2,1)S(1)}, u32[]{:S(2)}, u32[]{:S(2)}) collective-permute-start(bf16[4,9,8,256]{3,2,1,0:T(8,128)(2,1)S(1)} %shard_map.142.refs_0_), channel_id=1, source_target_pairs={{0,2},{1,5},{2,0},{3,7},{4,6},{5,1},{6,4},{7,3},{8,10},{9,13},{10,... | collective-permute-start | bytes 442376 | tf_op jit(solution)/shard_map/ppermute | solution.py:22
  37.3 6.8 %collective-permute-start.5 = (bf16[8,9,8,256]{3,2,1,0:T(8,128)(2,1)S(1)}, bf16[8,9,8,256]{3,2,1,0:T(8,128)(2,1)S(1)}, u32[]{:S(2)}, u32[]{:S(2)}) collective-permute-start(bf16[8,9,8,256]{3,2,1,0:T(8,128)(2,1)S(1)} %shard_map.143.refs_1_), channel_id=1, source_target_pairs={{0,8},{1,9},{2,10},{3,11},{4,12},{5,13},{6,14},{7,15},{8,0},{9,1},... | collective-permute-start | bytes 884744 | tf_op jit(solution)/shard_map/ppermute | solution.py:22
  38.6 5.5 %collective-permute-start.1 = (bf16[4,224,256]{2,1,0:T(8,128)(2,1)S(1)}, bf16[4,224,256]{2,1,0:T(8,128)(2,1)S(1)}, u32[]{:S(2)}, u32[]{:S(2)}) collective-permute-start(bf16[4,224,256]{2,1,0:T(8,128)(2,1)S(1)} %get-tuple-element.16), channel_id=1, source_target_pairs={{1,0},{2,1},{3,2},{4,3},{5,4},{6,5},{7,6},{9,8},{10,9},{11,10},{12... | collective-permute-start | bytes 1376264 | tf_op jit(solution)/shard_map/ppermute | solution.py:130
  39.8 8.9 %collective-permute-start.11 = (bf16[8,18,8,256]{3,2,1,0:T(8,128)(2,1)S(1)}, bf16[8,18,8,256]{3,2,1,0:T(8,128)(2,1)S(1)}, u32[]{:S(2)}, u32[]{:S(2)}) collective-permute-start(bf16[8,18,8,256]{3,2,1,0:T(8,128)(2,1)S(1)} %shard_map.146.refs_2_.refs_6_), channel_id=1, source_target_pairs={{0,1},{1,0},{2,3},{3,2},{4,5},{5,4},{6,7},{7,6},{8,9},{9,8},{10,11... | collective-permute-start | bytes 1769480 | tf_op jit(solution)/shard_map/ppermute | solution.py:22
  41.0 7.7 %collective-permute-start.12 = (bf16[8,18,8,256]{3,2,1,0:T(8,128)(2,1)S(1)}, bf16[8,18,8,256]{3,2,1,0:T(8,128)(2,1)S(1)}, u32[]{:S(2)}, u32[]{:S(2)}) collective-permute-start(bf16[8,18,8,256]{3,2,1,0:T(8,128)(2,1)S(1)} %collective-permute-done.10.refs_3_.refs_7_), channel_id=1, source_target_pairs={{0,1},{1,0},{2,3},{3,2},{4,5},{5,4},{6,7},{7,6},{8,9},{9,8},{10,11... | collective-permute-start | bytes 1769480 | tf_op jit(solution)/shard_map/ppermute | solution.py:22
  41.1 4.5 %collective-permute-start.6 = (bf16[8,9,8,256]{3,2,1,0:T(8,128)(2,1)S(1)}, bf16[8,9,8,256]{3,2,1,0:T(8,128)(2,1)S(1)}, u32[]{:S(2)}, u32[]{:S(2)}) collective-permute-start(bf16[8,9,8,256]{3,2,1,0:T(8,128)(2,1)S(1)} %shard_map.143.refs_1_), channel_id=1, source_target_pairs={{0,1},{1,0},{2,3},{3,2},{4,5},{5,4},{6,7},{7,6},{8,9},{9,8},{10,11... | collective-permute-start | bytes 884744 | tf_op jit(solution)/shard_map/ppermute | solution.py:22
  44.1 1.6 %collective-permute-start.7 = (bf16[8,9,8,256]{3,2,1,0:T(8,128)(2,1)S(1)}, bf16[8,9,8,256]{3,2,1,0:T(8,128)(2,1)S(1)}, u32[]{:S(2)}, u32[]{:S(2)}) collective-permute-start(bf16[8,9,8,256]{3,2,1,0:T(8,128)(2,1)S(1)} %collective-permute-done.5.refs_2_), channel_id=1, source_target_pairs={{0,1},{1,0},{2,3},{3,2},{4,5},{5,4},{6,7},{7,6},{8,9},{9,8},{10,11... | collective-permute-start | bytes 884744 | tf_op jit(solution)/shard_map/ppermute | solution.py:22
  48.8 15.1 %copy-start.3 = (f32[256]{0:T(256)S(1)}, f32[256]{0:T(256)}, u32[]{:S(2)}) copy-start(f32[256]{0:T(256)} %param.18) | copy-start | bytes 3076
  48.8 15.1 %copy-start.4 = (f32[256]{0:T(256)S(1)}, f32[256]{0:T(256)}, u32[]{:S(2)}) copy-start(f32[256]{0:T(256)} %param.19) | copy-start | bytes 3076
  48.8 15.1 %copy-start.5 = (f32[256]{0:T(256)S(1)}, f32[256]{0:T(256)}, u32[]{:S(2)}) copy-start(f32[256]{0:T(256)} %param.20) | copy-start | bytes 3076
  48.8 15.1 %copy-start.6 = (f32[256]{0:T(256)S(1)}, f32[256]{0:T(256)}, u32[]{:S(2)}) copy-start(f32[256]{0:T(256)} %param.21) | copy-start | bytes 3076
  48.8 15.1 %copy-start.7 = (f32[256]{0:T(256)S(1)}, f32[256]{0:T(256)}, u32[]{:S(2)}) copy-start(f32[256]{0:T(256)} %param.22) | copy-start | bytes 3076
  48.8 15.1 %copy-start.8 = (f32[256]{0:T(256)S(1)}, f32[256]{0:T(256)}, u32[]{:S(2)}) copy-start(f32[256]{0:T(256)} %param.23) | copy-start | bytes 3076
  50.4 5.9 %collective-permute-start.13 = (f32[1,24,256]{2,1,0:T(8,128)S(1)}, f32[1,24,256]{2,1,0:T(8,128)S(1)}, u32[]{:S(2)}, u32[]{:S(2)}) collective-permute-start(f32[1,24,256]{2,1,0:T(8,128)S(1)} %bitcast.18), channel_id=1, source_target_pairs={{0,1},{1,0},{2,3},{3,2},{4,5},{5,4},{6,7},{7,6},{8,9},{9,8},{10,11... | collective-permute-start | bytes 73736 | tf_op jit(solution)/shard_map/ppermute | solution.py:22
  56.3 4.1 %collective-permute-start.14 = (f32[2,24,256]{2,1,0:T(8,128)S(1)}, f32[2,24,256]{2,1,0:T(8,128)S(1)}, u32[]{:S(2)}, u32[]{:S(2)}) collective-permute-start(f32[2,24,256]{2,1,0:T(8,128)S(1)} %shard_map.149.refs_9_), channel_id=1, source_target_pairs={{0,2},{1,3},{2,0},{3,1},{4,6},{5,7},{6,4},{7,5},{8,10},{9,11},{10,... | collective-permute-start | bytes 147464 | tf_op jit(solution)/shard_map/ppermute | solution.py:22
  57.8 4.1 %collective-permute-start.15 = (f32[2,24,256]{2,1,0:T(8,128)S(1)}, f32[2,24,256]{2,1,0:T(8,128)S(1)}, u32[]{:S(2)}, u32[]{:S(2)}) collective-permute-start(f32[2,24,256]{2,1,0:T(8,128)S(1)} %shard_map.149.refs_9_), channel_id=1, source_target_pairs={{0,4},{1,5},{2,6},{3,7},{4,0},{5,1},{6,2},{7,3},{8,12},{9,13},{10,... | collective-permute-start | bytes 147464 | tf_op jit(solution)/shard_map/ppermute | solution.py:22
  58.9 5.0 %collective-permute-start.16 = (f32[2,24,256]{2,1,0:T(8,128)S(1)}, f32[2,24,256]{2,1,0:T(8,128)S(1)}, u32[]{:S(2)}, u32[]{:S(2)}) collective-permute-start(f32[2,24,256]{2,1,0:T(8,128)S(1)} %shard_map.149.refs_9_), channel_id=1, source_target_pairs={{0,6},{1,7},{2,4},{3,5},{4,2},{5,3},{6,0},{7,1},{8,14},{9,15},{10,... | collective-permute-start | bytes 147464 | tf_op jit(solution)/shard_map/ppermute | solution.py:22

commit v5 on v4

--- a/solution.py
+++ b/solution.py
@@ -59,21 +59,24 @@
         if k + 1 < len(lead):
             together = joined(together, received)
     chunks = halved(together, received, lengths[0])
-    orders = [[(q, r), (r, q), (p, p)], [(p, p), (q, r), (r, q)]]
-    swapped = [(len(lead), len(lead) + 1), (len(lead) + 1, len(lead) + 2)]
+    orders = [[(q, r), (p, p), (r, q)], [(p, p), (q, r), (r, q)]]
+    swapped = [(len(lead) + 0, len(lead) + 2), (len(lead) + 1, len(lead) + 2)]
     result = []
-    for chunk, order, places, members in zip(chunks, orders, swapped, (range(1), range(1, len(lengths)))):
-        for step in (0, 1):
-            received = exchange(chunk, AXES, size, order[step])
-            chunk = joined(chunk, received)
-        received = exchange(chunk, AXES, size, order[2])
-        near = exchange(chunk, AXES, size, (1, 1))
-        far = exchange(received, AXES, size, (1, 1))
+    result = []
+    for chunk, order, places, members in zip(chunks, orders, swapped, (lengths[:1], lengths[1:])):
+        received = exchange(chunk, AXES, size, order[0])
+        chunk = joined(chunk, received)
+        received = exchange(chunk, AXES, size, order[1])
+        if len(members) == 1:
+            pieces = [joined(chunk, received)]
+        else:
+            pieces = halved(chunk, received, members[0])
         steps = [(bit, bit) for bit in lead] + order
-        start = 0
-        for k in members:
-            result.append(([chunk, received, near, far], start, steps, places))
-            start += lengths[k]
+        for piece in pieces:
+            last = exchange(piece, AXES, size, order[2])
+            near = exchange(piece, AXES, size, (1, 1))
+            far = exchange(last, AXES, size, (1, 1))
+            result.append(([piece, last, near, far], 0, steps, places))
     return result
 
 
@@ -140,7 +143,7 @@
     for start in range(0, len(bits), 2) if len(bits) % 2 == 0 else [-1] + list(range(1, len(bits), 2)):
         some = bits[max(start, 0) : start + 2]
         whole = held[0] if len(held) == 1 else joined(*held)
-        masks = some if len(some) == 1 else some + [some[0] | some[1]]
+        masks = some if len(some) == 1 else [some[0] | some[1]] + some
         held = [whole] + [exchange(whole, "space", size, (m, m)) for m in masks]
     return held
 
@@ -370,8 +373,9 @@
     before, after = halos(l3, l4, l5)
     x3, x4, x5 = prepare(l3, l4, l5, before, after)
     (f3,), stats3 = convolve([x3], weights[:1], outer)
-    (f4, f5), stats45 = convolve([x4, x5], weights[1:], outer)
-    stats = statistics_of_all(joined(stats3, stats45))
+    (f4,), stats4 = convolve([x4], weights[1:2], outer)
+    (f5,), stats5 = convolve([x5], weights[2:], outer)
+    stats = statistics_of_all(joined(stats3, stats4, stats5))
     affine = [a[None] for a in (gain3, shift3, gain4, shift4, gain5, shift5)]
     return tuple(normalize([f3, f4, f5], affine, stats))
 

time: 66.4 us -> 60.2 us (0.907)
  waiting for transfers between devices: 29.9 us -> 19.7 us
  starting transfers between devices: 24.9 us -> 28.5 us
    ppermute x15 -> x18, waiting for transfers between devices: 29.9 us -> 19.7 us  [exchange(): lax.ppermute(array, axes, [(i, i ^ masks[i % 2]) for i in range(size)])]
    ppermute x15 -> x18, starting transfers between devices: 22.3 us -> 25.9 us  [exchange(): lax.ppermute(array, axes, [(i, i ^ masks[i % 2]) for i in range(size)])]
    pallas_call x12 -> x13, Pallas kernels: 9.65 us -> 9.95 us  [call(): pl.pallas_call(body, out_shape=outs, in_specs=in_specs or [VMEM] * len(in...]
  transfers between devices with their start and end apart: 17 -> 20, of which waited for: 10 -> 8; matrix products, arithmetic and copies ran while one was open for 0% -> 0% of each run, Pallas kernels for 9% -> 11%
where the time goes in v5:
time: 60.2 us; the launch traced here: 60 us
  starting transfers between devices  28.5 us (47%)
  waiting for transfers between devices  19.7 us (33%)
  Pallas kernels  9.95 us (17%)
  other arithmetic  0.92 us (2%)
  between operations  0.88 us (1%)
    ppermute x18, starting transfers between devices, exchange(): lax.ppermute(array, axes, [(i, i ^ masks[i % 2]) for i in range(size)])  25.9 us
    ppermute x18, waiting for transfers between devices, exchange(): lax.ppermute(array, axes, [(i, i ^ masks[i % 2]) for i in range(size)])  19.7 us
    pallas_call x13, Pallas kernels, call(): pl.pallas_call(body, out_shape=outs, in_specs=in_specs or [VMEM] * len(in...  9.95 us
    ppermute x1, starting transfers between devices, halos(): before = lax.ppermute(bottom, 'space', ahead)  1.32 us
    ppermute x1, starting transfers between devices, halos(): after = lax.ppermute(top, 'space', [(j, i) for i, j in ahead])  1.28 us
  transfers between devices with their start and end apart: 20, of which 8 were waited for; matrix products, arithmetic and copies ran while one was open for 0% of the time, Pallas kernels for 11%

profile of v5, /device:TPU:0, one launch (start us, length us, event | category | flops | bytes accessed | tf_op | source)
XLA Modules:
  0.0 60.0 jit_solution(14091985252204037760)
XLA Ops:
  0.6 0.0 copy-start
  0.6 0.0 copy-start.1
  0.7 0.0 copy-start.2
  0.7 0.9 %maximum_bitcast_fusion.first = bf16[1,27,8,256]{3,2,1,0:T(8,128)(2,1)S(1)} fusion(bf16[9,8,256]{2,1,0:T(8,128)(2,1)} %bitcast.26, bf16[9,8,256]{2,1,0:T(8,128)(2,1)} %bitcast.27, bf16[9,8,256]{2,1,0:T(8,128)(2,1)} %bitcast.28), kind=kLoop, calls=%fused_computation | loop fusion | flops 110592 | bytes 221184 | tf_op jit(solution)/shard_map/broadcast_in_dim | solution.py:92
  1.6 4.1 %collective-permute-start.2 = (bf16[1,27,8,256]{3,2,1,0:T(8,128)(2,1)S(1)}, bf16[1,27,8,256]{3,2,1,0:T(8,128)(2,1)S(1)}, u32[]{:S(2)}, u32[]{:S(2)}) collective-permute-start(bf16[1,27,8,256]{3,2,1,0:T(8,128)(2,1)S(1)} %maximum_bitcast_fusion.first), channel_id=1, source_target_pairs={{0,16},{1,17},{2,18},{3,19},{4,20},{5,21},{6,22},{7,23},{8,24},{9,... | collective-permute-start | bytes 331784 | tf_op jit(solution)/shard_map/ppermute | solution.py:22
  5.7 5.4 %collective-permute-done.2.second = bf16[1,27,8,256]{3,2,1,0:T(8,128)(2,1)S(1)} collective-permute-done((bf16[1,27,8,256]{3,2,1,0:T(8,128)(2,1)S(1)}, bf16[1,27,8,256]{3,2,1,0:T(8,128)(2,1)S(1)}, u32[]{:S(2)}, u32[]{:S(2)}) %collective-permute-start.2) | collective-permute-done | bytes 110624 | tf_op jit(solution)/shard_map/ppermute | solution.py:22
  11.2 1.6 %collective-permute-start.3 = (bf16[2,9,8,256]{3,2,1,0:T(8,128)(2,1)S(1)}, bf16[2,9,8,256]{3,2,1,0:T(8,128)(2,1)S(1)}, u32[]{:S(2)}, u32[]{:S(2)}) collective-permute-start(bf16[2,9,8,256]{3,2,1,0:T(8,128)(2,1)S(1)} %get-tuple-element.21.refs_0_), channel_id=1, source_target_pairs={{0,4},{1,3},{2,6},{3,1},{4,0},{5,7},{6,2},{7,5},{8,12},{9,11},{10,... | collective-permute-start | bytes 221192 | tf_op jit(solution)/shard_map/ppermute | solution.py:22
  12.8 1.2 %shard_map.139 = (bf16[4,224,256]{2,1,0:T(8,128)(2,1)S(1)}, bf16[4,224,256]{2,1,0:T(8,128)(2,1)S(1)}) custom-call(bf16[4,4,128,256]{3,2,1,0:T(8,128)(2,1)} %l3.3, bf16[4,2,64,256]{3,2,1,0:T(8,128)(2,1)} %l4.3, bf16[4,1,32,256]{3,2,1,0:T(8,128)(2,1)} %l5.3), custom_call_target="tpu_custom_call" | custom-call | flops 229376 | bytes 2293760 | tf_op jit(solution)/shard_map/pallas_call | solution.py:153
  14.0 1.3 %collective-permute-start = (bf16[4,224,256]{2,1,0:T(8,128)(2,1)S(1)}, bf16[4,224,256]{2,1,0:T(8,128)(2,1)S(1)}, u32[]{:S(2)}, u32[]{:S(2)}) collective-permute-start(bf16[4,224,256]{2,1,0:T(8,128)(2,1)S(1)} %get-tuple-element.18), channel_id=1, source_target_pairs={{0,1},{1,2},{2,3},{3,4},{4,5},{5,6},{6,7},{8,9},{9,10},{10,11},{11... | collective-permute-start | bytes 1376264 | tf_op jit(solution)/shard_map/ppermute | solution.py:132
  15.3 1.1 %collective-permute-start.8 = (bf16[2,18,8,256]{3,2,1,0:T(8,128)(2,1)S(1)}, bf16[2,18,8,256]{3,2,1,0:T(8,128)(2,1)S(1)}, u32[]{:S(2)}, u32[]{:S(2)}) collective-permute-start(bf16[2,18,8,256]{3,2,1,0:T(8,128)(2,1)S(1)} %get-tuple-element.24.refs_0_), channel_id=1, source_target_pairs={{0,8},{1,9},{2,10},{3,11},{4,12},{5,13},{6,14},{7,15},{8,0},{9,1},... | collective-permute-start | bytes 442376 | tf_op jit(solution)/shard_map/ppermute | solution.py:22
  16.4 0.0 collective-permute-done.3.refs_1_
  16.4 1.1 %collective-permute-start.4 = (bf16[4,9,8,256]{3,2,1,0:T(8,128)(2,1)S(1)}, bf16[4,9,8,256]{3,2,1,0:T(8,128)(2,1)S(1)}, u32[]{:S(2)}, u32[]{:S(2)}) collective-permute-start(bf16[4,9,8,256]{3,2,1,0:T(8,128)(2,1)S(1)} %shard_map.142.refs_0_), channel_id=1, source_target_pairs={{0,8},{1,9},{2,10},{3,11},{4,12},{5,13},{6,14},{7,15},{8,0},{9,1},... | collective-permute-start | bytes 442376 | tf_op jit(solution)/shard_map/ppermute | solution.py:22
  17.5 3.4 %collective-permute-done.8.refs_1_ = bf16[2,18,8,256]{3,2,1,0:T(8,128)(2,1)S(1)} collective-permute-done((bf16[2,18,8,256]{3,2,1,0:T(8,128)(2,1)S(1)}, bf16[2,18,8,256]{3,2,1,0:T(8,128)(2,1)S(1)}, u32[]{:S(2)}, u32[]{:S(2)}) %collective-permute-start.8) | collective-permute-done | bytes 147488 | tf_op jit(solution)/shard_map/ppermute | solution.py:22
  20.9 1.7 %collective-permute-start.9 = (bf16[4,18,8,256]{3,2,1,0:T(8,128)(2,1)S(1)}, bf16[4,18,8,256]{3,2,1,0:T(8,128)(2,1)S(1)}, u32[]{:S(2)}, u32[]{:S(2)}) collective-permute-start(bf16[4,18,8,256]{3,2,1,0:T(8,128)(2,1)S(1)} %shard_map.145.first), channel_id=1, source_target_pairs={{0,4},{1,3},{2,6},{3,1},{4,0},{5,7},{6,2},{7,5},{8,12},{9,11},{10,... | collective-permute-start | bytes 884744 | tf_op jit(solution)/shard_map/ppermute | solution.py:22
  22.6 1.5 %collective-permute-done.4.refs_1_ = bf16[4,9,8,256]{3,2,1,0:T(8,128)(2,1)S(1)} collective-permute-done((bf16[4,9,8,256]{3,2,1,0:T(8,128)(2,1)S(1)}, bf16[4,9,8,256]{3,2,1,0:T(8,128)(2,1)S(1)}, u32[]{:S(2)}, u32[]{:S(2)}) %collective-permute-start.4) | collective-permute-done | bytes 147488 | tf_op jit(solution)/shard_map/ppermute | solution.py:22
  24.0 2.9 %collective-permute-start.5 = (bf16[8,9,8,256]{3,2,1,0:T(8,128)(2,1)S(1)}, bf16[8,9,8,256]{3,2,1,0:T(8,128)(2,1)S(1)}, u32[]{:S(2)}, u32[]{:S(2)}) collective-permute-start(bf16[8,9,8,256]{3,2,1,0:T(8,128)(2,1)S(1)} %shard_map.143.refs_1_), channel_id=1, source_target_pairs={{0,2},{1,5},{2,0},{3,7},{4,6},{5,1},{6,4},{7,3},{8,10},{9,13},{10,... | collective-permute-start | bytes 884744 | tf_op jit(solution)/shard_map/ppermute | solution.py:22
  27.0 1.3 %collective-permute-start.1 = (bf16[4,224,256]{2,1,0:T(8,128)(2,1)S(1)}, bf16[4,224,256]{2,1,0:T(8,128)(2,1)S(1)}, u32[]{:S(2)}, u32[]{:S(2)}) collective-permute-start(bf16[4,224,256]{2,1,0:T(8,128)(2,1)S(1)} %get-tuple-element.19), channel_id=1, source_target_pairs={{1,0},{2,1},{3,2},{4,3},{5,4},{6,5},{7,6},{9,8},{10,9},{11,10},{12... | collective-permute-start | bytes 1376264 | tf_op jit(solution)/shard_map/ppermute | solution.py:133
  28.3 0.0 collective-permute-done.9.second
  28.3 4.5 %collective-permute-start.13 = (bf16[8,9,8,256]{3,2,1,0:T(8,128)(2,1)S(1)}, bf16[8,9,8,256]{3,2,1,0:T(8,128)(2,1)S(1)}, u32[]{:S(2)}, u32[]{:S(2)}) collective-permute-start(bf16[8,9,8,256]{3,2,1,0:T(8,128)(2,1)S(1)} %get-tuple-element.28.refs_1_), channel_id=1, source_target_pairs={{0,2},{1,5},{2,0},{3,7},{4,6},{5,1},{6,4},{7,3},{8,10},{9,13},{10,... | collective-permute-start | bytes 884744 | tf_op jit(solution)/shard_map/ppermute | solution.py:22
  32.8 0.0 collective-permute-start.6
  32.8 0.0 collective-permute-done.before
  32.8 0.2 collective-permute-start.10
  33.0 0.0 collective-permute-done.5.refs_2_
  33.0 0.4 collective-permute-start.7
  33.4 0.0 collective-permute-done.1.after
  33.4 3.7 %collective-permute-start.14 = (bf16[8,9,8,256]{3,2,1,0:T(8,128)(2,1)S(1)}, bf16[8,9,8,256]{3,2,1,0:T(8,128)(2,1)S(1)}, u32[]{:S(2)}, u32[]{:S(2)}) collective-permute-start(bf16[8,9,8,256]{3,2,1,0:T(8,128)(2,1)S(1)} %get-tuple-element.28.refs_1_), channel_id=1, source_target_pairs={{0,1},{1,0},{2,3},{3,2},{4,5},{5,4},{6,7},{7,6},{8,9},{9,8},{10,11... | collective-permute-start | bytes 884744 | tf_op jit(solution)/shard_map/ppermute | solution.py:22
  37.2 3.3 %collective-permute-done.13.refs_2_ = bf16[8,9,8,256]{3,2,1,0:T(8,128)(2,1)S(1)} collective-permute-done((bf16[8,9,8,256]{3,2,1,0:T(8,128)(2,1)S(1)}, bf16[8,9,8,256]{3,2,1,0:T(8,128)(2,1)S(1)}, u32[]{:S(2)}, u32[]{:S(2)}) %collective-permute-start.13) | collective-permute-done | bytes 294944 | tf_op jit(solution)/shard_map/ppermute | solution.py:22
  40.5 0.0 collective-permute-start.15
  40.5 0.0 collective-permute-done.6.refs_3_
  40.5 0.5 collective-permute-start.11
  41.0 2.6 %collective-permute-done.10.refs_2_ = bf16[8,9,8,256]{3,2,1,0:T(8,128)(2,1)S(1)} collective-permute-done((bf16[8,9,8,256]{3,2,1,0:T(8,128)(2,1)S(1)}, bf16[8,9,8,256]{3,2,1,0:T(8,128)(2,1)S(1)}, u32[]{:S(2)}, u32[]{:S(2)}) %collective-permute-start.10) | collective-permute-done | bytes 294944 | tf_op jit(solution)/shard_map/ppermute | solution.py:22
  43.7 0.0 collective-permute-start.12
  43.7 0.0 copy-done
  43.7 0.0 copy-done.1
  43.7 0.0 copy-done.2
  43.7 1.5 %shard_map.140 = (bf16[4,6,128,768]{3,2,1,0:T(8,128)(2,1)S(1)}, bf16[4,4,64,768]{3,2,1,0:T(8,128)(2,1)S(1)}, bf16[4,3,32,768]{3,2,1,0:T(8,128)(2,1)S(1)}) custom-call(bf16[4,4,128,256]{3,2,1,0:T(8,128)(2,1)S(1)} %copy-done, bf16[4,2,64,256]{3,2,1,0:T(8,128)(2,1)S(1)} %copy-done.1, bf16[4,1,32,256]{3,2,1,0:T(8,128)(2,1)S(1)} %copy-done.2, ...), custom_call_target="tpu_custom_call" | custom-call | flops 27525120 | bytes 9175040 | tf_op jit(solution)/shard_map/pallas_call | solution.py:153
  45.2 0.0 collective-permute-done.7.refs_4_
  45.2 3.1 %shard_map.144 = (f32[4,4,128,256]{3,2,1,0:T(8,128)S(1)}, f32[8,256]{1,0:T(8,128)S(1)}) custom-call(bf16[4,6,128,768]{3,2,1,0:T(8,128)(2,1)S(1)} %get-tuple-element.20.refs_0_, bf16[8,9,8,256]{3,2,1,0:T(8,128)(2,1)S(1)} %shard_map.143.refs_1_, bf16[8,9,8,256]{3,2,1,0:T(8,128)(2,1)S(1)} %collective-permute-done.5.refs_2_, ...), custom_call_target="tpu_custom_call" | custom-call | flops 2415919104 | bytes 8003584 | tf_op jit(solution)/shard_map/pallas_call | solution.py:153
  48.3 0.0 collective-permute-done.14.refs_3_
  48.3 0.0 collective-permute-done.15.refs_4_
  48.3 0.0 copy-start.3
  48.3 0.0 copy-start.4
  48.3 0.0 copy-start.5
  48.3 0.0 copy-start.6
  48.3 0.0 copy-start.7
  48.3 0.0 copy-start.8
  48.4 0.8 %shard_map.148 = (f32[4,1,32,256]{3,2,1,0:T(8,128)S(1)}, f32[8,256]{1,0:T(8,128)S(1)}) custom-call(bf16[4,3,32,768]{3,2,1,0:T(8,128)(2,1)S(1)} %get-tuple-element.27.refs_0_, bf16[8,9,8,256]{3,2,1,0:T(8,128)(2,1)S(1)} %get-tuple-element.28.refs_1_, bf16[8,9,8,256]{3,2,1,0:T(8,128)(2,1)S(1)} %collective-permute-done.13.refs_2_, ...), custom_call_target="tpu_custom_call" | custom-call | flops 150994944 | bytes 1908736 | tf_op jit(solution)/shard_map/pallas_call | solution.py:153
  49.2 0.0 collective-permute-done.11.refs_3_
  49.2 0.0 collective-permute-done.12.refs_4_
  49.2 1.1 %shard_map.147 = (f32[4,2,64,256]{3,2,1,0:T(8,128)S(1)}, f32[8,256]{1,0:T(8,128)S(1)}) custom-call(bf16[4,4,64,768]{3,2,1,0:T(8,128)(2,1)S(1)} %get-tuple-element.23.refs_0_, bf16[8,9,8,256]{3,2,1,0:T(8,128)(2,1)S(1)} %get-tuple-element.25.refs_1_, bf16[8,9,8,256]{3,2,1,0:T(8,128)(2,1)S(1)} %collective-permute-done.10.refs_2_, ...), custom_call_target="tpu_custom_call" | custom-call | flops 603979776 | bytes 3284992 | tf_op jit(solution)/shard_map/pallas_call | solution.py:153
  50.3 0.6 collective-permute-start.16
  50.8 0.8 %collective-permute-done.16.refs_1_ = f32[1,24,256]{2,1,0:T(8,128)S(1)} collective-permute-done((f32[1,24,256]{2,1,0:T(8,128)S(1)}, f32[1,24,256]{2,1,0:T(8,128)S(1)}, u32[]{:S(2)}, u32[]{:S(2)}) %collective-permute-start.16) | collective-permute-done | bytes 24608 | tf_op jit(solution)/shard_map/ppermute | solution.py:22
  51.7 0.7 %collective-permute-start.17 = (f32[2,24,256]{2,1,0:T(8,128)S(1)}, f32[2,24,256]{2,1,0:T(8,128)S(1)}, u32[]{:S(2)}, u32[]{:S(2)}) collective-permute-start(f32[2,24,256]{2,1,0:T(8,128)S(1)} %shard_map.150.refs_9_), channel_id=1, source_target_pairs={{0,6},{1,7},{2,4},{3,5},{4,2},{5,3},{6,0},{7,1},{8,14},{9,15},{10,... | collective-permute-start | bytes 147464 | tf_op jit(solution)/shard_map/ppermute | solution.py:22
  52.3 1.3 %collective-permute-start.18 = (f32[2,24,256]{2,1,0:T(8,128)S(1)}, f32[2,24,256]{2,1,0:T(8,128)S(1)}, u32[]{:S(2)}, u32[]{:S(2)}) collective-permute-start(f32[2,24,256]{2,1,0:T(8,128)S(1)} %shard_map.150.refs_9_), channel_id=1, source_target_pairs={{0,2},{1,3},{2,0},{3,1},{4,6},{5,7},{6,4},{7,5},{8,10},{9,11},{10,... | collective-permute-start | bytes 147464 | tf_op jit(solution)/shard_map/ppermute | solution.py:22
  53.6 1.5 %collective-permute-start.19 = (f32[2,24,256]{2,1,0:T(8,128)S(1)}, f32[2,24,256]{2,1,0:T(8,128)S(1)}, u32[]{:S(2)}, u32[]{:S(2)}) collective-permute-start(f32[2,24,256]{2,1,0:T(8,128)S(1)} %shard_map.150.refs_9_), channel_id=1, source_target_pairs={{0,4},{1,5},{2,6},{3,7},{4,0},{5,1},{6,2},{7,3},{8,12},{9,13},{10,... | collective-permute-start | bytes 147464 | tf_op jit(solution)/shard_map/ppermute | solution.py:22
  55.2 1.7 %collective-permute-done.17.refs_10_ = f32[2,24,256]{2,1,0:T(8,128)S(1)} collective-permute-done((f32[2,24,256]{2,1,0:T(8,128)S(1)}, f32[2,24,256]{2,1,0:T(8,128)S(1)}, u32[]{:S(2)}, u32[]{:S(2)}) %collective-permute-start.17) | collective-permute-done | bytes 49184 | tf_op jit(solution)/shard_map/ppermute | solution.py:22
  56.9 0.0 collective-permute-done.18.refs_11_
  56.9 0.9 %collective-permute-done.19.refs_12_ = f32[2,24,256]{2,1,0:T(8,128)S(1)} collective-permute-done((f32[2,24,256]{2,1,0:T(8,128)S(1)}, f32[2,24,256]{2,1,0:T(8,128)S(1)}, u32[]{:S(2)}, u32[]{:S(2)}) %collective-permute-start.19) | collective-permute-done | bytes 49184 | tf_op jit(solution)/shard_map/ppermute | solution.py:22
  57.7 0.0 copy-done.3
  57.7 0.0 copy-done.4
  57.7 0.0 copy-done.5
  57.7 0.0 copy-done.6
  57.8 0.0 copy-done.7
  57.8 2.2 %shard_map.151 = (f32[4,4,128,256]{3,2,1,0:T(8,128)}, f32[4,2,64,256]{3,2,1,0:T(8,128)}, f32[4,1,32,256]{3,2,1,0:T(8,128)}) custom-call(f32[4,4,128,256]{3,2,1,0:T(8,128)S(1)} %get-tuple-element.22.refs_0_, f32[4,2,64,256]{3,2,1,0:T(8,128)S(1)} %get-tuple-element.26.refs_1_, f32[4,1,32,256]{3,2,1,0:T(8,128)S(1)} %get-tuple-element.29.refs_2_, ...), custom_call_target="tpu_custom_call" | custom-call | flops 5505024 | bytes 5707776 | tf_op jit(solution)/shard_map/pallas_call | solution.py:153
  (8 shorter events, 0.1 us)
Async XLA Ops:
  0.6 43.0 %copy-start = (bf16[4,4,128,256]{3,2,1,0:T(8,128)(2,1)S(1)}, bf16[4,4,128,256]{3,2,1,0:T(8,128)(2,1)}, u32[]{:S(2)}) copy-start(bf16[4,4,128,256]{3,2,1,0:T(8,128)(2,1)} %l3.3) | copy-start | bytes 3145732
  0.6 43.0 %copy-start.1 = (bf16[4,2,64,256]{3,2,1,0:T(8,128)(2,1)S(1)}, bf16[4,2,64,256]{3,2,1,0:T(8,128)(2,1)}, u32[]{:S(2)}) copy-start(bf16[4,2,64,256]{3,2,1,0:T(8,128)(2,1)} %l4.3) | copy-start | bytes 786436
  0.7 43.0 %copy-start.2 = (bf16[4,1,32,256]{3,2,1,0:T(8,128)(2,1)S(1)}, bf16[4,1,32,256]{3,2,1,0:T(8,128)(2,1)}, u32[]{:S(2)}) copy-start(bf16[4,1,32,256]{3,2,1,0:T(8,128)(2,1)} %l5.3) | copy-start | bytes 196612
  1.6 9.6 %collective-permute-start.2 = (bf16[1,27,8,256]{3,2,1,0:T(8,128)(2,1)S(1)}, bf16[1,27,8,256]{3,2,1,0:T(8,128)(2,1)S(1)}, u32[]{:S(2)}, u32[]{:S(2)}) collective-permute-start(bf16[1,27,8,256]{3,2,1,0:T(8,128)(2,1)S(1)} %maximum_bitcast_fusion.first), channel_id=1, source_target_pairs={{0,16},{1,17},{2,18},{3,19},{4,20},{5,21},{6,22},{7,23},{8,24},{9,... | collective-permute-start | bytes 331784 | tf_op jit(solution)/shard_map/ppermute | solution.py:22
  11.2 5.2 %collective-permute-start.3 = (bf16[2,9,8,256]{3,2,1,0:T(8,128)(2,1)S(1)}, bf16[2,9,8,256]{3,2,1,0:T(8,128)(2,1)S(1)}, u32[]{:S(2)}, u32[]{:S(2)}) collective-permute-start(bf16[2,9,8,256]{3,2,1,0:T(8,128)(2,1)S(1)} %get-tuple-element.21.refs_0_), channel_id=1, source_target_pairs={{0,4},{1,3},{2,6},{3,1},{4,0},{5,7},{6,2},{7,5},{8,12},{9,11},{10,... | collective-permute-start | bytes 221192 | tf_op jit(solution)/shard_map/ppermute | solution.py:22
  14.0 18.9 %collective-permute-start = (bf16[4,224,256]{2,1,0:T(8,128)(2,1)S(1)}, bf16[4,224,256]{2,1,0:T(8,128)(2,1)S(1)}, u32[]{:S(2)}, u32[]{:S(2)}) collective-permute-start(bf16[4,224,256]{2,1,0:T(8,128)(2,1)S(1)} %get-tuple-element.18), channel_id=1, source_target_pairs={{0,1},{1,2},{2,3},{3,4},{4,5},{5,6},{6,7},{8,9},{9,10},{10,11},{11... | collective-permute-start | bytes 1376264 | tf_op jit(solution)/shard_map/ppermute | solution.py:132
  15.3 5.6 %collective-permute-start.8 = (bf16[2,18,8,256]{3,2,1,0:T(8,128)(2,1)S(1)}, bf16[2,18,8,256]{3,2,1,0:T(8,128)(2,1)S(1)}, u32[]{:S(2)}, u32[]{:S(2)}) collective-permute-start(bf16[2,18,8,256]{3,2,1,0:T(8,128)(2,1)S(1)} %get-tuple-element.24.refs_0_), channel_id=1, source_target_pairs={{0,8},{1,9},{2,10},{3,11},{4,12},{5,13},{6,14},{7,15},{8,0},{9,1},... | collective-permute-start | bytes 442376 | tf_op jit(solution)/shard_map/ppermute | solution.py:22
  16.4 7.6 %collective-permute-start.4 = (bf16[4,9,8,256]{3,2,1,0:T(8,128)(2,1)S(1)}, bf16[4,9,8,256]{3,2,1,0:T(8,128)(2,1)S(1)}, u32[]{:S(2)}, u32[]{:S(2)}) collective-permute-start(bf16[4,9,8,256]{3,2,1,0:T(8,128)(2,1)S(1)} %shard_map.142.refs_0_), channel_id=1, source_target_pairs={{0,8},{1,9},{2,10},{3,11},{4,12},{5,13},{6,14},{7,15},{8,0},{9,1},... | collective-permute-start | bytes 442376 | tf_op jit(solution)/shard_map/ppermute | solution.py:22
  20.9 7.4 %collective-permute-start.9 = (bf16[4,18,8,256]{3,2,1,0:T(8,128)(2,1)S(1)}, bf16[4,18,8,256]{3,2,1,0:T(8,128)(2,1)S(1)}, u32[]{:S(2)}, u32[]{:S(2)}) collective-permute-start(bf16[4,18,8,256]{3,2,1,0:T(8,128)(2,1)S(1)} %shard_map.145.first), channel_id=1, source_target_pairs={{0,4},{1,3},{2,6},{3,1},{4,0},{5,7},{6,2},{7,5},{8,12},{9,11},{10,... | collective-permute-start | bytes 884744 | tf_op jit(solution)/shard_map/ppermute | solution.py:22
  24.0 9.0 %collective-permute-start.5 = (bf16[8,9,8,256]{3,2,1,0:T(8,128)(2,1)S(1)}, bf16[8,9,8,256]{3,2,1,0:T(8,128)(2,1)S(1)}, u32[]{:S(2)}, u32[]{:S(2)}) collective-permute-start(bf16[8,9,8,256]{3,2,1,0:T(8,128)(2,1)S(1)} %shard_map.143.refs_1_), channel_id=1, source_target_pairs={{0,2},{1,5},{2,0},{3,7},{4,6},{5,1},{6,4},{7,3},{8,10},{9,13},{10,... | collective-permute-start | bytes 884744 | tf_op jit(solution)/shard_map/ppermute | solution.py:22
  27.0 6.4 %collective-permute-start.1 = (bf16[4,224,256]{2,1,0:T(8,128)(2,1)S(1)}, bf16[4,224,256]{2,1,0:T(8,128)(2,1)S(1)}, u32[]{:S(2)}, u32[]{:S(2)}) collective-permute-start(bf16[4,224,256]{2,1,0:T(8,128)(2,1)S(1)} %get-tuple-element.19), channel_id=1, source_target_pairs={{1,0},{2,1},{3,2},{4,3},{5,4},{6,5},{7,6},{9,8},{10,9},{11,10},{12... | collective-permute-start | bytes 1376264 | tf_op jit(solution)/shard_map/ppermute | solution.py:133
  28.3 12.2 %collective-permute-start.13 = (bf16[8,9,8,256]{3,2,1,0:T(8,128)(2,1)S(1)}, bf16[8,9,8,256]{3,2,1,0:T(8,128)(2,1)S(1)}, u32[]{:S(2)}, u32[]{:S(2)}) collective-permute-start(bf16[8,9,8,256]{3,2,1,0:T(8,128)(2,1)S(1)} %get-tuple-element.28.refs_1_), channel_id=1, source_target_pairs={{0,2},{1,5},{2,0},{3,7},{4,6},{5,1},{6,4},{7,3},{8,10},{9,13},{10,... | collective-permute-start | bytes 884744 | tf_op jit(solution)/shard_map/ppermute | solution.py:22
  32.8 7.7 %collective-permute-start.6 = (bf16[8,9,8,256]{3,2,1,0:T(8,128)(2,1)S(1)}, bf16[8,9,8,256]{3,2,1,0:T(8,128)(2,1)S(1)}, u32[]{:S(2)}, u32[]{:S(2)}) collective-permute-start(bf16[8,9,8,256]{3,2,1,0:T(8,128)(2,1)S(1)} %shard_map.143.refs_1_), channel_id=1, source_target_pairs={{0,1},{1,0},{2,3},{3,2},{4,5},{5,4},{6,7},{7,6},{8,9},{9,8},{10,11... | collective-permute-start | bytes 884744 | tf_op jit(solution)/shard_map/ppermute | solution.py:22
  32.8 10.8 %collective-permute-start.10 = (bf16[8,9,8,256]{3,2,1,0:T(8,128)(2,1)S(1)}, bf16[8,9,8,256]{3,2,1,0:T(8,128)(2,1)S(1)}, u32[]{:S(2)}, u32[]{:S(2)}) collective-permute-start(bf16[8,9,8,256]{3,2,1,0:T(8,128)(2,1)S(1)} %get-tuple-element.25.refs_1_), channel_id=1, source_target_pairs={{0,2},{1,5},{2,0},{3,7},{4,6},{5,1},{6,4},{7,3},{8,10},{9,13},{10,... | collective-permute-start | bytes 884744 | tf_op jit(solution)/shard_map/ppermute | solution.py:22
  33.0 12.2 %collective-permute-start.7 = (bf16[8,9,8,256]{3,2,1,0:T(8,128)(2,1)S(1)}, bf16[8,9,8,256]{3,2,1,0:T(8,128)(2,1)S(1)}, u32[]{:S(2)}, u32[]{:S(2)}) collective-permute-start(bf16[8,9,8,256]{3,2,1,0:T(8,128)(2,1)S(1)} %collective-permute-done.5.refs_2_), channel_id=1, source_target_pairs={{0,1},{1,0},{2,3},{3,2},{4,5},{5,4},{6,7},{7,6},{8,9},{9,8},{10,11... | collective-permute-start | bytes 884744 | tf_op jit(solution)/shard_map/ppermute | solution.py:22
  33.4 14.8 %collective-permute-start.14 = (bf16[8,9,8,256]{3,2,1,0:T(8,128)(2,1)S(1)}, bf16[8,9,8,256]{3,2,1,0:T(8,128)(2,1)S(1)}, u32[]{:S(2)}, u32[]{:S(2)}) collective-permute-start(bf16[8,9,8,256]{3,2,1,0:T(8,128)(2,1)S(1)} %get-tuple-element.28.refs_1_), channel_id=1, source_target_pairs={{0,1},{1,0},{2,3},{3,2},{4,5},{5,4},{6,7},{7,6},{8,9},{9,8},{10,11... | collective-permute-start | bytes 884744 | tf_op jit(solution)/shard_map/ppermute | solution.py:22
  40.5 7.8 %collective-permute-start.15 = (bf16[8,9,8,256]{3,2,1,0:T(8,128)(2,1)S(1)}, bf16[8,9,8,256]{3,2,1,0:T(8,128)(2,1)S(1)}, u32[]{:S(2)}, u32[]{:S(2)}) collective-permute-start(bf16[8,9,8,256]{3,2,1,0:T(8,128)(2,1)S(1)} %collective-permute-done.13.refs_2_), channel_id=1, source_target_pairs={{0,1},{1,0},{2,3},{3,2},{4,5},{5,4},{6,7},{7,6},{8,9},{9,8},{10,11... | collective-permute-start | bytes 884744 | tf_op jit(solution)/shard_map/ppermute | solution.py:22
  40.5 8.6 %collective-permute-start.11 = (bf16[8,9,8,256]{3,2,1,0:T(8,128)(2,1)S(1)}, bf16[8,9,8,256]{3,2,1,0:T(8,128)(2,1)S(1)}, u32[]{:S(2)}, u32[]{:S(2)}) collective-permute-start(bf16[8,9,8,256]{3,2,1,0:T(8,128)(2,1)S(1)} %get-tuple-element.25.refs_1_), channel_id=1, source_target_pairs={{0,1},{1,0},{2,3},{3,2},{4,5},{5,4},{6,7},{7,6},{8,9},{9,8},{10,11... | collective-permute-start | bytes 884744 | tf_op jit(solution)/shard_map/ppermute | solution.py:22
  43.7 5.5 %collective-permute-start.12 = (bf16[8,9,8,256]{3,2,1,0:T(8,128)(2,1)S(1)}, bf16[8,9,8,256]{3,2,1,0:T(8,128)(2,1)S(1)}, u32[]{:S(2)}, u32[]{:S(2)}) collective-permute-start(bf16[8,9,8,256]{3,2,1,0:T(8,128)(2,1)S(1)} %collective-permute-done.10.refs_2_), channel_id=1, source_target_pairs={{0,1},{1,0},{2,3},{3,2},{4,5},{5,4},{6,7},{7,6},{8,9},{9,8},{10,11... | collective-permute-start | bytes 884744 | tf_op jit(solution)/shard_map/ppermute | solution.py:22
  48.3 9.5 %copy-start.3 = (f32[256]{0:T(256)S(1)}, f32[256]{0:T(256)}, u32[]{:S(2)}) copy-start(f32[256]{0:T(256)} %param.18) | copy-start | bytes 3076
  48.3 9.4 %copy-start.4 = (f32[256]{0:T(256)S(1)}, f32[256]{0:T(256)}, u32[]{:S(2)}) copy-start(f32[256]{0:T(256)} %param.19) | copy-start | bytes 3076
  48.3 9.4 %copy-start.5 = (f32[256]{0:T(256)S(1)}, f32[256]{0:T(256)}, u32[]{:S(2)}) copy-start(f32[256]{0:T(256)} %param.20) | copy-start | bytes 3076
  48.3 9.4 %copy-start.6 = (f32[256]{0:T(256)S(1)}, f32[256]{0:T(256)}, u32[]{:S(2)}) copy-start(f32[256]{0:T(256)} %param.21) | copy-start | bytes 3076
  48.3 9.4 %copy-start.7 = (f32[256]{0:T(256)S(1)}, f32[256]{0:T(256)}, u32[]{:S(2)}) copy-start(f32[256]{0:T(256)} %param.22) | copy-start | bytes 3076
  48.3 9.4 %copy-start.8 = (f32[256]{0:T(256)S(1)}, f32[256]{0:T(256)}, u32[]{:S(2)}) copy-start(f32[256]{0:T(256)} %param.23) | copy-start | bytes 3076
  50.3 1.4 %collective-permute-start.16 = (f32[1,24,256]{2,1,0:T(8,128)S(1)}, f32[1,24,256]{2,1,0:T(8,128)S(1)}, u32[]{:S(2)}, u32[]{:S(2)}) collective-permute-start(f32[1,24,256]{2,1,0:T(8,128)S(1)} %bitcast.18), channel_id=1, source_target_pairs={{0,1},{1,0},{2,3},{3,2},{4,5},{5,4},{6,7},{7,6},{8,9},{9,8},{10,11... | collective-permute-start | bytes 73736 | tf_op jit(solution)/shard_map/ppermute | solution.py:22
  51.7 5.2 %collective-permute-start.17 = (f32[2,24,256]{2,1,0:T(8,128)S(1)}, f32[2,24,256]{2,1,0:T(8,128)S(1)}, u32[]{:S(2)}, u32[]{:S(2)}) collective-permute-start(f32[2,24,256]{2,1,0:T(8,128)S(1)} %shard_map.150.refs_9_), channel_id=1, source_target_pairs={{0,6},{1,7},{2,4},{3,5},{4,2},{5,3},{6,0},{7,1},{8,14},{9,15},{10,... | collective-permute-start | bytes 147464 | tf_op jit(solution)/shard_map/ppermute | solution.py:22
  52.3 4.5 %collective-permute-start.18 = (f32[2,24,256]{2,1,0:T(8,128)S(1)}, f32[2,24,256]{2,1,0:T(8,128)S(1)}, u32[]{:S(2)}, u32[]{:S(2)}) collective-permute-start(f32[2,24,256]{2,1,0:T(8,128)S(1)} %shard_map.150.refs_9_), channel_id=1, source_target_pairs={{0,2},{1,3},{2,0},{3,1},{4,6},{5,7},{6,4},{7,5},{8,10},{9,11},{10,... | collective-permute-start | bytes 147464 | tf_op jit(solution)/shard_map/ppermute | solution.py:22
  53.6 4.1 %collective-permute-start.19 = (f32[2,24,256]{2,1,0:T(8,128)S(1)}, f32[2,24,256]{2,1,0:T(8,128)S(1)}, u32[]{:S(2)}, u32[]{:S(2)}) collective-permute-start(f32[2,24,256]{2,1,0:T(8,128)S(1)} %shard_map.150.refs_9_), channel_id=1, source_target_pairs={{0,4},{1,5},{2,6},{3,7},{4,0},{5,1},{6,2},{7,3},{8,12},{9,13},{10,... | collective-permute-start | bytes 147464 | tf_op jit(solution)/shard_map/ppermute | solution.py:22
